TPU v7x, 256 devices: a whole 4x4x8 slice. The times are simulated.
256 devices in a mesh: dom: 128 (over x, z, y), feat: 2 (over core).
Axes of the slice: x: 4, y: 4, z: 8, core: 2. Of those that a mesh axis runs over, the one named last changes fastest.
Arguments:
- features: bfloat16 [131072, 512], P('dom', 'feat'), may hold values from -6 to 6
- grad_out: bfloat16 [131072, 512], P('dom', 'feat'), may hold values from -6 to 6
- pre_act: bfloat16 [131072, 512], P('dom', 'feat'), may hold values from -6 to 6
- neigh_mean: bfloat16 [131072, 512], P('dom', 'feat'), may hold values from -6 to 6
- w_self: bfloat16 [512, 512], P('feat'), may hold values from -0.25 to 0.25
- w_neigh: bfloat16 [512, 512], P('feat'), may hold values from -0.25 to 0.25
- edge_from: int32 [1048576], P('dom'), may hold values from 0 to 5119
- edge_to: int32 [1048576], P('dom'), may hold values from 0 to 5119
- edge_count: int32 [128], P('dom'), may hold values from 2048 to 8192, as said below
- mirror_master: int32 [524288], P('dom'), may hold values from 0 to 63
- degrees: int32 [131072], P('dom'), may hold values from 1 to 16
Outputs:
- input_grad: bfloat16 [131072, 512], P('dom', 'feat')
- self_weight_grad: float32 [512, 512], P('feat')
- neigh_weight_grad: float32 [512, 512], P('feat')
Inputs may be any that keep to these rules, and one draw needn't show every extreme that they name: `edge_count`: equals 8192 in at least one partition.
All inputs are finite; a program needn't handle non-finite values.
Results may differ from a plain program's by a relative error of at most 0.0044.
Values may be sent and summed in bfloat16 or wider, within the bound.
No kernel may reach another device: no remote copies, remote signals or barrier semaphores. Data moves between devices by JAX's collectives and lax.ppermute only.
A program may use at most 64 MiB of HBM per device.

v0:
```python
import jax
import jax.numpy as jnp
from jax import lax
from jax.sharding import PartitionSpec as P


def sent_to_all(array, axis):
    copies = jnp.broadcast_to(array, (lax.axis_size(axis), *array.shape))
    return lax.all_to_all(copies, axis, split_axis=0, concat_axis=0, tiled=True)


def laid_out(tiles, dim):
    tiles = jnp.moveaxis(tiles, 0, dim)
    dims = tiles.shape
    return tiles.reshape(*dims[:dim], dims[dim] * dims[dim + 1], *dims[dim + 2 :])


def collect(array, axis, dim):
    tiles = sent_to_all(array, axis)
    return laid_out(tiles, dim)


def together(arrays, axis):
    vector, at, finished = (jnp.concatenate([a.reshape(-1) for a in arrays]), 0, [])
    running = lax.psum(vector, axis)
    for a in arrays:
        finished.append(running[at : at + a.size].reshape(a.shape))
        at += a.size
    return tuple(finished)


def on_device(
    features,
    grad_out,
    pre_act,
    neigh_mean,
    w_self,
    w_neigh,
    edge_from,
    edge_to,
    edge_count,
    mirror_master,
    degrees,
):
    masters = features.shape[0]
    width_loc = features.shape[1]
    parts = lax.axis_size("dom")
    mirror_count = mirror_master.shape[0]
    slots = mirror_count // parts
    grad_pre = (grad_out.astype(jnp.float32) * (pre_act > 0).astype(jnp.float32)).astype(
        jnp.bfloat16
    )
    wanted = mirror_master.reshape(parts, slots)
    asked = lax.all_to_all(wanted, "dom", split_axis=0, concat_axis=0, tiled=True)
    block_cols = collect(grad_pre, "feat", 1)
    contract = (((1,), (1,)), ((), ()))
    self_sum = lax.dot_general(block_cols, w_self, contract, preferred_element_type=jnp.float32)
    neigh_sum = lax.dot_general(block_cols, w_neigh, contract, preferred_element_type=jnp.float32)
    over_rows = (((0,), (0,)), ((), ()))
    grad_self = lax.dot_general(features, block_cols, over_rows, preferred_element_type=jnp.float32)
    grad_neigh = lax.dot_general(
        neigh_mean, block_cols, over_rows, preferred_element_type=jnp.float32
    )
    self_part, neigh_part, grad_self, grad_neigh = (self_sum, neigh_sum, grad_self, grad_neigh)
    scaled = (neigh_part / degrees[:, None].astype(jnp.float32)).astype(jnp.bfloat16)
    replies = scaled[asked.reshape(-1)].reshape(parts, slots, width_loc)
    mirror_rows = lax.all_to_all(replies, "dom", split_axis=0, concat_axis=0, tiled=True).reshape(
        mirror_count, width_loc
    )
    tables = jnp.concatenate([scaled, mirror_rows], axis=0)
    local_rows = tables.shape[0]
    edges = edge_from.shape[0]
    block_len = min(edges, 4096)
    blocks = edges // block_len
    positions = jnp.arange(edges, dtype=jnp.int32).reshape(blocks, block_len)
    limit = edge_count[0]

    def add_block(summed, pieces):
        sources, sinks, places = pieces
        is_live = places < limit
        contrib = jnp.where(is_live[:, None], tables[sinks].astype(jnp.float32), jnp.float32(0.0))
        return (summed.at[sources].add(contrib), None)

    summed, unused = lax.scan(
        add_block,
        jnp.zeros((local_rows, width_loc), jnp.float32),
        (edge_from.reshape(blocks, block_len), edge_to.reshape(blocks, block_len), positions),
    )
    mirror_grad = summed[masters:].astype(jnp.bfloat16)
    returned = lax.all_to_all(
        mirror_grad.reshape(parts, slots, width_loc), "dom", split_axis=0, concat_axis=0, tiled=True
    )
    master_add = jax.ops.segment_sum(
        returned.reshape(mirror_count, width_loc).astype(jnp.float32),
        asked.reshape(-1),
        num_segments=masters,
    )
    input_grad = (self_part + summed[:masters] + master_add).astype(jnp.bfloat16)
    self_weight_grad, neigh_weight_grad = together((grad_self, grad_neigh), "dom")
    return (input_grad, self_weight_grad, neigh_weight_grad)


def solution(mesh):
    placed = (
        P("dom", "feat"),
        P("dom", "feat"),
        P("dom", "feat"),
        P("dom", "feat"),
        P("feat", None),
        P("feat", None),
        P("dom"),
        P("dom"),
        P("dom"),
        P("dom"),
        P("dom"),
    )
    return jax.shard_map(
        on_device,
        mesh=mesh,
        in_specs=placed,
        out_specs=(P("dom", "feat"), P("feat", None), P("feat", None)),
        check_vma=False,
    )
```

profile of v0, /device:TPU:2, one launch (start us, length us, event | category | flops | bytes accessed | tf_op | source)
XLA Modules:
  0.0 340.1 jit_solution(16749855297623334223)
XLA Ops:
  7.2 0.0 copy-start
  7.2 0.0 copy-start.8
  7.2 0.0 copy-start.7
  7.2 0.0 copy-start.9
  7.2 1.4 select_convert_fusion
  8.6 0.2 copy.17
  8.8 1.1 broadcast_in_dim.24
  9.9 3.6 %all-to-all-start = ((bf16[2,1024,256]{1,2,0:T(8,128)(2,1)}), bf16[2,1024,256]{1,2,0:T(8,128)(2,1)S(1)}, u32[]{:S(2)}, u32[]{:S(2)}) async-start(bf16[2,1024,256]{1,2,0:T(8,128)(2,1)} %broadcast_in_dim.24), calls=%async_computation | async-start | bytes 2097152 | tf_op jit(solution)/shard_map/all_to_all | solution.py:9
  13.5 0.0 copy-done.8
  13.5 0.0 copy-done.7
  13.6 0.7 all_to_all.16
  14.3 1.4 all-to-all-done
  15.6 0.0 copy-start.2
  15.6 15.5 %all-to-all-start.1 = ((s32[128,1,32]{2,1,0:T(1,128)}), s32[128,1,32]{2,1,0:T(1,128)S(1)}, u32[]{:S(2)}, u32[]{:S(2)}) async-start(s32[128,1,32]{2,1,0:T(1,128)} %bitcast.8), calls=%async_computation.1 | async-start | bytes 131072 | tf_op jit(solution)/shard_map/all_to_all | solution.py:54
  31.2 0.0 copy-done.9
  31.2 0.5 fusion.8
  31.7 0.0 copy-done
  31.7 0.4 convolution_bitcast_fusion.1
  32.2 9.8 %all-to-all-done.1 = s32[128,1,32]{2,1,0:T(1,128)S(1)} async-done(((s32[128,1,32]{2,1,0:T(1,128)}), s32[128,1,32]{2,1,0:T(1,128)S(1)}, u32[]{:S(2)}, u32[]{:S(2)}) %all-to-all-start.1) | async-done | bytes 16416 | tf_op jit(solution)/shard_map/all_to_all | solution.py:54
  42.0 0.5 broadcast.84
  42.5 0.8 reduce.7
  43.3 0.1 reshape.166
  43.5 16.9 %gather_fusion = bf16[4096,256]{1,0:T(8,128)(2,1)} fusion(bf16[1024,256]{1,0:T(8,128)(2,1)S(1)} %fusion.8, s32[4096]{0:T(1024)S(1)} %broadcast_clamp_fusion.1), kind=kCustom, calls=%fused_computation.1 | custom fusion | bytes 4210688 | tf_op jit(solution)/shard_map/gather | solution.py:66
  60.4 8.1 %all-to-all-start.2 = ((bf16[128,32,256]{2,1,0:T(8,128)(2,1)}), bf16[128,32,256]{2,1,0:T(8,128)(2,1)}, u32[]{:S(2)}, u32[]{:S(2)}) async-start(bf16[128,32,256]{2,1,0:T(8,128)(2,1)} %bitcast.45), calls=%async_computation.2 | async-start | bytes 4194304 | tf_op jit(solution)/shard_map/all_to_all | solution.py:67
  68.5 0.2 all-reduce.2.cloned.1.call-start
  68.8 0.0 copy-done.2
  68.8 1.5 convolution_bitcast_fusion
  70.3 0.0 copy-start.5
  70.3 0.0 copy-start.6
  70.3 0.2 copy.19
  70.5 0.1 copy.21
  70.6 0.2 copy.20
  70.8 0.1 copy.22
  71.0 1.1 pad_maximum_fusion.1
  72.0 0.0 all-reduce.2.cloned.1.call-update
  72.1 0.0 copy-done.5
  72.1 0.0 copy-done.6
  72.2 52.1 %all-to-all-done.2 = bf16[128,32,256]{2,1,0:T(8,128)(2,1)} async-done(((bf16[128,32,256]{2,1,0:T(8,128)(2,1)}), bf16[128,32,256]{2,1,0:T(8,128)(2,1)}, u32[]{:S(2)}, u32[]{:S(2)}) %all-to-all-start.2) | async-done | bytes 2097184 | tf_op jit(solution)/shard_map/all_to_all | solution.py:67
  124.3 3.2 pad_maximum_fusion
  127.5 0.0 copy-start.1
  127.5 2.6 broadcast_in_dim.25
  130.2 0.2 copy-done.1
  130.4 86.3 %while.10 = (s32[]{:T(128)}, f32[5120,256]{1,0:T(8,128)}, s32[2,4096]{1,0:T(2,128)S(1)}, s32[2,4096]{1,0:T(2,128)S(1)}, s32[]{:T(128)}, /*index=5*/s32[2,4096]{1...) while((s32[]{:T(128)}, f32[5120,256]{1,0:T(8,128)}, s32[2,4096]{1,0:T(2,128)S(1)}, ...), condition=%wide.region_2.3_spmd, body=%wide.region_0.2_spmd.sunk | while | flops 3178498 | bytes 8004201 | solution.py:84
  130.4 0.7 compare_reduce_fusion.2
  131.1 42.4 %scatter_custom_fusion.7 = f32[5120,256]{1,0:T(8,128)} fusion(f32[5120,256]{1,0:T(8,128)} %get-tuple-element.116, s32[4096]{0:T(1024)S(1)} %bitcast.52, f32[]{:T(128)} %constant.16.clone.1..sunk, pred[4096]{0:T(1024)(128)(4,1)S(1)} %compare_reduce_fusion.2, bf16[5120,256]{1,0:T(8,128)(2,1)S(1)} %get-tuple-element.130, s32[4096]{0:T(1024)S(1)} %broadcast_clamp_fusion.3), kind=kCustom, calls=%fused_computation.4.clone.1 | custom fusion | flops 3145728 | bytes 7885312 | tf_op jit(solution)/shard_map/while/body/eval_jaxpr/scatter-add | solution.py:82
  173.6 0.7 compare_reduce_fusion.2
  174.3 42.4 %scatter_custom_fusion.7 = f32[5120,256]{1,0:T(8,128)} fusion(f32[5120,256]{1,0:T(8,128)} %get-tuple-element.116, s32[4096]{0:T(1024)S(1)} %bitcast.52, f32[]{:T(128)} %constant.16.clone.1..sunk, pred[4096]{0:T(1024)(128)(4,1)S(1)} %compare_reduce_fusion.2, bf16[5120,256]{1,0:T(8,128)(2,1)S(1)} %get-tuple-element.130, s32[4096]{0:T(1024)S(1)} %broadcast_clamp_fusion.3), kind=kCustom, calls=%fused_computation.4.clone.1 | custom fusion | flops 3145728 | bytes 7885312 | tf_op jit(solution)/shard_map/while/body/eval_jaxpr/scatter-add | solution.py:82
  216.7 3.8 %slice.52 = bf16[4096,256]{1,0:T(8,128)(2,1)} slice(f32[5120,256]{1,0:T(8,128)} %get-tuple-element.40), slice={[1024:5120], [0:256]} | slice | bytes 4194304 | tf_op jit(solution)/shard_map/slice | solution.py:89
  220.5 0.0 copy-start.3
  220.5 0.0 copy-start.4
  220.5 8.1 %all-to-all-start.3 = ((bf16[128,32,256]{2,1,0:T(8,128)(2,1)}), bf16[128,32,256]{2,1,0:T(8,128)(2,1)}, u32[]{:S(2)}, u32[]{:S(2)}) async-start(bf16[128,32,256]{2,1,0:T(8,128)(2,1)} %bitcast.44), calls=%async_computation.3 | async-start | bytes 4194304 | tf_op jit(solution)/shard_map/all_to_all | solution.py:90
  228.6 0.1 reshape.199
  228.7 75.5 %all-reduce.2.cloned.1.call-done = f32[262144]{0:T(1024)} async-done(((f32[262144]{0:T(1024)}), f32[262144]{0:T(1024)}) %all-reduce.2.cloned.1.call-update) | async-done | bytes 1048592 | tf_op jit(solution)/shard_map/psum | solution.py:25
  304.2 1.3 fusion.9
  305.4 0.9 slice.36
  306.3 0.9 slice.38
  307.2 0.0 copy-done.3
  307.2 0.0 copy-done.4
  307.2 1.7 convolution_add_fusion
  308.9 0.0 all-to-all-done.3
  308.9 23.4 %scatter_custom_fusion.1 = f32[1024,256]{1,0:T(8,128)S(1)} fusion(f32[1024,256]{1,0:T(8,128)S(1)} %convolution_add_fusion, s32[4096]{0:T(1024)S(1)} %reshape.199, bf16[4096,256]{1,0:T(8,128)(2,1)} %bitcast.16), kind=kCustom, calls=%fused_computation.15 | custom fusion | flops 2097152 | bytes 3145728 | tf_op jit(solution)/shard_map/scatter-add | solution.py:93
  332.4 0.8 convert_element_type.33
  (10 shorter events, 0.2 us)
Async XLA Ops:
  7.2 24.5 %copy-start = (bf16[1024,256]{1,0:T(8,128)(2,1)S(1)}, bf16[1024,256]{1,0:T(8,128)(2,1)}, u32[]{:S(2)}) copy-start(bf16[1024,256]{1,0:T(8,128)(2,1)} %param.13) | copy-start | bytes 1572868
  7.2 6.3 %copy-start.8 = (s32[1024]{0:T(1024)S(1)}, s32[1024]{0:T(1024)}, u32[]{:S(2)}) copy-start(s32[1024]{0:T(1024)} %param.23) | copy-start | bytes 12292
  7.2 6.4 %copy-start.7 = (s32[4096]{0:T(1024)S(1)}, s32[4096]{0:T(1024)}, u32[]{:S(2)}) copy-start(s32[4096]{0:T(1024)} %param.22) | copy-start | bytes 49156
  7.2 24.0 %copy-start.9 = (bf16[256,512]{1,0:T(8,128)(2,1)S(1)}, bf16[256,512]{1,0:T(8,128)(2,1)}, u32[]{:S(2)}) copy-start(bf16[256,512]{1,0:T(8,128)(2,1)} %param.18) | copy-start | bytes 786436
  9.9 5.7 %all-to-all-start = ((bf16[2,1024,256]{1,2,0:T(8,128)(2,1)}), bf16[2,1024,256]{1,2,0:T(8,128)(2,1)S(1)}, u32[]{:S(2)}, u32[]{:S(2)}) async-start(bf16[2,1024,256]{1,2,0:T(8,128)(2,1)} %broadcast_in_dim.24), calls=%async_computation | async-start | bytes 2097152 | tf_op jit(solution)/shard_map/all_to_all | solution.py:9
  15.6 53.1 %copy-start.2 = (bf16[2,1024,256]{1,2,0:T(8,128)(2,1)}, bf16[2,1024,256]{1,2,0:T(8,128)(2,1)S(1)}, u32[]{:S(2)}) copy-start(bf16[2,1024,256]{1,2,0:T(8,128)(2,1)S(1)} %all-to-all-done) | copy-start | bytes 3145732
  15.6 26.4 %all-to-all-start.1 = ((s32[128,1,32]{2,1,0:T(1,128)}), s32[128,1,32]{2,1,0:T(1,128)S(1)}, u32[]{:S(2)}, u32[]{:S(2)}) async-start(s32[128,1,32]{2,1,0:T(1,128)} %bitcast.8), calls=%async_computation.1 | async-start | bytes 131072 | tf_op jit(solution)/shard_map/all_to_all | solution.py:54
  60.4 63.9 %all-to-all-start.2 = ((bf16[128,32,256]{2,1,0:T(8,128)(2,1)}), bf16[128,32,256]{2,1,0:T(8,128)(2,1)}, u32[]{:S(2)}, u32[]{:S(2)}) async-start(bf16[128,32,256]{2,1,0:T(8,128)(2,1)} %bitcast.45), calls=%async_computation.2 | async-start | bytes 4194304 | tf_op jit(solution)/shard_map/all_to_all | solution.py:67
  68.5 235.6 %all-reduce.2.cloned.1.call-start = ((), (), s32[]{:S(2)}) async-start(), calls=%async_computation.4 | async-start | bytes 2097152 | tf_op jit(solution)/shard_map/psum | solution.py:25
  70.3 1.8 copy-start.5
  70.3 1.8 copy-start.6
  127.5 2.8 copy-start.1
  220.5 86.7 %copy-start.3 = (bf16[2,1024,256]{1,2,0:T(8,128)(2,1)S(1)}, bf16[2,1024,256]{1,2,0:T(8,128)(2,1)}, u32[]{:S(2)}) copy-start(bf16[2,1024,256]{1,2,0:T(8,128)(2,1)} %copy-done.2) | copy-start | bytes 3145732
  220.5 86.7 %copy-start.4 = (bf16[256,512]{1,0:T(8,128)(2,1)S(1)}, bf16[256,512]{1,0:T(8,128)(2,1)}, u32[]{:S(2)}) copy-start(bf16[256,512]{1,0:T(8,128)(2,1)} %param.17) | copy-start | bytes 786436
  220.5 88.4 %all-to-all-start.3 = ((bf16[128,32,256]{2,1,0:T(8,128)(2,1)}), bf16[128,32,256]{2,1,0:T(8,128)(2,1)}, u32[]{:S(2)}, u32[]{:S(2)}) async-start(bf16[128,32,256]{2,1,0:T(8,128)(2,1)} %bitcast.44), calls=%async_computation.3 | async-start | bytes 4194304 | tf_op jit(solution)/shard_map/all_to_all | solution.py:90
Sparse Core Ops, SparseCore 0:
  74.7 229.4 all-reduce.1
where the time goes:
time: 341 us; the launch traced here: 340 us
  waiting for transfers between devices  139 us (41%)
  other arithmetic  117 us (34%)
  starting transfers between devices  35.6 us (10%)
  local copies, waits for them, and re-layouts  30 us (9%)
  between operations  14.3 us (4%)
  matrix products  4.15 us (1%)
    scatter-add x2, other arithmetic, add_block(): return (summed.at[sources].add(contrib), None)  84.8 us
    psum x1, waiting for transfers between devices, together(): running = lax.psum(vector, axis)  75.5 us
    all_to_all x1, waiting for transfers between devices, on_device(): lax.all_to_all(replies, 'dom', split_axis=0, concat_axis=0, tiled=True)  52.1 us
    scatter-add x1, other arithmetic, on_device(): jax.ops.segment_sum(returned.reshape(mirror_count, width_loc).astype(jnp....  23.4 us
    gather x1, local copies, waits for them, and re-layouts, on_device(): replies = scaled[asked.reshape(-1)].reshape(parts, slots, width_loc)  16.9 us
    all_to_all x1, starting transfers between devices, on_device(): lax.all_to_all(wanted, 'dom', split_axis=0, concat_axis=0, tiled=True)  15.5 us
    all_to_all x1, waiting for transfers between devices, on_device(): lax.all_to_all(wanted, 'dom', split_axis=0, concat_axis=0, tiled=True)  9.84 us
    all_to_all x1, starting transfers between devices, on_device(): lax.all_to_all(mirror_grad.reshape(parts, slots, width_loc), 'dom', split...  8.13 us
  transfers between devices with their start and end apart: 5, of which 4 were waited for; matrix products, arithmetic and copies ran while one was open for 31% of the time, Pallas kernels for 0%

commit v1 on v0

v1 whole, which is shorter than its diff:
```python
import functools

import jax
import jax.numpy as jnp
from jax import lax
from jax.experimental import pallas as pl
from jax.experimental.pallas import tpu as pltpu
from jax.sharding import PartitionSpec as P

LANES = 128
SUB = 8
CHAINS = 4
UNROLL = 8
VMEM = pl.BlockSpec(memory_space=pltpu.VMEM)
SMEM = pl.BlockSpec(memory_space=pltpu.SMEM)


def picks(asked_ref, group, hub):
    wanted = asked_ref[pl.ds(group, 1), :]
    rows = lax.broadcasted_iota(jnp.int32, (hub, wanted.shape[1]), 0)
    return (rows == wanted).astype(jnp.float32).astype(jnp.bfloat16)


def pack_kernel(slots, asked_ref, hub_ref, pay_ref, out_ref):
    hub = hub_ref.shape[0]
    groups = asked_ref.shape[0]
    per = asked_ref.shape[1] // slots
    pay = out_ref.shape[1] - slots

    def one(group, carry):
        chosen = picks(asked_ref, group, hub)
        rows = lax.dot_general(
            chosen, hub_ref[...], (((0,), (0,)), ((), ())), preferred_element_type=jnp.float32
        ).astype(jnp.bfloat16)
        for k in range(per):
            peer = group * per + k
            out_ref[peer, 0:slots, :] = rows[k * slots : (k + 1) * slots]
            out_ref[peer, slots:, :] = pay_ref[pl.ds(pl.multiple_of(peer * pay, SUB), pay), :]
        return carry

    lax.fori_loop(0, groups, one, 0)


def edge_kernel(slots, from_ref, to_ref, own_ref, got_ref, master_ref, send_ref, table, *sums):
    masters, width = own_ref.shape
    parts = got_ref.shape[0]
    pay = got_ref.shape[1] - slots
    halves = width // LANES
    tall = SUB * halves
    edges = from_ref.shape[0]

    def put(base, block):
        for g in range(block.shape[0] // SUB):
            for h in range(halves):
                at = pl.multiple_of(base + g * tall + h * SUB, SUB)
                table[pl.ds(at, SUB), :] = block[g * SUB : (g + 1) * SUB, h * LANES : (h + 1) * LANES]

    def own(i, carry):
        block = own_ref[pl.ds(pl.multiple_of(i * 32, 32), 32), :].astype(jnp.float32)
        put(i * 32 * halves, block)
        return carry

    lax.fori_loop(0, masters // 32, own, 0)

    def got(p, total):
        put((masters + p * slots) * halves, got_ref[p, 0:slots, :].astype(jnp.float32))
        return total + got_ref[p, slots:, :].astype(jnp.float32)

    total = lax.fori_loop(0, parts, got, jnp.zeros((pay, width), jnp.float32))
    share = total.astype(jnp.bfloat16)

    clear = 16 * SUB

    def zero(i, carry):
        for s in sums:
            s[pl.ds(pl.multiple_of(i * clear, clear), clear), :] = jnp.zeros((clear, LANES), jnp.float32)
        return carry

    lax.fori_loop(0, table.shape[0] // clear, zero, 0)

    step = CHAINS * UNROLL

    def add(i, carry):
        for j in range(step):
            src = from_ref[i * step + j]
            dst = to_ref[i * step + j]
            into = sums[j % CHAINS]
            at = pl.ds(src, halves, stride=SUB)
            into[at, :] = into[at, :] + table[pl.ds(dst, halves, stride=SUB), :]
        return carry

    lax.fori_loop(0, edges // step, add, 0)

    def merged(base, rows, h):
        tiles = []
        for g in range(rows // SUB):
            at = pl.ds(pl.multiple_of(base + g * tall + h * SUB, SUB), SUB)
            value = sums[0][at, :]
            for s in sums[1:]:
                value = value + s[at, :]
            tiles.append(value)
        return jnp.concatenate(tiles, axis=0)

    def finish(i, carry):
        for h in range(halves):
            cols = slice(h * LANES, (h + 1) * LANES)
            master_ref[pl.ds(pl.multiple_of(i * 32, 32), 32), cols] = merged(i * 32 * halves, 32, h)
        return carry

    lax.fori_loop(0, masters // 32, finish, 0)

    def reply(p, carry):
        for h in range(halves):
            cols = slice(h * LANES, (h + 1) * LANES)
            block = merged((masters + p * slots) * halves, slots, h)
            send_ref[p, 0:slots, cols] = block.astype(jnp.bfloat16)
        send_ref[p, slots:, :] = share
        return carry

    lax.fori_loop(0, parts, reply, 0)


def final_kernel(slots, hub, asked_ref, got_ref, pre_ref, grad_ref, self_ref, neigh_ref):
    groups = asked_ref.shape[0]
    per = asked_ref.shape[1] // slots
    parts = got_ref.shape[0]
    pay = got_ref.shape[1] - slots
    width = pre_ref.shape[1]

    def one(group, total):
        chosen = picks(asked_ref, group, hub)
        rows = jnp.concatenate([got_ref[group * per + k, 0:slots, :] for k in range(per)], axis=0)
        return total + jnp.dot(chosen, rows, preferred_element_type=jnp.float32)

    total = lax.fori_loop(0, groups, one, jnp.zeros((hub, width), jnp.float32))
    grad_ref[0:hub, :] = (pre_ref[0:hub, :] + total).astype(jnp.bfloat16)
    grad_ref[hub:, :] = pre_ref[hub:, :].astype(jnp.bfloat16)

    quarter = parts // 4
    for which, ref in ((0, self_ref), (1, neigh_ref)):
        for half in range(2):

            def place(i, carry, which=which, ref=ref, half=half):
                peer = (which * 2 + half) * quarter + i
                rows = pl.ds(pl.multiple_of(i * pay, SUB), pay)
                ref[rows, half * width : (half + 1) * width] = got_ref[peer, slots:, :].astype(jnp.float32)
                return carry

            lax.fori_loop(0, quarter, place, 0)


def on_device(
    features,
    grad_out,
    pre_act,
    neigh_mean,
    w_self,
    w_neigh,
    edge_from,
    edge_to,
    edge_count,
    mirror_master,
    degrees,
):
    masters, width = features.shape
    parts = lax.axis_size("dom")
    mirrors = mirror_master.shape[0]
    slots = mirrors // parts
    hub = min(masters, 64)
    local = masters + mirrors
    halves = width // LANES
    edges = edge_from.shape[0]

    wanted = mirror_master.reshape(parts, slots)
    asked = lax.all_to_all(wanted, "dom", split_axis=0, concat_axis=0, tiled=True)
    asked = asked.reshape(mirrors // LANES, LANES)

    def spot(row):
        return (row // SUB) * (SUB * halves) + row % SUB

    live = jnp.arange(edges, dtype=jnp.int32) < edge_count[0]
    from_at = spot(jnp.where(live, edge_from, local))
    to_at = spot(edge_to)

    grad_pre = (grad_out.astype(jnp.float32) * (pre_act > 0).astype(jnp.float32)).astype(jnp.bfloat16)
    other = lax.ppermute(grad_pre, "feat", [(0, 1), (1, 0)])
    first = lax.axis_index("feat") == 0
    block_cols = jnp.concatenate(
        [jnp.where(first, grad_pre, other), jnp.where(first, other, grad_pre)], axis=1
    )
    contract = (((1,), (1,)), ((), ()))
    over_rows = (((0,), (0,)), ((), ()))
    neigh_part = lax.dot_general(block_cols, w_neigh, contract, preferred_element_type=jnp.float32)
    scaled = (neigh_part / degrees[:, None].astype(jnp.float32)).astype(jnp.bfloat16)
    grad_self = lax.dot_general(features, block_cols, over_rows, preferred_element_type=jnp.float32)
    grad_neigh = lax.dot_general(neigh_mean, block_cols, over_rows, preferred_element_type=jnp.float32)
    pay = jnp.concatenate(
        [grad_self[:, :width], grad_self[:, width:], grad_neigh[:, :width], grad_neigh[:, width:]], axis=0
    ).astype(jnp.bfloat16)
    tail = pay.shape[0] // parts

    message = jax.ShapeDtypeStruct((parts, slots + tail, width), jnp.bfloat16)
    sent = pl.pallas_call(
        functools.partial(pack_kernel, slots),
        out_shape=message,
        in_specs=[VMEM] * 3,
        out_specs=VMEM,
        name="pack",
    )(asked, scaled[:hub], pay)
    got = lax.all_to_all(sent, "dom", split_axis=0, concat_axis=0, tiled=True)

    lanes = local * halves
    spare = SUB * halves
    master_sum, back = pl.pallas_call(
        functools.partial(edge_kernel, slots),
        out_shape=(jax.ShapeDtypeStruct((masters, width), jnp.float32), message),
        in_specs=[SMEM, SMEM, VMEM, VMEM],
        out_specs=[VMEM, VMEM],
        scratch_shapes=[pltpu.VMEM((lanes, LANES), jnp.float32)]
        + [pltpu.VMEM((lanes + spare, LANES), jnp.float32) for _ in range(CHAINS)],
        name="edges",
    )(from_at, to_at, scaled, got)
    home = lax.all_to_all(back, "dom", split_axis=0, concat_axis=0, tiled=True)

    self_part = lax.dot_general(block_cols, w_self, contract, preferred_element_type=jnp.float32)
    pre = self_part + master_sum
    return pl.pallas_call(
        functools.partial(final_kernel, slots, hub),
        out_shape=(
            jax.ShapeDtypeStruct((masters, width), jnp.bfloat16),
            jax.ShapeDtypeStruct(w_self.shape, jnp.float32),
            jax.ShapeDtypeStruct(w_neigh.shape, jnp.float32),
        ),
        in_specs=[VMEM] * 3,
        out_specs=[VMEM] * 3,
        name="final",
    )(asked, home, pre)


def solution(mesh):
    placed = (
        P("dom", "feat"),
        P("dom", "feat"),
        P("dom", "feat"),
        P("dom", "feat"),
        P("feat", None),
        P("feat", None),
        P("dom"),
        P("dom"),
        P("dom"),
        P("dom"),
        P("dom"),
    )
    return jax.shard_map(
        on_device,
        mesh=mesh,
        in_specs=placed,
        out_specs=(P("dom", "feat"), P("feat", None), P("feat", None)),
        check_vma=False,
    )
```

time: 341 us -> 220 us (0.65)
  other arithmetic: 117 us -> 4.49 us
  Pallas kernels: 0 us -> 39.3 us
  local copies, waits for them, and re-layouts: 30 us -> 8.11 us
  between operations: 14.3 us -> 1.44 us
  waiting for transfers between devices: 139 us -> 130 us
  starting transfers between devices: 35.6 us -> 31 us
    scatter-add x3 -> x0, other arithmetic: 108 us -> none  [the longest x2 84.8 us: add_block(): return (summed.at[sources].add(contrib), None)]
    psum x1 -> x0, waiting for transfers between devices: 75.5 us -> none  [together(): running = lax.psum(vector, axis)]
    all_to_all x3 -> x2, waiting for transfers between devices: 53.5 us -> 120 us  [the longest x1 61.4 us: on_device(): got = lax.all_to_all(sent, 'dom', split_axis=0, concat_axis=0, tiled=True)]
    pallas_call x0 -> x3, Pallas kernels: none -> 39.3 us  [the longest x1 21.6 us: on_device(): pl.pallas_call(functools.partial(edge_kernel, slots), out_shape=(jax.Shap...]
    gather x1 -> x0, local copies, waits for them, and re-layouts: 16.9 us -> none  [on_device(): replies = scaled[asked.reshape(-1)].reshape(parts, slots, width_loc)]
    slice x4 -> x2, local copies, waits for them, and re-layouts: 6.79 us -> 0.64 us  [the longest x1 0.6 us: on_device(): scaled[:hub]]
    all_to_all x3 -> x2, starting transfers between devices: 19.8 us -> 15.4 us  [the longest x1 8.27 us: on_device(): home = lax.all_to_all(back, 'dom', split_axis=0, concat_axis=0, tiled=True)]
    unnamed x22, local copies, waits for them, and re-layouts: 0.51 us -> 4.86 us
  transfers between devices with their start and end apart: 5 -> 4, of which waited for: 4 -> 3; matrix products, arithmetic and copies ran while one was open for 31% -> 3% of each run, Pallas kernels for 0% -> 0%
where the time goes in v1:
time: 220 us; the launch traced here: 219 us
  waiting for transfers between devices  130 us (59%)
  Pallas kernels  39.3 us (18%)
  starting transfers between devices  31 us (14%)
  local copies, waits for them, and re-layouts  8.11 us (4%)
  other arithmetic  4.49 us (2%)
  matrix products  4.41 us (2%)
    all_to_all x1, waiting for transfers between devices, on_device(): got = lax.all_to_all(sent, 'dom', split_axis=0, concat_axis=0, tiled=True)  61.4 us
    all_to_all x1, waiting for transfers between devices, on_device(): home = lax.all_to_all(back, 'dom', split_axis=0, concat_axis=0, tiled=True)  58.7 us
    pallas_call x1, Pallas kernels, on_device(): pl.pallas_call(functools.partial(edge_kernel, slots), out_shape=(jax.Shap...  21.6 us
    all_to_all x1, starting transfers between devices, on_device(): lax.all_to_all(wanted, 'dom', split_axis=0, concat_axis=0, tiled=True)  15.5 us
    all_to_all x1, waiting for transfers between devices, on_device(): lax.all_to_all(wanted, 'dom', split_axis=0, concat_axis=0, tiled=True)  10.2 us
    pallas_call x1, Pallas kernels, on_device(): pl.pallas_call(functools.partial(pack_kernel, slots), out_shape=message,...  9.11 us
    pallas_call x1, Pallas kernels, on_device(): pl.pallas_call(functools.partial(final_kernel, slots, hub), out_shape=(ja...  8.56 us
    all_to_all x1, starting transfers between devices, on_device(): home = lax.all_to_all(back, 'dom', split_axis=0, concat_axis=0, tiled=True)  8.27 us
  transfers between devices with their start and end apart: 4, of which 3 were waited for; matrix products, arithmetic and copies ran while one was open for 3% of the time, Pallas kernels for 0%

profile of v1, /device:TPU:2, one launch (start us, length us, event | category | flops | bytes accessed | tf_op | source)
XLA Modules:
  0.0 219.1 jit_solution(5516668208598262063)
XLA Ops:
  0.6 0.0 copy-start
  0.6 1.4 select_convert_fusion
  2.1 0.1 collective-permute-start
  2.2 1.4 all_to_all.12
  3.6 15.5 %all-to-all-start = ((s32[128,1,32]{2,1,0:T(1,128)}), s32[128,1,32]{2,1,0:T(1,128)S(1)}, u32[]{:S(2)}, u32[]{:S(2)}) async-start(s32[128,1,32]{2,1,0:T(1,128)} %bitcast), calls=%async_computation | async-start | bytes 131072 | tf_op jit(solution)/shard_map/all_to_all | solution.py:175
  19.1 0.7 convert_element_type.17
  19.8 10.2 %all-to-all-done = s32[128,1,32]{2,1,0:T(1,128)S(1)} async-done(((s32[128,1,32]{2,1,0:T(1,128)}), s32[128,1,32]{2,1,0:T(1,128)S(1)}, u32[]{:S(2)}, u32[]{:S(2)}) %all-to-all-start) | async-done | bytes 16416 | tf_op jit(solution)/shard_map/all_to_all | solution.py:175
  30.1 0.5 broadcast.37
  30.6 0.8 reduce.3
  31.4 0.7 reshape.16.asked_ref
  32.1 0.0 copy-start.9
  32.1 0.0 collective-permute-done
  32.1 0.1 broadcast_select_fusion.1
  32.1 0.0 copy-start.3
  32.2 0.0 copy-start.4
  32.2 0.0 copy-done
  32.2 0.5 fusion.1
  32.7 0.6 copy-done.9
  33.2 0.0 copy-start.10
  33.2 0.5 fusion.2
  33.7 0.0 copy-done.3
  33.7 0.0 copy-done.4
  33.8 0.4 copy-done.10
  34.2 0.5 fusion.own_ref
  34.7 0.0 copy-start.5
  34.7 0.8 copy-done.5
  35.5 0.6 slice.24.hub_ref
  36.1 0.8 pad_maximum_fusion.1.pay_ref
  36.9 9.1 %pack.1 = bf16[128,40,256]{2,1,0:T(8,128)(2,1)} custom-call(s32[32,128]{1,0:T(8,128)} %reshape.16.asked_ref, bf16[64,256]{1,0:T(8,128)(2,1)} %slice.24.hub_ref, bf16[1024,256]{1,0:T(8,128)(2,1)} %pad_maximum_fusion.1.pay_ref), custom_call_target="tpu_custom_call" | custom-call | tf_op jit(solution)/shard_map/pack/pallas_call | solution.py:203
  46.0 0.0 copy-start.7
  46.0 0.0 copy-start.8
  46.0 7.1 %all-to-all-start.1 = ((bf16[128,40,256]{2,1,0:T(8,128)(2,1)}), bf16[128,40,256]{2,1,0:T(8,128)(2,1)S(1)}, u32[]{:S(2)}, u32[]{:S(2)}) async-start(bf16[128,40,256]{2,1,0:T(8,128)(2,1)} %pack.1), calls=%async_computation.1 | async-start | bytes 5242880 | tf_op jit(solution)/shard_map/all_to_all | solution.py:210
  53.8 0.0 copy-done.7
  53.8 0.0 copy-done.8
  53.8 0.7 fusion.4
  54.5 61.4 %all-to-all-done.1.got_ref = bf16[128,40,256]{2,1,0:T(8,128)(2,1)S(1)} async-done(((bf16[128,40,256]{2,1,0:T(8,128)(2,1)}), bf16[128,40,256]{2,1,0:T(8,128)(2,1)S(1)}, u32[]{:S(2)}, u32[]{:S(2)}) %all-to-all-start.1) | async-done | bytes 2621472 | tf_op jit(solution)/shard_map/all_to_all | solution.py:210
  115.9 0.0 copy-start.1
  116.0 1.5 copy-done.1
  117.5 21.6 %edges.1 = (f32[1024,256]{1,0:T(8,128)}, bf16[128,40,256]{2,1,0:T(8,128)(2,1)}) custom-call(s32[8192]{0:T(1024)} %get-tuple-element.15.from_ref, s32[8192]{0:T(1024)} %get-tuple-element.16.to_ref, bf16[1024,256]{1,0:T(8,128)(2,1)} %copy-done.5, bf16[128,40,256]{2,1,0:T(8,128)(2,1)} %copy-done.1), custom_call_target="tpu_custom_call" | custom-call | tf_op jit(solution)/shard_map/edges/pallas_call | solution.py:214
  139.1 0.0 copy-start.6
  139.1 8.3 %all-to-all-start.2 = ((bf16[128,40,256]{2,1,0:T(8,128)(2,1)}), bf16[128,40,256]{2,1,0:T(8,128)(2,1)S(1)}, u32[]{:S(2)}, u32[]{:S(2)}) async-start(bf16[128,40,256]{2,1,0:T(8,128)(2,1)} %get-tuple-element.5), calls=%async_computation.2 | async-start | bytes 5242880 | tf_op jit(solution)/shard_map/all_to_all | solution.py:223
  147.4 0.0 copy-done.6
  147.4 3.0 %convolution_add_fusion.pre_ref = f32[1024,256]{1,0:T(8,128)} fusion(f32[1024,256]{1,0:T(8,128)} %get-tuple-element.6, bf16[256,512]{1,0:T(8,128)(2,1)S(1)} %copy-done.6, bf16[1024,256]{1,0:T(8,128)(2,1)} %copy-done.4, bf16[1024,256]{1,0:T(8,128)(2,1)} %copy-done.3), kind=kOutput, calls=%fused_computation | convolution fusion | flops 270794752 | bytes 3407872 | tf_op jit(solution)/shard_map/dot_general | solution.py:225
  150.4 58.7 %all-to-all-done.2.got_ref = bf16[128,40,256]{2,1,0:T(8,128)(2,1)S(1)} async-done(((bf16[128,40,256]{2,1,0:T(8,128)(2,1)}), bf16[128,40,256]{2,1,0:T(8,128)(2,1)S(1)}, u32[]{:S(2)}, u32[]{:S(2)}) %all-to-all-start.2) | async-done | bytes 2621472 | tf_op jit(solution)/shard_map/all_to_all | solution.py:223
  209.0 0.0 copy-start.2
  209.0 1.5 copy-done.2
  210.5 8.6 %final.1 = (bf16[1024,256]{1,0:T(8,128)(2,1)}, f32[256,512]{1,0:T(8,128)}, f32[256,512]{1,0:T(8,128)}) custom-call(s32[32,128]{1,0:T(8,128)} %reshape.16.asked_ref, bf16[128,40,256]{2,1,0:T(8,128)(2,1)} %copy-done.2, f32[1024,256]{1,0:T(8,128)} %convolution_add_fusion.pre_ref), custom_call_target="tpu_custom_call" | custom-call | tf_op jit(solution)/shard_map/final/pallas_call | solution.py:227
  (1 shorter events, 0.0 us)
Async XLA Ops:
  0.6 31.5 %copy-start = (bf16[1024,256]{1,0:T(8,128)(2,1)S(1)}, bf16[1024,256]{1,0:T(8,128)(2,1)}, u32[]{:S(2)}) copy-start(bf16[1024,256]{1,0:T(8,128)(2,1)} %param.11) | copy-start | bytes 1572868
  2.1 30.0 %collective-permute-start = (bf16[1024,256]{1,0:T(8,128)(2,1)S(1)}, bf16[1024,256]{1,0:T(8,128)(2,1)S(1)}, u32[]{:S(2)}, u32[]{:S(2)}) collective-permute-start(bf16[1024,256]{1,0:T(8,128)(2,1)S(1)} %select_convert_fusion), channel_id=1, source_target_pairs={{0,1},{1,0},{2,3},{3,2},{4,5},{5,4},{6,7},{7,6},{8,9},{9,8},{10,11... | collective-permute-start | bytes 1572872 | tf_op jit(solution)/shard_map/ppermute | solution.py:186
  3.6 26.5 %all-to-all-start = ((s32[128,1,32]{2,1,0:T(1,128)}), s32[128,1,32]{2,1,0:T(1,128)S(1)}, u32[]{:S(2)}, u32[]{:S(2)}) async-start(s32[128,1,32]{2,1,0:T(1,128)} %bitcast), calls=%async_computation | async-start | bytes 131072 | tf_op jit(solution)/shard_map/all_to_all | solution.py:175
  32.1 1.2 copy-start.9
  32.1 1.6 copy-start.3
  32.2 1.6 copy-start.4
  33.2 0.9 copy-start.10
  34.7 0.8 copy-start.5
  46.0 7.8 %copy-start.7 = (s32[8192]{0:T(1024)S(1)}, s32[8192]{0:T(1024)}, u32[]{:S(2)}) copy-start(s32[8192]{0:T(1024)} %param.17) | copy-start | bytes 98308
  46.0 7.8 %copy-start.8 = (s32[8192]{0:T(1024)S(1)}, s32[8192]{0:T(1024)}, u32[]{:S(2)}) copy-start(s32[8192]{0:T(1024)} %param.18) | copy-start | bytes 98308
  46.0 69.9 %all-to-all-start.1 = ((bf16[128,40,256]{2,1,0:T(8,128)(2,1)}), bf16[128,40,256]{2,1,0:T(8,128)(2,1)S(1)}, u32[]{:S(2)}, u32[]{:S(2)}) async-start(bf16[128,40,256]{2,1,0:T(8,128)(2,1)} %pack.1), calls=%async_computation.1 | async-start | bytes 5242880 | tf_op jit(solution)/shard_map/all_to_all | solution.py:210
  115.9 1.5 copy-start.1
  139.1 8.3 %copy-start.6 = (bf16[256,512]{1,0:T(8,128)(2,1)S(1)}, bf16[256,512]{1,0:T(8,128)(2,1)}, u32[]{:S(2)}) copy-start(bf16[256,512]{1,0:T(8,128)(2,1)} %param.15) | copy-start | bytes 786436
  139.1 69.9 %all-to-all-start.2 = ((bf16[128,40,256]{2,1,0:T(8,128)(2,1)}), bf16[128,40,256]{2,1,0:T(8,128)(2,1)S(1)}, u32[]{:S(2)}, u32[]{:S(2)}) async-start(bf16[128,40,256]{2,1,0:T(8,128)(2,1)} %get-tuple-element.5), calls=%async_computation.2 | async-start | bytes 5242880 | tf_op jit(solution)/shard_map/all_to_all | solution.py:223
  209.0 1.5 copy-start.2

commit v2 on v1

--- a/solution.py
+++ b/solution.py
@@ -15,33 +15,50 @@
 SMEM = pl.BlockSpec(memory_space=pltpu.SMEM)
 
 
-def picks(asked_ref, group, hub):
-    wanted = asked_ref[pl.ds(group, 1), :]
+def near(array):
+    return pltpu.with_memory_space_constraint(array, pltpu.VMEM)
+
+
+def picks(wanted, hub):
     rows = lax.broadcasted_iota(jnp.int32, (hub, wanted.shape[1]), 0)
     return (rows == wanted).astype(jnp.float32).astype(jnp.bfloat16)
 
 
-def pack_kernel(slots, asked_ref, hub_ref, pay_ref, out_ref):
-    hub = hub_ref.shape[0]
-    groups = asked_ref.shape[0]
-    per = asked_ref.shape[1] // slots
+def grouped(asked_ref, slots):
+    per = LANES // slots
+    rows = asked_ref.shape[0] // per
+    lane = lax.broadcasted_iota(jnp.int32, (rows, LANES), 1)
+    dense = asked_ref[pl.ds(0, rows, stride=per), :]
+    for k in range(1, per):
+        part = pltpu.roll(asked_ref[pl.ds(k, rows, stride=per), :], k * slots, 1)
+        dense = jnp.where(lane < k * slots, dense, part)
+    return dense
+
+
+def pack_kernel(slots, asked_ref, hub_ref, pay_ref, out_ref, dense_ref):
+    hub, width = hub_ref.shape
+    parts = out_ref.shape[0]
     pay = out_ref.shape[1] - slots
-
-    def one(group, carry):
-        chosen = picks(asked_ref, group, hub)
-        rows = lax.dot_general(
-            chosen, hub_ref[...], (((0,), (0,)), ((), ())), preferred_element_type=jnp.float32
-        ).astype(jnp.bfloat16)
-        for k in range(per):
-            peer = group * per + k
-            out_ref[peer, 0:slots, :] = rows[k * slots : (k + 1) * slots]
-            out_ref[peer, slots:, :] = pay_ref[pl.ds(pl.multiple_of(peer * pay, SUB), pay), :]
-        return carry
-
-    lax.fori_loop(0, groups, one, 0)
-
-
-def edge_kernel(slots, from_ref, to_ref, own_ref, got_ref, master_ref, send_ref, table, *sums):
+    dense_ref[...] = grouped(asked_ref, slots)
+    rows = min(4, dense_ref.shape[0])
+    peers = rows * LANES // slots
+
+    def one(i, carry):
+        for r in range(rows):
+            chosen = picks(dense_ref[pl.ds(i * rows + r, 1), :], hub)
+            found = lax.dot_general(
+                chosen, hub_ref[...], (((0,), (0,)), ((), ())), preferred_element_type=jnp.float32
+            ).astype(jnp.bfloat16)
+            for k in range(LANES // slots):
+                peer = i * peers + r * (LANES // slots) + k
+                out_ref[peer, 0:slots, :] = found[k * slots : (k + 1) * slots]
+                out_ref[peer, slots:, :] = pay_ref[pl.ds(pl.multiple_of(peer * pay, SUB), pay), :]
+        return carry
+
+    lax.fori_loop(0, parts // peers, one, 0)
+
+
+def edge_kernel(slots, from_ref, to_ref, own_ref, got_ref, self_ref, pre_ref, send_ref, table, *sums):
     masters, width = own_ref.shape
     parts = got_ref.shape[0]
     pay = got_ref.shape[1] - slots
@@ -103,8 +120,9 @@
 
     def finish(i, carry):
         for h in range(halves):
+            rows = pl.ds(pl.multiple_of(i * 32, 32), 32)
             cols = slice(h * LANES, (h + 1) * LANES)
-            master_ref[pl.ds(pl.multiple_of(i * 32, 32), 32), cols] = merged(i * 32 * halves, 32, h)
+            pre_ref[rows, cols] = self_ref[rows, cols] + merged(i * 32 * halves, 32, h)
         return carry
 
     lax.fori_loop(0, masters // 32, finish, 0)
@@ -120,19 +138,23 @@
     lax.fori_loop(0, parts, reply, 0)
 
 
-def final_kernel(slots, hub, asked_ref, got_ref, pre_ref, grad_ref, self_ref, neigh_ref):
-    groups = asked_ref.shape[0]
-    per = asked_ref.shape[1] // slots
+def final_kernel(slots, hub, dense_ref, got_ref, pre_ref, grad_ref, self_ref, neigh_ref):
     parts = got_ref.shape[0]
     pay = got_ref.shape[1] - slots
     width = pre_ref.shape[1]
-
-    def one(group, total):
-        chosen = picks(asked_ref, group, hub)
-        rows = jnp.concatenate([got_ref[group * per + k, 0:slots, :] for k in range(per)], axis=0)
-        return total + jnp.dot(chosen, rows, preferred_element_type=jnp.float32)
-
-    total = lax.fori_loop(0, groups, one, jnp.zeros((hub, width), jnp.float32))
+    rows = min(4, dense_ref.shape[0])
+    peers = rows * LANES // slots
+
+    def one(i, total):
+        chosen = [picks(dense_ref[pl.ds(i * rows + r, 1), :], hub) for r in range(rows)]
+        found = [got_ref[i * peers + k, 0:slots, :] for k in range(peers)]
+        return total + jnp.dot(
+            jnp.concatenate(chosen, axis=1),
+            jnp.concatenate(found, axis=0),
+            preferred_element_type=jnp.float32,
+        )
+
+    total = lax.fori_loop(0, parts // peers, one, jnp.zeros((hub, width), jnp.float32))
     grad_ref[0:hub, :] = (pre_ref[0:hub, :] + total).astype(jnp.bfloat16)
     grad_ref[hub:, :] = pre_ref[hub:, :].astype(jnp.bfloat16)
 
@@ -171,9 +193,8 @@
     halves = width // LANES
     edges = edge_from.shape[0]
 
-    wanted = mirror_master.reshape(parts, slots)
+    wanted = jnp.pad(mirror_master.reshape(parts, slots), ((0, 0), (0, LANES - slots)))
     asked = lax.all_to_all(wanted, "dom", split_axis=0, concat_axis=0, tiled=True)
-    asked = asked.reshape(mirrors // LANES, LANES)
 
     def spot(row):
         return (row // SUB) * (SUB * halves) + row % SUB
@@ -192,6 +213,7 @@
     over_rows = (((0,), (0,)), ((), ()))
     neigh_part = lax.dot_general(block_cols, w_neigh, contract, preferred_element_type=jnp.float32)
     scaled = (neigh_part / degrees[:, None].astype(jnp.float32)).astype(jnp.bfloat16)
+    self_part = lax.dot_general(block_cols, w_self, contract, preferred_element_type=jnp.float32)
     grad_self = lax.dot_general(features, block_cols, over_rows, preferred_element_type=jnp.float32)
     grad_neigh = lax.dot_general(neigh_mean, block_cols, over_rows, preferred_element_type=jnp.float32)
     pay = jnp.concatenate(
@@ -199,31 +221,34 @@
     ).astype(jnp.bfloat16)
     tail = pay.shape[0] // parts
 
-    message = jax.ShapeDtypeStruct((parts, slots + tail, width), jnp.bfloat16)
-    sent = pl.pallas_call(
+    message = pltpu.VMEM((parts, slots + tail, width), jnp.bfloat16)
+    sent, dense = pl.pallas_call(
         functools.partial(pack_kernel, slots),
-        out_shape=message,
+        out_shape=(message, jax.ShapeDtypeStruct((mirrors // LANES, LANES), jnp.int32)),
         in_specs=[VMEM] * 3,
-        out_specs=VMEM,
+        out_specs=[VMEM] * 2,
+        compiler_params=pltpu.CompilerParams(vmem_limit_bytes=8 << 20),
         name="pack",
-    )(asked, scaled[:hub], pay)
+    )(asked, near(scaled[:hub]), near(pay))
+    sent, from_at, to_at, self_part, scaled, dense = lax.optimization_barrier(
+        (sent, from_at, to_at, self_part, scaled, dense)
+    )
     got = lax.all_to_all(sent, "dom", split_axis=0, concat_axis=0, tiled=True)
 
     lanes = local * halves
     spare = SUB * halves
-    master_sum, back = pl.pallas_call(
+    pre, back = pl.pallas_call(
         functools.partial(edge_kernel, slots),
-        out_shape=(jax.ShapeDtypeStruct((masters, width), jnp.float32), message),
-        in_specs=[SMEM, SMEM, VMEM, VMEM],
+        out_shape=(pltpu.VMEM((masters, width), jnp.float32), message),
+        in_specs=[SMEM, SMEM, VMEM, VMEM, VMEM],
         out_specs=[VMEM, VMEM],
         scratch_shapes=[pltpu.VMEM((lanes, LANES), jnp.float32)]
         + [pltpu.VMEM((lanes + spare, LANES), jnp.float32) for _ in range(CHAINS)],
+        compiler_params=pltpu.CompilerParams(vmem_limit_bytes=36 << 20),
         name="edges",
-    )(from_at, to_at, scaled, got)
+    )(from_at, to_at, near(scaled), near(got), near(self_part))
     home = lax.all_to_all(back, "dom", split_axis=0, concat_axis=0, tiled=True)
 
-    self_part = lax.dot_general(block_cols, w_self, contract, preferred_element_type=jnp.float32)
-    pre = self_part + master_sum
     return pl.pallas_call(
         functools.partial(final_kernel, slots, hub),
         out_shape=(
@@ -233,8 +258,9 @@
         ),
         in_specs=[VMEM] * 3,
         out_specs=[VMEM] * 3,
+        compiler_params=pltpu.CompilerParams(vmem_limit_bytes=12 << 20),
         name="final",
-    )(asked, home, pre)
+    )(dense, near(home), near(pre))
 
 
 def solution(mesh):

time: 220 us -> 198 us (0.900)
  blocking collectives: 0 us -> 141 us
  waiting for transfers between devices: 130 us -> 5.69 us
  starting transfers between devices: 31 us -> 15.6 us
  Pallas kernels: 39.3 us -> 25.9 us
  local copies, waits for them, and re-layouts: 8.11 us -> 2.39 us
  matrix products: 4.41 us -> 1.9 us
    all_to_all x0 -> x2, blocking collectives: none -> 141 us  [the longest x1 71.2 us: on_device(): got = lax.all_to_all(sent, 'dom', split_axis=0, concat_axis=0, tiled=True)]
    all_to_all x2 -> x0, waiting for transfers between devices: 120 us -> none  [the longest x1 61.4 us: on_device(): got = lax.all_to_all(sent, 'dom', split_axis=0, concat_axis=0, tiled=True)]
    all_to_all x2 -> x0, starting transfers between devices: 15.4 us -> none  [the longest x1 8.27 us: on_device(): home = lax.all_to_all(back, 'dom', split_axis=0, concat_axis=0, tiled=True)]
    pallas_call x2, Pallas kernels: 30.7 us -> 22.5 us  [the longest x1 20.3 us: on_device(): pl.pallas_call(functools.partial(edge_kernel, slots), out_shape=(pltpu.VM...]
    pallas_call x1, Pallas kernels: 8.56 us -> 3.47 us  [on_device(): pl.pallas_call(functools.partial(final_kernel, slots, hub), out_shape=(ja...]
    all_to_all x1, waiting for transfers between devices: 10.2 us -> 5.69 us  [on_device(): lax.all_to_all(wanted, 'dom', split_axis=0, concat_axis=0, tiled=True)]
    unnamed x22 -> x8, local copies, waits for them, and re-layouts: 4.86 us -> 0.91 us
    dot_general x1, matrix products: 2.98 us -> 0.47 us  [on_device(): lax.dot_general(block_cols, w_self, contract, preferred_element_type=jnp....]
  transfers between devices with their start and end apart: 4 -> 2, of which waited for: 3 -> 1; matrix products, arithmetic and copies ran while one was open for 3% -> 3% of each run, Pallas kernels for 0% -> 0%
where the time goes in v2:
time: 198 us; the launch traced here: 197 us
  blocking collectives  141 us (71%)
  Pallas kernels  25.9 us (13%)
  starting transfers between devices  15.6 us (8%)
  waiting for transfers between devices  5.69 us (3%)
  other arithmetic  3.06 us (2%)
  local copies, waits for them, and re-layouts  2.39 us (1%)
    all_to_all x1, blocking collectives, on_device(): got = lax.all_to_all(sent, 'dom', split_axis=0, concat_axis=0, tiled=True)  71.2 us
    all_to_all x1, blocking collectives, on_device(): home = lax.all_to_all(back, 'dom', split_axis=0, concat_axis=0, tiled=True)  69.9 us
    pallas_call x1, Pallas kernels, on_device(): pl.pallas_call(functools.partial(edge_kernel, slots), out_shape=(pltpu.VM...  20.3 us
    all_to_all x1, starting transfers between devices, on_device(): lax.all_to_all(wanted, 'dom', split_axis=0, concat_axis=0, tiled=True)  15.5 us
    all_to_all x1, waiting for transfers between devices, on_device(): lax.all_to_all(wanted, 'dom', split_axis=0, concat_axis=0, tiled=True)  5.69 us
  transfers between devices with their start and end apart: 2, of which 1 were waited for; matrix products, arithmetic and copies ran while one was open for 3% of the time, Pallas kernels for 0%

profile of v2, /device:TPU:2, one launch (start us, length us, event | category | flops | bytes accessed | tf_op | source)
XLA Modules:
  0.0 197.1 jit_solution(15827006699602712366)
XLA Ops:
  0.6 0.0 copy-start
  0.6 1.4 select_convert_fusion
  2.1 0.1 collective-permute-start
  2.2 0.8 reshape.13
  3.0 0.6 pad.4
  3.6 15.5 %all-to-all-start = ((s32[128,1,128]{2,1,0:T(1,128)}), s32[128,1,128]{2,1,0:T(1,128)S(1)}, u32[]{:S(2)}, u32[]{:S(2)}) async-start(s32[128,1,128]{2,1,0:T(1,128)} %bitcast.1), calls=%async_computation | async-start | bytes 131072 | tf_op jit(solution)/shard_map/all_to_all | solution.py:197
  19.8 0.7 convert_element_type.17
  20.5 0.8 fusion.4
  21.3 0.0 copy-start.1
  21.3 0.0 collective-permute-done
  21.3 0.1 broadcast_select_fusion.1
  21.4 0.0 copy-done
  21.4 0.5 fusion.1
  21.9 0.4 copy-done.1
  22.4 0.0 copy-start.2
  22.4 0.0 copy-start.3
  22.4 0.5 fusion.2
  22.9 0.5 copy-done.2
  23.3 0.5 fusion.16.self_ref
  23.8 0.0 copy-done.3
  23.8 0.5 fusion.own_ref
  24.4 5.7 %all-to-all-done = s32[128,1,128]{2,1,0:T(1,128)S(1)} async-done(((s32[128,1,128]{2,1,0:T(1,128)}), s32[128,1,128]{2,1,0:T(1,128)S(1)}, u32[]{:S(2)}, u32[]{:S(2)}) %all-to-all-start) | async-done | bytes 65568 | tf_op jit(solution)/shard_map/all_to_all | solution.py:197
  30.1 2.2 %pack.1 = (bf16[128,40,256]{2,1,0:T(8,128)(2,1)S(1)}, s32[32,128]{1,0:T(8,128)S(1)}) custom-call(s32[128,128]{1,0:T(8,128)S(1)} %bitcast.14, bf16[64,256]{1,0:T(8,128)(2,1)S(1)} %slice.24.hub_ref, bf16[1024,256]{1,0:T(8,128)(2,1)S(1)} %pad_maximum_fusion.1.pay_ref), custom_call_target="tpu_custom_call" | custom-call | tf_op jit(solution)/shard_map/pack/pallas_call | solution.py:225
  32.2 71.2 %all_to_all.21.got_ref = bf16[128,40,256]{2,1,0:T(8,128)(2,1)S(1)} all-to-all(bf16[128,40,256]{2,1,0:T(8,128)(2,1)S(1)} %get-tuple-element.19), channel_id=1, replica_groups=mesh['dom'=128,'feat'=2] {'dom'}, dimensions={0} | all-to-all | bytes 5242880 | tf_op jit(solution)/shard_map/all_to_all | solution.py:236
  103.4 20.3 %edges.1 = (f32[1024,256]{1,0:T(8,128)S(1)}, bf16[128,40,256]{2,1,0:T(8,128)(2,1)S(1)}) custom-call(s32[8192]{0:T(1024)S(1)} %get-tuple-element.16.from_ref, s32[8192]{0:T(1024)S(1)} %get-tuple-element.17.to_ref, bf16[1024,256]{1,0:T(8,128)(2,1)S(1)} %fusion.own_ref, bf16[128,40,256]{2,1,0:T(8,128)(2,1)S(1)} %all_to_all.21.got_ref, ...), custom_call_target="tpu_custom_call" | custom-call | tf_op jit(solution)/shard_map/edges/pallas_call | solution.py:240
  123.7 69.9 %all_to_all.22.got_ref = bf16[128,40,256]{2,1,0:T(8,128)(2,1)S(1)} all-to-all(bf16[128,40,256]{2,1,0:T(8,128)(2,1)S(1)} %get-tuple-element.21), channel_id=1, replica_groups=mesh['dom'=128,'feat'=2] {'dom'}, dimensions={0} | all-to-all | bytes 5242880 | tf_op jit(solution)/shard_map/all_to_all | solution.py:250
  193.6 3.5 %final.1 = (bf16[1024,256]{1,0:T(8,128)(2,1)}, f32[256,512]{1,0:T(8,128)}, f32[256,512]{1,0:T(8,128)}) custom-call(s32[32,128]{1,0:T(8,128)S(1)} %get-tuple-element.15.dense_ref, bf16[128,40,256]{2,1,0:T(8,128)(2,1)S(1)} %all_to_all.22.got_ref, f32[1024,256]{1,0:T(8,128)S(1)} %get-tuple-element.22.pre_ref), custom_call_target="tpu_custom_call" | custom-call | tf_op jit(solution)/shard_map/final/pallas_call | solution.py:252
  (3 shorter events, 0.1 us)
Async XLA Ops:
  0.6 20.8 %copy-start = (bf16[1024,256]{1,0:T(8,128)(2,1)S(1)}, bf16[1024,256]{1,0:T(8,128)(2,1)}, u32[]{:S(2)}) copy-start(bf16[1024,256]{1,0:T(8,128)(2,1)} %param.11) | copy-start | bytes 1572868
  2.1 19.3 %collective-permute-start = (bf16[1024,256]{1,0:T(8,128)(2,1)S(1)}, bf16[1024,256]{1,0:T(8,128)(2,1)S(1)}, u32[]{:S(2)}, u32[]{:S(2)}) collective-permute-start(bf16[1024,256]{1,0:T(8,128)(2,1)S(1)} %select_convert_fusion), channel_id=1, source_target_pairs={{0,1},{1,0},{2,3},{3,2},{4,5},{5,4},{6,7},{7,6},{8,9},{9,8},{10,11... | collective-permute-start | bytes 1572872 | tf_op jit(solution)/shard_map/ppermute | solution.py:207
  3.6 26.5 %all-to-all-start = ((s32[128,1,128]{2,1,0:T(1,128)}), s32[128,1,128]{2,1,0:T(1,128)S(1)}, u32[]{:S(2)}, u32[]{:S(2)}) async-start(s32[128,1,128]{2,1,0:T(1,128)} %bitcast.1), calls=%async_computation | async-start | bytes 131072 | tf_op jit(solution)/shard_map/all_to_all | solution.py:197
  21.3 1.0 copy-start.1
  22.4 0.9 copy-start.2
  22.4 1.4 copy-start.3

commit v3 on v1

v3 whole, which is shorter than its diff:
```python
import functools

import jax
import jax.numpy as jnp
from jax import lax
from jax.experimental import pallas as pl
from jax.experimental.pallas import tpu as pltpu
from jax.sharding import PartitionSpec as P

LANES = 128
SUB = 8
GRID = (4, 8, 4)
CHAINS = 4
UNROLL = 8
VMEM = pl.BlockSpec(memory_space=pltpu.VMEM)
SMEM = pl.BlockSpec(memory_space=pltpu.SMEM)


def near(array):
    return pltpu.with_memory_space_constraint(array, pltpu.VMEM)


def ring(axis, shift):
    nx, nz, ny = GRID
    pairs = []
    for x in range(nx):
        for z in range(nz):
            for y in range(ny):
                tx = (x + shift) % nx if axis == "x" else x
                ty = (y + shift) % ny if axis == "y" else y
                pairs.append(((x * nz + z) * ny + y, (tx * nz + z) * ny + ty))
    return pairs


def columns():
    nx, nz, ny = GRID
    return [[(x * nz + z) * ny + y for z in range(nz)] for x in range(nx) for y in range(ny)]


def sum_of(arrays):
    total = arrays[0].astype(jnp.float32)
    for a in arrays[1:]:
        total = total + a.astype(jnp.float32)
    return total


def picks_kernel(spot_ref, out_ref):
    groups, lanes = spot_ref.shape
    rows = out_ref.shape[2]

    def one(g, carry):
        spread = jnp.broadcast_to(spot_ref[pl.ds(g, 1), :].astype(jnp.float32), (LANES, lanes))
        across = jnp.concatenate([jnp.transpose(spread)] * (rows // min(rows, LANES)), axis=1)
        hub = lax.broadcasted_iota(jnp.int32, (lanes, across.shape[1]), 1).astype(jnp.float32)
        chosen = (across == hub).astype(jnp.float32).astype(jnp.bfloat16)
        out_ref[g] = chosen[:, 0:rows]
        return carry

    lax.fori_loop(0, groups, one, 0)


def edge_kernel(grid, slots, from_ref, to_ref, place_ref, own_ref, self_ref, spot_ref, pick_ref, *rest):
    nx, nz, ny = grid
    got_x = rest[0:ny]
    got_y = rest[ny : ny + nx]
    pre_ref = rest[ny + nx]
    back_x = rest[ny + nx + 1 : 2 * ny + nx + 1]
    back_y = rest[2 * ny + nx + 1 : 2 * (ny + nx) + 1]
    table = rest[2 * (ny + nx) + 1]
    sums = rest[2 * (ny + nx) + 2 :]
    masters, width = own_ref.shape
    halves = width // LANES
    tall = SUB * halves
    edges = from_ref.shape[0]
    deep = nz // 2

    def put(base, block):
        for g in range(block.shape[0] // SUB):
            for h in range(halves):
                at = pl.multiple_of(base + g * tall + h * SUB, SUB)
                table[pl.ds(at, SUB), :] = block[g * SUB : (g + 1) * SUB, h * LANES : (h + 1) * LANES]

    def own(i, carry):
        put(i * 32 * halves, own_ref[pl.ds(pl.multiple_of(i * 32, 32), 32), :].astype(jnp.float32))
        return carry

    lax.fori_loop(0, masters // 32, own, 0)

    def base_of(x, y, high, z):
        owner = (x * nz + high * deep + z) * ny + y
        return (masters + owner * slots) * halves

    def blocks(high, first, second):
        if high:
            x, y = place_ref[first], place_ref[nx + second]
        else:
            x, y = place_ref[second], place_ref[nx + first]
        return x, y, (x * ny + y) * 2 + high

    for high, got in ((0, got_x), (1, got_y)):
        for first in range(len(got)):

            def fetch(second, carry, high=high, first=first, got=got):
                x, y, group = blocks(high, first, second)
                rows = jnp.dot(pick_ref[group], got[first][second], preferred_element_type=jnp.float32)
                for z in range(deep):
                    put(base_of(x, y, high, z), rows[z * slots : (z + 1) * slots])
                return carry

            for second in range(got[first].shape[0]):
                fetch(second, 0)

    clear = 16 * SUB

    def zero(i, carry):
        for s in sums:
            s[pl.ds(pl.multiple_of(i * clear, clear), clear), :] = jnp.zeros((clear, LANES), jnp.float32)
        return carry

    lax.fori_loop(0, table.shape[0] // clear, zero, 0)

    step = CHAINS * UNROLL

    def add(i, carry):
        for j in range(step):
            src = from_ref[i * step + j]
            dst = to_ref[i * step + j]
            into = sums[j % CHAINS]
            at = pl.ds(src, halves, stride=SUB)
            into[at, :] = into[at, :] + table[pl.ds(dst, halves, stride=SUB), :]
        return carry

    lax.fori_loop(0, edges // step, add, 0)

    def merged(base, rows, h):
        tiles = []
        for g in range(rows // SUB):
            at = pl.ds(pl.multiple_of(base + g * tall + h * SUB, SUB), SUB)
            value = sums[0][at, :]
            for s in sums[1:]:
                value = value + s[at, :]
            tiles.append(value)
        return jnp.concatenate(tiles, axis=0)

    def finish(i, carry):
        for h in range(halves):
            rows = pl.ds(pl.multiple_of(i * 32, 32), 32)
            cols = slice(h * LANES, (h + 1) * LANES)
            pre_ref[rows, cols] = self_ref[rows, cols] + merged(i * 32 * halves, 32, h)
        return carry

    lax.fori_loop(0, masters // 32, finish, 0)

    for high, back in ((0, back_x), (1, back_y)):
        for first in range(len(back)):
            for second in range(back[first].shape[0]):
                x, y, group = blocks(high, first, second)
                target = spot_ref[pl.ds(group, 1), :]
                rows = lax.broadcasted_iota(jnp.int32, (back[first].shape[1], target.shape[1]), 0)
                chosen = (rows == target).astype(jnp.float32).astype(jnp.bfloat16)
                block = jnp.concatenate(
                    [
                        jnp.concatenate(
                            [merged(base_of(x, y, high, z), slots, h) for h in range(halves)], axis=1
                        ).astype(jnp.bfloat16)
                        for z in range(deep)
                    ],
                    axis=0,
                )
                back[first][second] = jnp.dot(
                    chosen, block, preferred_element_type=jnp.float32
                ).astype(jnp.bfloat16)


def final_kernel(home_ref, pre_ref, weight_ref, grad_ref, self_ref, neigh_ref):
    hub = home_ref.shape[1]
    parts, pay, width = weight_ref.shape
    total = pre_ref[0:hub, :]
    for z in range(home_ref.shape[0]):
        total = total + home_ref[z].astype(jnp.float32)
    grad_ref[0:hub, :] = total.astype(jnp.bfloat16)
    grad_ref[hub:, :] = pre_ref[hub:, :].astype(jnp.bfloat16)
    quarter = parts // 4
    for which, ref in ((0, self_ref), (1, neigh_ref)):
        for half in range(2):

            def place(i, carry, which=which, ref=ref, half=half):
                peer = (which * 2 + half) * quarter + i
                rows = pl.ds(pl.multiple_of(i * pay, SUB), pay)
                ref[rows, half * width : (half + 1) * width] = weight_ref[peer].astype(jnp.float32)
                return carry

            lax.fori_loop(0, quarter, place, 0)


def on_device(
    features,
    grad_out,
    pre_act,
    neigh_mean,
    w_self,
    w_neigh,
    edge_from,
    edge_to,
    edge_count,
    mirror_master,
    degrees,
):
    nx, nz, ny = GRID
    deep = nz // 2
    masters, width = features.shape
    parts = lax.axis_size("dom")
    mirrors = mirror_master.shape[0]
    slots = mirrors // parts
    hub = min(masters, 64)
    local = masters + mirrors
    halves = width // LANES
    edges = edge_from.shape[0]
    contract = (((1,), (1,)), ((), ()))
    over_rows = (((0,), (0,)), ((), ()))
    first = lax.axis_index("feat") == 0

    def both(rows_out, rows_act):
        mine = (rows_out.astype(jnp.float32) * (rows_act > 0).astype(jnp.float32)).astype(jnp.bfloat16)
        other = lax.ppermute(mine, "feat", [(0, 1), (1, 0)])
        return jnp.concatenate([jnp.where(first, mine, other), jnp.where(first, other, mine)], axis=1)

    def scale(cols, degree):
        part = lax.dot_general(cols, w_neigh, contract, preferred_element_type=jnp.float32)
        return (part / degree[:, None].astype(jnp.float32)).astype(jnp.bfloat16)

    shared = scale(both(grad_out[:hub], pre_act[:hub]), degrees[:hub])
    column = lax.all_to_all(
        jnp.broadcast_to(shared, (nz, *shared.shape)),
        "dom",
        split_axis=0,
        concat_axis=0,
        axis_index_groups=columns(),
        tiled=True,
    )
    column, grad_out, pre_act = lax.optimization_barrier((column, grad_out, pre_act))

    low = column[:deep].reshape(deep * hub, width)
    high = column[deep:].reshape(deep * hub, width)
    low_set = jnp.stack([low] + [lax.ppermute(low, "dom", ring("x", k)) for k in range(1, nx)])
    high_set = jnp.stack([high] + [lax.ppermute(high, "dom", ring("y", k)) for k in range(1, ny)])

    block_cols = both(grad_out, pre_act)
    scaled = scale(block_cols, degrees)
    self_part = lax.dot_general(block_cols, w_self, contract, preferred_element_type=jnp.float32)
    grad_self = lax.dot_general(features, block_cols, over_rows, preferred_element_type=jnp.float32)
    grad_neigh = lax.dot_general(neigh_mean, block_cols, over_rows, preferred_element_type=jnp.float32)
    pay = jnp.concatenate(
        [grad_self[:, :width], grad_self[:, width:], grad_neigh[:, :width], grad_neigh[:, width:]], axis=0
    ).astype(jnp.bfloat16)
    tail = pay.shape[0] // parts

    low_set, high_set, pay = lax.optimization_barrier((low_set, high_set, pay))
    low_got = [low_set] + [lax.ppermute(low_set, "dom", ring("y", k)) for k in range(1, ny)]
    high_got = [high_set] + [lax.ppermute(high_set, "dom", ring("x", k)) for k in range(1, nx)]
    pieces = lax.all_to_all(
        pay.reshape(parts, tail, width), "dom", split_axis=0, concat_axis=0, tiled=True
    )

    order = mirror_master.reshape(nx, 2, deep, ny, slots).transpose(0, 3, 1, 2, 4)
    spots = order.reshape(nx * ny * 2, deep * slots) + jnp.repeat(
        jnp.arange(deep, dtype=jnp.int32) * hub, slots
    )
    chosen = pl.pallas_call(
        picks_kernel,
        out_shape=pltpu.VMEM((nx * ny * 2, deep * slots, deep * hub), jnp.bfloat16),
        in_specs=[VMEM],
        out_specs=VMEM,
        compiler_params=pltpu.CompilerParams(vmem_limit_bytes=8 << 20),
        name="picks",
    )(spots)

    def spot(row):
        return (row // SUB) * (SUB * halves) + row % SUB

    live = jnp.arange(edges, dtype=jnp.int32) < edge_count[0]
    from_at = spot(jnp.where(live, edge_from, local))
    to_at = spot(edge_to)
    me = lax.axis_index("dom")
    my_x, my_y = me // (nz * ny), me % ny
    place = jnp.concatenate(
        [(my_x - jnp.arange(nx, dtype=jnp.int32)) % nx, (my_y - jnp.arange(ny, dtype=jnp.int32)) % ny]
    ).astype(jnp.int32)

    lanes = local * halves
    low_type = jax.ShapeDtypeStruct(low_set.shape, jnp.bfloat16)
    high_type = jax.ShapeDtypeStruct(high_set.shape, jnp.bfloat16)
    results = pl.pallas_call(
        functools.partial(edge_kernel, GRID, slots),
        out_shape=[jax.ShapeDtypeStruct((masters, width), jnp.float32)] + [low_type] * ny + [high_type] * nx,
        in_specs=[SMEM] * 3 + [VMEM] * (4 + nx + ny),
        out_specs=[VMEM] * (1 + nx + ny),
        scratch_shapes=[pltpu.VMEM((lanes, LANES), jnp.float32)]
        + [pltpu.VMEM((lanes + SUB * halves, LANES), jnp.float32) for _ in range(CHAINS)],
        compiler_params=pltpu.CompilerParams(vmem_limit_bytes=34 << 20),
        name="edges",
    )(from_at, to_at, place, *(near(a) for a in (scaled, self_part, spots, chosen, *low_got, *high_got)))
    pre, low_back, high_back = results[0], results[1 : 1 + ny], results[1 + ny :]

    share = jnp.sum(pieces.astype(jnp.float32), axis=0).astype(jnp.bfloat16)
    low_back, high_back, share = lax.optimization_barrier((low_back, high_back, share))
    low_part = [low_back[0]] + [lax.ppermute(low_back[k], "dom", ring("y", -k)) for k in range(1, ny)]
    high_part = [high_back[0]] + [lax.ppermute(high_back[k], "dom", ring("x", -k)) for k in range(1, nx)]
    weights = lax.all_to_all(
        jnp.broadcast_to(share, (parts, *share.shape)), "dom", split_axis=0, concat_axis=0, tiled=True
    )
    low_sum = [sum_of([p[k] for p in low_part]) for k in range(nx)]
    high_sum = [sum_of([p[k] for p in high_part]) for k in range(ny)]
    low_sent = [low_sum[0]] + [
        lax.ppermute(low_sum[k].astype(jnp.bfloat16), "dom", ring("x", -k)) for k in range(1, nx)
    ]
    high_sent = [high_sum[0]] + [
        lax.ppermute(high_sum[k].astype(jnp.bfloat16), "dom", ring("y", -k)) for k in range(1, ny)
    ]
    column_sum = jnp.concatenate([sum_of(low_sent), sum_of(high_sent)], axis=0).astype(jnp.bfloat16)
    column_sum, weights, pre = lax.optimization_barrier((column_sum, weights, pre))
    home = lax.all_to_all(
        column_sum.reshape(nz, hub, width),
        "dom",
        split_axis=0,
        concat_axis=0,
        axis_index_groups=columns(),
        tiled=True,
    )
    return pl.pallas_call(
        final_kernel,
        out_shape=(
            jax.ShapeDtypeStruct((masters, width), jnp.bfloat16),
            jax.ShapeDtypeStruct(w_self.shape, jnp.float32),
            jax.ShapeDtypeStruct(w_neigh.shape, jnp.float32),
        ),
        in_specs=[VMEM] * 3,
        out_specs=[VMEM] * 3,
        compiler_params=pltpu.CompilerParams(vmem_limit_bytes=12 << 20),
        name="final",
    )(near(home), near(pre), near(weights))


def solution(mesh):
    placed = (
        P("dom", "feat"),
        P("dom", "feat"),
        P("dom", "feat"),
        P("dom", "feat"),
        P("feat", None),
        P("feat", None),
        P("dom"),
        P("dom"),
        P("dom"),
        P("dom"),
        P("dom"),
    )

    return jax.shard_map(
        on_device,
        mesh=mesh,
        in_specs=placed,
        out_specs=(P("dom", "feat"), P("feat", None), P("feat", None)),
        check_vma=False,
    )
```

time: 220 us -> 203 us (0.923)
  waiting for transfers between devices: 130 us -> 46 us
  blocking collectives: 0 us -> 37.5 us
  starting transfers between devices: 31 us -> 66.2 us
  Pallas kernels: 39.3 us -> 24.9 us
  other arithmetic: 4.49 us -> 11.4 us
    all_to_all x3 -> x2, waiting for transfers between devices: 130 us -> 0.01 us  [the longest x1 0.01 us: on_device(): lax.all_to_all(pay.reshape(parts, tail, width), 'dom', split_axis=0, conc...]
    ppermute x1 -> x26, waiting for transfers between devices: 0.01 us -> 46 us  [the longest x3 18.8 us: on_device(): lax.ppermute(low_set, 'dom', ring('y', k))]
    ppermute x1 -> x26, starting transfers between devices: 0.09 us -> 41.9 us  [the longest x3 6.31 us: on_device(): lax.ppermute(high_back[k], 'dom', ring('x', -k))]
    all_to_all x0 -> x2, blocking collectives: none -> 37.5 us  [the longest x1 20.5 us: on_device(): lax.all_to_all(jnp.broadcast_to(shared, (nz, *shared.shape)), 'dom', spli...]
    pallas_call x3, Pallas kernels: 39.3 us -> 24.9 us  [the longest x1 19.5 us: on_device(): pl.pallas_call(functools.partial(edge_kernel, GRID, slots), out_shape=[ja...]
    all_to_all x3 -> x2, starting transfers between devices: 30.9 us -> 24.3 us  [the longest x1 13.7 us: on_device(): lax.all_to_all(jnp.broadcast_to(share, (parts, *share.shape)), 'dom', spl...]
    unnamed x22 -> x54, local copies, waits for them, and re-layouts: 4.86 us -> 8.89 us
    another operation x0 -> x4, other arithmetic: none -> 3.25 us
  transfers between devices with their start and end apart: 4 -> 28, of which waited for: 3 -> 10; matrix products, arithmetic and copies ran while one was open for 3% -> 5% of each run, Pallas kernels for 0% -> 11%
where the time goes in v3:
time: 203 us; the launch traced here: 202 us
  starting transfers between devices  66.2 us (33%)
  waiting for transfers between devices  46 us (23%)
  blocking collectives  37.5 us (18%)
  Pallas kernels  24.9 us (12%)
  other arithmetic  11.4 us (6%)
  local copies, waits for them, and re-layouts  10.2 us (5%)
  matrix products  4.25 us (2%)
    all_to_all x1, blocking collectives, on_device(): lax.all_to_all(jnp.broadcast_to(shared, (nz, *shared.shape)), 'dom', spli...  20.5 us
    pallas_call x1, Pallas kernels, on_device(): pl.pallas_call(functools.partial(edge_kernel, GRID, slots), out_shape=[ja...  19.5 us
    ppermute x3, waiting for transfers between devices, on_device(): lax.ppermute(low_set, 'dom', ring('y', k))  18.8 us
    all_to_all x1, blocking collectives, on_device(): lax.all_to_all(column_sum.reshape(nz, hub, width), 'dom', split_axis=0, c...  17 us
    all_to_all x1, starting transfers between devices, on_device(): lax.all_to_all(jnp.broadcast_to(share, (parts, *share.shape)), 'dom', spl...  13.7 us
    ppermute x3, waiting for transfers between devices, on_device(): lax.ppermute(low_back[k], 'dom', ring('y', -k))  13 us
    all_to_all x1, starting transfers between devices, on_device(): lax.all_to_all(pay.reshape(parts, tail, width), 'dom', split_axis=0, conc...  10.5 us
    unnamed x54, local copies, waits for them, and re-layouts  8.89 us
  transfers between devices with their start and end apart: 28, of which 10 were waited for; matrix products, arithmetic and copies ran while one was open for 5% of the time, Pallas kernels for 11%

profile of v3, /device:TPU:2, one launch (start us, length us, event | category | flops | bytes accessed | tf_op | source)
XLA Modules:
  0.0 202.1 jit_solution(6381983283266087278)
XLA Ops:
  0.7 0.8 select_convert_fusion.1
  1.6 0.7 slice_convert_fusion
  2.3 0.5 collective-permute-done
  2.8 1.2 fusion.3
  4.0 20.5 %all_to_all.20 = bf16[8,64,256]{2,1,0:T(8,128)(2,1)S(1)} all-to-all(bf16[8,64,256]{2,1,0:T(8,128)(2,1)S(1)} %broadcast_in_dim.16), channel_id=1, replica_groups={{0,8,16,24,32,40,48,56},{2,10,18,26,34,42,50,58},{4,12,20,28,36,44,52,6..., dimensions={0} | all-to-all | bytes 524288 | tf_op jit(solution)/shard_map/all_to_all | solution.py:233
  24.5 1.4 select_convert_fusion
  26.0 0.6 collective-permute-start.4
  26.6 2.4 %collective-permute-start.3 = (bf16[256,256]{1,0:T(8,128)(2,1)S(1)}, bf16[256,256]{1,0:T(8,128)(2,1)S(1)}, u32[]{:S(2)}, u32[]{:S(2)}) collective-permute-start(bf16[256,256]{1,0:T(8,128)(2,1)S(1)} %bitcast.58), channel_id=1, source_target_pairs={{0,128},{2,130},{4,132},{6,134},{8,136},{10,138},{12,140},{14,142}... | collective-permute-start | bytes 393224 | tf_op jit(solution)/shard_map/ppermute | solution.py:245
  29.0 1.8 collective-permute-start.2
  30.8 3.0 %collective-permute-start.7 = (bf16[256,256]{1,0:T(8,128)(2,1)S(1)}, bf16[256,256]{1,0:T(8,128)(2,1)S(1)}, u32[]{:S(2)}, u32[]{:S(2)}) collective-permute-start(bf16[256,256]{1,0:T(8,128)(2,1)S(1)} %bitcast.53), channel_id=1, source_target_pairs={{0,6},{2,0},{4,2},{6,4},{8,14},{10,8},{12,10},{14,12},{16,22},{18,... | collective-permute-start | bytes 393224 | tf_op jit(solution)/shard_map/ppermute | solution.py:246
  33.8 1.3 collective-permute-start.6
  35.1 0.5 collective-permute-done.3
  35.7 1.6 collective-permute-start.5
  37.7 1.5 collective-permute-done.7
  39.2 1.2 collective-permute-done.6
  40.4 2.7 %collective-permute-done.5 = bf16[256,256]{1,0:T(8,128)(2,1)S(1)} collective-permute-done((bf16[256,256]{1,0:T(8,128)(2,1)S(1)}, bf16[256,256]{1,0:T(8,128)(2,1)S(1)}, u32[]{:S(2)}, u32[]{:S(2)}) %collective-permute-start.5) | collective-permute-done | bytes 131104 | tf_op jit(solution)/shard_map/ppermute | solution.py:246
  43.1 0.9 pad_maximum_fusion.2.rest_4_
  44.1 0.5 fusion.1
  44.6 0.6 copy-done.24
  45.1 0.5 fusion.2
  45.7 0.8 pad_maximum_fusion.3
  46.6 10.5 %all-to-all-start.1 = ((bf16[128,8,256]{2,1,0:T(8,128)(2,1)}), bf16[128,8,256]{2,1,0:T(8,128)(2,1)}, u32[]{:S(2)}, u32[]{:S(2)}) async-start(bf16[128,8,256]{2,1,0:T(8,128)(2,1)} %bitcast.14), calls=%async_computation.1 | async-start | bytes 1048576 | tf_op jit(solution)/shard_map/all_to_all | solution.py:261
  57.1 2.8 %collective-permute-start.10 = (bf16[4,256,256]{2,1,0:T(8,128)(2,1)S(1)}, bf16[4,256,256]{2,1,0:T(8,128)(2,1)}, u32[]{:S(2)}, u32[]{:S(2)}) collective-permute-start(bf16[4,256,256]{2,1,0:T(8,128)(2,1)S(1)} %pad_maximum_fusion.1.rest_0_), channel_id=1, source_target_pairs={{0,6},{2,0},{4,2},{6,4},{8,14},{10,8},{12,10},{14,12},{16,22},{18,... | collective-permute-start | bytes 1572872 | tf_op jit(solution)/shard_map/ppermute | solution.py:259
  60.5 3.3 %picks.1.pick_ref = bf16[32,128,256]{2,1,0:T(8,128)(2,1)S(1)} custom-call(s32[32,128]{1,0:T(8,128)S(1)} %broadcast_add_fusion.spot_ref), custom_call_target="tpu_custom_call" | custom-call | tf_op jit(solution)/shard_map/picks/pallas_call | solution.py:269
  64.1 0.9 collective-permute-start.9
  65.1 0.9 collective-permute-start.8
  66.4 2.7 %collective-permute-start.12 = (bf16[4,256,256]{2,1,0:T(8,128)(2,1)}, bf16[4,256,256]{2,1,0:T(8,128)(2,1)S(1)}, u32[]{:S(2)}, u32[]{:S(2)}) collective-permute-start(bf16[4,256,256]{2,1,0:T(8,128)(2,1)} %pad_maximum_fusion.2.rest_4_), channel_id=1, source_target_pairs={{0,128},{2,130},{4,132},{6,134},{8,136},{10,138},{12,140},{14,142}... | collective-permute-start | bytes 1572872 | tf_op jit(solution)/shard_map/ppermute | solution.py:260
  69.1 16.6 %collective-permute-done.10.rest_3_ = bf16[4,256,256]{2,1,0:T(8,128)(2,1)} collective-permute-done((bf16[4,256,256]{2,1,0:T(8,128)(2,1)S(1)}, bf16[4,256,256]{2,1,0:T(8,128)(2,1)}, u32[]{:S(2)}, u32[]{:S(2)}) %collective-permute-start.10) | collective-permute-done | bytes 524320 | tf_op jit(solution)/shard_map/ppermute | solution.py:259
  85.7 1.4 collective-permute-start.11
  87.1 1.7 fusion.35.self_ref
  89.3 2.1 %collective-permute-done.8.rest_1_ = bf16[4,256,256]{2,1,0:T(8,128)(2,1)S(1)} collective-permute-done((bf16[4,256,256]{2,1,0:T(8,128)(2,1)S(1)}, bf16[4,256,256]{2,1,0:T(8,128)(2,1)S(1)}, u32[]{:S(2)}, u32[]{:S(2)}) %collective-permute-start.8) | collective-permute-done | bytes 524320 | tf_op jit(solution)/shard_map/ppermute | solution.py:259
  91.5 3.6 %collective-permute-done.11.rest_5_ = bf16[4,256,256]{2,1,0:T(8,128)(2,1)S(1)} collective-permute-done((bf16[4,256,256]{2,1,0:T(8,128)(2,1)}, bf16[4,256,256]{2,1,0:T(8,128)(2,1)S(1)}, u32[]{:S(2)}, u32[]{:S(2)}) %collective-permute-start.11) | collective-permute-done | bytes 524320 | tf_op jit(solution)/shard_map/ppermute | solution.py:260
  95.1 19.5 %edges.1 = (f32[1024,256]{1,0:T(8,128)S(1)}, bf16[4,256,256]{2,1,0:T(8,128)(2,1)S(1)}, bf16[4,256,256]{2,1,0:T(8,128)(2,1)S(1)}, bf16[4,256,256]{2,1,0:T(8,128)(...) custom-call(s32[8192]{0:T(1024)S(1)} %get-tuple-element.77.from_ref,, ...), custom_call_target="tpu_custom_call" | custom-call | tf_op jit(solution)/shard_map/edges/pallas_call | solution.py:293
  114.6 1.0 copy-done.2
  115.7 0.8 copy-done.4
  116.5 0.8 copy-done.6
  117.3 0.8 copy-done.8
  118.1 0.8 copy-done.9
  118.9 0.8 copy-done.10
  119.7 0.8 copy-done.11
  120.4 0.8 copy-done.12
  121.3 0.8 copy-done.13
  122.1 1.3 reduce_sum.12
  123.3 3.7 %collective-permute-start.14 = (bf16[4,256,256]{2,1,0:T(8,128)(2,1)}, bf16[4,256,256]{2,1,0:T(8,128)(2,1)S(1)}, u32[]{:S(2)}, u32[]{:S(2)}) collective-permute-start(bf16[4,256,256]{2,1,0:T(8,128)(2,1)} %copy-done.13), channel_id=1, source_target_pairs={{0,6},{2,0},{4,2},{6,4},{8,14},{10,8},{12,10},{14,12},{16,22},{18,... | collective-permute-start | bytes 1572872 | tf_op jit(solution)/shard_map/ppermute | solution.py:307
  127.0 1.0 collective-permute-start.16
  128.0 2.3 %collective-permute-start.20 = (bf16[4,256,256]{2,1,0:T(8,128)(2,1)}, bf16[4,256,256]{2,1,0:T(8,128)(2,1)S(1)}, u32[]{:S(2)}, u32[]{:S(2)}) collective-permute-start(bf16[4,256,256]{2,1,0:T(8,128)(2,1)} %copy-done.10), channel_id=1, source_target_pairs={{0,192},{2,194},{4,196},{6,198},{8,200},{10,202},{12,204},{14,206}... | collective-permute-start | bytes 1572872 | tf_op jit(solution)/shard_map/ppermute | solution.py:308
  130.3 2.0 collective-permute-start.21
  132.3 13.0 %collective-permute-done.14 = bf16[4,256,256]{2,1,0:T(8,128)(2,1)S(1)} collective-permute-done((bf16[4,256,256]{2,1,0:T(8,128)(2,1)}, bf16[4,256,256]{2,1,0:T(8,128)(2,1)S(1)}, u32[]{:S(2)}, u32[]{:S(2)}) %collective-permute-start.14) | collective-permute-done | bytes 524320 | tf_op jit(solution)/shard_map/ppermute | solution.py:307
  145.3 2.0 collective-permute-start.22
  147.3 0.8 broadcast_in_dim.18
  148.2 13.7 %all-to-all-start.2 = ((bf16[128,8,256]{2,1,0:T(8,128)(2,1)}), bf16[128,8,256]{2,1,0:T(8,128)(2,1)S(1)}, u32[]{:S(2)}, u32[]{:S(2)}) async-start(bf16[128,8,256]{2,1,0:T(8,128)(2,1)} %broadcast_in_dim.18), calls=%async_computation.2 | async-start | bytes 1048576 | tf_op jit(solution)/shard_map/all_to_all | solution.py:309
  161.9 1.4 fusion.10
  163.3 0.9 collective-permute-start.17
  164.2 1.2 collective-permute-start.19
  165.4 0.8 copy-done.18
  166.2 3.7 %collective-permute-start.18 = (bf16[256,256]{1,0:T(8,128)(2,1)S(1)}, bf16[256,256]{1,0:T(8,128)(2,1)S(1)}, u32[]{:S(2)}, u32[]{:S(2)}) collective-permute-start(bf16[256,256]{1,0:T(8,128)(2,1)S(1)} %get-tuple-element.59), channel_id=1, source_target_pairs={{0,128},{2,130},{4,132},{6,134},{8,136},{10,138},{12,140},{14,142}... | collective-permute-start | bytes 393224 | tf_op jit(solution)/shard_map/ppermute | solution.py:315
  170.0 1.5 fusion.13
  171.5 2.8 %collective-permute-start.23 = (bf16[256,256]{1,0:T(8,128)(2,1)S(1)}, bf16[256,256]{1,0:T(8,128)(2,1)S(1)}, u32[]{:S(2)}, u32[]{:S(2)}) collective-permute-start(bf16[256,256]{1,0:T(8,128)(2,1)S(1)} %get-tuple-element.60), channel_id=1, source_target_pairs={{0,6},{2,0},{4,2},{6,4},{8,14},{10,8},{12,10},{14,12},{16,22},{18,... | collective-permute-start | bytes 393224 | tf_op jit(solution)/shard_map/ppermute | solution.py:318
  174.3 2.3 %collective-permute-start.24 = (bf16[256,256]{1,0:T(8,128)(2,1)S(1)}, bf16[256,256]{1,0:T(8,128)(2,1)S(1)}, u32[]{:S(2)}, u32[]{:S(2)}) collective-permute-start(bf16[256,256]{1,0:T(8,128)(2,1)S(1)} %get-tuple-element.62), channel_id=1, source_target_pairs={{0,4},{2,6},{4,0},{6,2},{8,12},{10,14},{12,8},{14,10},{16,20},{18,... | collective-permute-start | bytes 393224 | tf_op jit(solution)/shard_map/ppermute | solution.py:318
  176.6 1.2 fusion.9
  177.7 4.1 %collective-permute-done.25 = bf16[256,256]{1,0:T(8,128)(2,1)S(1)} collective-permute-done((bf16[256,256]{1,0:T(8,128)(2,1)S(1)}, bf16[256,256]{1,0:T(8,128)(2,1)S(1)}, u32[]{:S(2)}, u32[]{:S(2)}) %collective-permute-start.25) | collective-permute-done | bytes 131104 | tf_op jit(solution)/shard_map/ppermute | solution.py:318
  181.8 1.2 fusion.6
  183.1 17.0 %all_to_all.21.home_ref = bf16[8,64,256]{2,1,0:T(8,128)(2,1)S(1)} all-to-all(bf16[8,64,256]{2,1,0:T(8,128)(2,1)S(1)} %bitcast.52), channel_id=1, replica_groups={{0,8,16,24,32,40,48,56},{2,10,18,26,34,42,50,58},{4,12,20,28,36,44,52,6..., dimensions={0} | all-to-all | bytes 524288 | tf_op jit(solution)/shard_map/all_to_all | solution.py:322
  200.1 2.0 final.1
  (85 shorter events, 2.0 us)
Async XLA Ops:
  0.6 43.4 %copy-start = (bf16[1024,256]{1,0:T(8,128)(2,1)S(1)}, bf16[1024,256]{1,0:T(8,128)(2,1)}, u32[]{:S(2)}) copy-start(bf16[1024,256]{1,0:T(8,128)(2,1)} %param.11) | copy-start | bytes 1572868
  0.6 36.8 %copy-start.22 = (s32[4096]{0:T(1024)S(1)}, s32[4096]{0:T(1024)}, u32[]{:S(2)}) copy-start(s32[4096]{0:T(1024)} %param.20) | copy-start | bytes 49156
  1.5 1.3 collective-permute-start
  25.8 18.1 %collective-permute-start.1 = (bf16[1024,256]{1,0:T(8,128)(2,1)S(1)}, bf16[1024,256]{1,0:T(8,128)(2,1)S(1)}, u32[]{:S(2)}, u32[]{:S(2)}) collective-permute-start(bf16[1024,256]{1,0:T(8,128)(2,1)S(1)} %select_convert_fusion), channel_id=1, source_target_pairs={{0,1},{1,0},{2,3},{3,2},{4,5},{5,4},{6,7},{7,6},{8,9},{9,8},{10,11... | collective-permute-start | bytes 1572872 | tf_op jit(solution)/shard_map/ppermute | solution.py:225
  26.0 7.9 %collective-permute-start.4 = (bf16[256,256]{1,0:T(8,128)(2,1)S(1)}, bf16[256,256]{1,0:T(8,128)(2,1)S(1)}, u32[]{:S(2)}, u32[]{:S(2)}) collective-permute-start(bf16[256,256]{1,0:T(8,128)(2,1)S(1)} %bitcast.57), channel_id=1, source_target_pairs={{0,192},{2,194},{4,196},{6,198},{8,200},{10,202},{12,204},{14,206}... | collective-permute-start | bytes 393224 | tf_op jit(solution)/shard_map/ppermute | solution.py:245
  26.6 9.1 %collective-permute-start.3 = (bf16[256,256]{1,0:T(8,128)(2,1)S(1)}, bf16[256,256]{1,0:T(8,128)(2,1)S(1)}, u32[]{:S(2)}, u32[]{:S(2)}) collective-permute-start(bf16[256,256]{1,0:T(8,128)(2,1)S(1)} %bitcast.58), channel_id=1, source_target_pairs={{0,128},{2,130},{4,132},{6,134},{8,136},{10,138},{12,140},{14,142}... | collective-permute-start | bytes 393224 | tf_op jit(solution)/shard_map/ppermute | solution.py:245
  29.0 8.6 %collective-permute-start.2 = (bf16[256,256]{1,0:T(8,128)(2,1)S(1)}, bf16[256,256]{1,0:T(8,128)(2,1)S(1)}, u32[]{:S(2)}, u32[]{:S(2)}) collective-permute-start(bf16[256,256]{1,0:T(8,128)(2,1)S(1)} %bitcast.59), channel_id=1, source_target_pairs={{0,64},{2,66},{4,68},{6,70},{8,72},{10,74},{12,76},{14,78},{16,80}... | collective-permute-start | bytes 393224 | tf_op jit(solution)/shard_map/ppermute | solution.py:245
  30.8 8.4 %collective-permute-start.7 = (bf16[256,256]{1,0:T(8,128)(2,1)S(1)}, bf16[256,256]{1,0:T(8,128)(2,1)S(1)}, u32[]{:S(2)}, u32[]{:S(2)}) collective-permute-start(bf16[256,256]{1,0:T(8,128)(2,1)S(1)} %bitcast.53), channel_id=1, source_target_pairs={{0,6},{2,0},{4,2},{6,4},{8,14},{10,8},{12,10},{14,12},{16,22},{18,... | collective-permute-start | bytes 393224 | tf_op jit(solution)/shard_map/ppermute | solution.py:246
  33.8 6.6 %collective-permute-start.6 = (bf16[256,256]{1,0:T(8,128)(2,1)S(1)}, bf16[256,256]{1,0:T(8,128)(2,1)S(1)}, u32[]{:S(2)}, u32[]{:S(2)}) collective-permute-start(bf16[256,256]{1,0:T(8,128)(2,1)S(1)} %bitcast.54), channel_id=1, source_target_pairs={{0,4},{2,6},{4,0},{6,2},{8,12},{10,14},{12,8},{14,10},{16,20},{18,... | collective-permute-start | bytes 393224 | tf_op jit(solution)/shard_map/ppermute | solution.py:246
  35.7 7.4 %collective-permute-start.5 = (bf16[256,256]{1,0:T(8,128)(2,1)S(1)}, bf16[256,256]{1,0:T(8,128)(2,1)S(1)}, u32[]{:S(2)}, u32[]{:S(2)}) collective-permute-start(bf16[256,256]{1,0:T(8,128)(2,1)S(1)} %bitcast.55), channel_id=1, source_target_pairs={{0,2},{2,4},{4,6},{6,0},{8,10},{10,12},{12,14},{14,8},{16,18},{18,... | collective-permute-start | bytes 393224 | tf_op jit(solution)/shard_map/ppermute | solution.py:246
  44.0 1.2 copy-start.24
  44.0 1.6 copy-start.14
  44.0 1.6 copy-start.16
  45.6 14.2 %copy-start.23 = (s32[1024]{0:T(1024)S(1)}, s32[1024]{0:T(1024)}, u32[]{:S(2)}) copy-start(s32[1024]{0:T(1024)} %param.21) | copy-start | bytes 12292
  45.7 18.4 %copy-start.20 = (s32[8192]{0:T(1024)S(1)}, s32[8192]{0:T(1024)}, u32[]{:S(2)}) copy-start(s32[8192]{0:T(1024)} %param.17) | copy-start | bytes 98308
  45.7 18.3 %copy-start.21 = (s32[8192]{0:T(1024)S(1)}, s32[8192]{0:T(1024)}, u32[]{:S(2)}) copy-start(s32[8192]{0:T(1024)} %param.18) | copy-start | bytes 98308
  45.7 41.4 %copy-start.25 = (bf16[256,512]{1,0:T(8,128)(2,1)S(1)}, bf16[256,512]{1,0:T(8,128)(2,1)}, u32[]{:S(2)}) copy-start(bf16[256,512]{1,0:T(8,128)(2,1)} %param.15) | copy-start | bytes 786436
  46.6 75.5 %all-to-all-start.1 = ((bf16[128,8,256]{2,1,0:T(8,128)(2,1)}), bf16[128,8,256]{2,1,0:T(8,128)(2,1)}, u32[]{:S(2)}, u32[]{:S(2)}) async-start(bf16[128,8,256]{2,1,0:T(8,128)(2,1)} %bitcast.14), calls=%async_computation.1 | async-start | bytes 1048576 | tf_op jit(solution)/shard_map/all_to_all | solution.py:261
  57.1 28.6 %collective-permute-start.10 = (bf16[4,256,256]{2,1,0:T(8,128)(2,1)S(1)}, bf16[4,256,256]{2,1,0:T(8,128)(2,1)}, u32[]{:S(2)}, u32[]{:S(2)}) collective-permute-start(bf16[4,256,256]{2,1,0:T(8,128)(2,1)S(1)} %pad_maximum_fusion.1.rest_0_), channel_id=1, source_target_pairs={{0,6},{2,0},{4,2},{6,4},{8,14},{10,8},{12,10},{14,12},{16,22},{18,... | collective-permute-start | bytes 1572872 | tf_op jit(solution)/shard_map/ppermute | solution.py:259
  63.9 24.9 %copy-start.15 = (bf16[1024,256]{1,0:T(8,128)(2,1)S(1)}, bf16[1024,256]{1,0:T(8,128)(2,1)}, u32[]{:S(2)}) copy-start(bf16[1024,256]{1,0:T(8,128)(2,1)} %copy-done.14) | copy-start | bytes 1572868
  63.9 24.9 %copy-start.17 = (bf16[1024,256]{1,0:T(8,128)(2,1)S(1)}, bf16[1024,256]{1,0:T(8,128)(2,1)}, u32[]{:S(2)}) copy-start(bf16[1024,256]{1,0:T(8,128)(2,1)} %copy-done.16) | copy-start | bytes 1572868
  63.9 24.9 %copy-start.26 = (bf16[256,512]{1,0:T(8,128)(2,1)S(1)}, bf16[256,512]{1,0:T(8,128)(2,1)}, u32[]{:S(2)}) copy-start(bf16[256,512]{1,0:T(8,128)(2,1)} %param.16) | copy-start | bytes 786436
  64.1 25.2 %collective-permute-start.9 = (bf16[4,256,256]{2,1,0:T(8,128)(2,1)S(1)}, bf16[4,256,256]{2,1,0:T(8,128)(2,1)S(1)}, u32[]{:S(2)}, u32[]{:S(2)}) collective-permute-start(bf16[4,256,256]{2,1,0:T(8,128)(2,1)S(1)} %pad_maximum_fusion.1.rest_0_), channel_id=1, source_target_pairs={{0,4},{2,6},{4,0},{6,2},{8,12},{10,14},{12,8},{14,10},{16,20},{18,... | collective-permute-start | bytes 1572872 | tf_op jit(solution)/shard_map/ppermute | solution.py:259
  65.1 26.4 %collective-permute-start.8 = (bf16[4,256,256]{2,1,0:T(8,128)(2,1)S(1)}, bf16[4,256,256]{2,1,0:T(8,128)(2,1)S(1)}, u32[]{:S(2)}, u32[]{:S(2)}) collective-permute-start(bf16[4,256,256]{2,1,0:T(8,128)(2,1)S(1)} %pad_maximum_fusion.1.rest_0_), channel_id=1, source_target_pairs={{0,2},{2,4},{4,6},{6,0},{8,10},{10,12},{12,14},{14,8},{16,18},{18,... | collective-permute-start | bytes 1572872 | tf_op jit(solution)/shard_map/ppermute | solution.py:259
  65.9 25.6 %collective-permute-start.13 = (bf16[4,256,256]{2,1,0:T(8,128)(2,1)}, bf16[4,256,256]{2,1,0:T(8,128)(2,1)S(1)}, u32[]{:S(2)}, u32[]{:S(2)}) collective-permute-start(bf16[4,256,256]{2,1,0:T(8,128)(2,1)} %pad_maximum_fusion.2.rest_4_), channel_id=1, source_target_pairs={{0,192},{2,194},{4,196},{6,198},{8,200},{10,202},{12,204},{14,206}... | collective-permute-start | bytes 1572872 | tf_op jit(solution)/shard_map/ppermute | solution.py:260
  66.4 25.1 %collective-permute-start.12 = (bf16[4,256,256]{2,1,0:T(8,128)(2,1)}, bf16[4,256,256]{2,1,0:T(8,128)(2,1)S(1)}, u32[]{:S(2)}, u32[]{:S(2)}) collective-permute-start(bf16[4,256,256]{2,1,0:T(8,128)(2,1)} %pad_maximum_fusion.2.rest_4_), channel_id=1, source_target_pairs={{0,128},{2,130},{4,132},{6,134},{8,136},{10,138},{12,140},{14,142}... | collective-permute-start | bytes 1572872 | tf_op jit(solution)/shard_map/ppermute | solution.py:260
  85.7 9.4 %collective-permute-start.11 = (bf16[4,256,256]{2,1,0:T(8,128)(2,1)}, bf16[4,256,256]{2,1,0:T(8,128)(2,1)S(1)}, u32[]{:S(2)}, u32[]{:S(2)}) collective-permute-start(bf16[4,256,256]{2,1,0:T(8,128)(2,1)} %pad_maximum_fusion.2.rest_4_), channel_id=1, source_target_pairs={{0,64},{2,66},{4,68},{6,70},{8,72},{10,74},{12,76},{14,78},{16,80}... | collective-permute-start | bytes 1572872 | tf_op jit(solution)/shard_map/ppermute | solution.py:260
  88.8 6.3 %copy-start.1 = (bf16[4,256,256]{2,1,0:T(8,128)(2,1)S(1)}, bf16[4,256,256]{2,1,0:T(8,128)(2,1)}, u32[]{:S(2)}) copy-start(bf16[4,256,256]{2,1,0:T(8,128)(2,1)} %pad_maximum_fusion.2.rest_4_) | copy-start | bytes 1572868
  114.6 1.0 copy-start.2
  115.7 0.8 copy-start.4
  116.5 0.8 copy-start.6
  117.3 0.8 copy-start.8
  118.1 0.8 copy-start.9
  118.9 0.8 copy-start.10
  119.6 0.8 copy-start.11
  120.4 0.8 copy-start.12
  121.3 0.8 copy-start.13
  122.1 39.9 %copy-start.7 = (bf16[4,256,256]{2,1,0:T(8,128)(2,1)S(1)}, bf16[4,256,256]{2,1,0:T(8,128)(2,1)}, u32[]{:S(2)}) copy-start(bf16[4,256,256]{2,1,0:T(8,128)(2,1)} %copy-done.6) | copy-start | bytes 1572868
  122.1 47.9 %copy-start.5 = (bf16[4,256,256]{2,1,0:T(8,128)(2,1)S(1)}, bf16[4,256,256]{2,1,0:T(8,128)(2,1)}, u32[]{:S(2)}) copy-start(bf16[4,256,256]{2,1,0:T(8,128)(2,1)} %copy-done.4) | copy-start | bytes 1572868
  123.3 21.9 %collective-permute-start.14 = (bf16[4,256,256]{2,1,0:T(8,128)(2,1)}, bf16[4,256,256]{2,1,0:T(8,128)(2,1)S(1)}, u32[]{:S(2)}, u32[]{:S(2)}) collective-permute-start(bf16[4,256,256]{2,1,0:T(8,128)(2,1)} %copy-done.13), channel_id=1, source_target_pairs={{0,6},{2,0},{4,2},{6,4},{8,14},{10,8},{12,10},{14,12},{16,22},{18,... | collective-permute-start | bytes 1572872 | tf_op jit(solution)/shard_map/ppermute | solution.py:307
  127.0 34.9 %collective-permute-start.15 = (bf16[4,256,256]{2,1,0:T(8,128)(2,1)}, bf16[4,256,256]{2,1,0:T(8,128)(2,1)}, u32[]{:S(2)}, u32[]{:S(2)}) collective-permute-start(bf16[4,256,256]{2,1,0:T(8,128)(2,1)} %copy-done.12), channel_id=1, source_target_pairs={{0,4},{2,6},{4,0},{6,2},{8,12},{10,14},{12,8},{14,10},{16,20},{18,... | collective-permute-start | bytes 1572872 | tf_op jit(solution)/shard_map/ppermute | solution.py:307
  127.0 34.9 %collective-permute-start.16 = (bf16[4,256,256]{2,1,0:T(8,128)(2,1)}, bf16[4,256,256]{2,1,0:T(8,128)(2,1)}, u32[]{:S(2)}, u32[]{:S(2)}) collective-permute-start(bf16[4,256,256]{2,1,0:T(8,128)(2,1)} %copy-done.11), channel_id=1, source_target_pairs={{0,2},{2,4},{4,6},{6,0},{8,10},{10,12},{12,14},{14,8},{16,18},{18,... | collective-permute-start | bytes 1572872 | tf_op jit(solution)/shard_map/ppermute | solution.py:307
  128.0 37.5 %collective-permute-start.20 = (bf16[4,256,256]{2,1,0:T(8,128)(2,1)}, bf16[4,256,256]{2,1,0:T(8,128)(2,1)S(1)}, u32[]{:S(2)}, u32[]{:S(2)}) collective-permute-start(bf16[4,256,256]{2,1,0:T(8,128)(2,1)} %copy-done.10), channel_id=1, source_target_pairs={{0,192},{2,194},{4,196},{6,198},{8,200},{10,202},{12,204},{14,206}... | collective-permute-start | bytes 1572872 | tf_op jit(solution)/shard_map/ppermute | solution.py:308
  130.3 39.7 %collective-permute-start.21 = (bf16[4,256,256]{2,1,0:T(8,128)(2,1)}, bf16[4,256,256]{2,1,0:T(8,128)(2,1)}, u32[]{:S(2)}, u32[]{:S(2)}) collective-permute-start(bf16[4,256,256]{2,1,0:T(8,128)(2,1)} %copy-done.9), channel_id=1, source_target_pairs={{0,128},{2,130},{4,132},{6,134},{8,136},{10,138},{12,140},{14,142}... | collective-permute-start | bytes 1572872 | tf_op jit(solution)/shard_map/ppermute | solution.py:308
  145.3 20.1 %copy-start.19 = (bf16[4,256,256]{2,1,0:T(8,128)(2,1)}, bf16[4,256,256]{2,1,0:T(8,128)(2,1)S(1)}, u32[]{:S(2)}) copy-start(bf16[4,256,256]{2,1,0:T(8,128)(2,1)S(1)} %collective-permute-done.14) | copy-start | bytes 1572868
  145.3 24.7 %collective-permute-start.22 = (bf16[4,256,256]{2,1,0:T(8,128)(2,1)}, bf16[4,256,256]{2,1,0:T(8,128)(2,1)}, u32[]{:S(2)}, u32[]{:S(2)}) collective-permute-start(bf16[4,256,256]{2,1,0:T(8,128)(2,1)} %copy-done.8), channel_id=1, source_target_pairs={{0,64},{2,66},{4,68},{6,70},{8,72},{10,74},{12,76},{14,78},{16,80}... | collective-permute-start | bytes 1572872 | tf_op jit(solution)/shard_map/ppermute | solution.py:308
  148.2 34.9 %all-to-all-start.2 = ((bf16[128,8,256]{2,1,0:T(8,128)(2,1)}), bf16[128,8,256]{2,1,0:T(8,128)(2,1)S(1)}, u32[]{:S(2)}, u32[]{:S(2)}) async-start(bf16[128,8,256]{2,1,0:T(8,128)(2,1)} %broadcast_in_dim.18), calls=%async_computation.2 | async-start | bytes 1048576 | tf_op jit(solution)/shard_map/all_to_all | solution.py:309
  163.3 10.9 %collective-permute-start.17 = (bf16[256,256]{1,0:T(8,128)(2,1)S(1)}, bf16[256,256]{1,0:T(8,128)(2,1)S(1)}, u32[]{:S(2)}, u32[]{:S(2)}) collective-permute-start(bf16[256,256]{1,0:T(8,128)(2,1)S(1)} %get-tuple-element.57), channel_id=1, source_target_pairs={{0,192},{2,194},{4,196},{6,198},{8,200},{10,202},{12,204},{14,206}... | collective-permute-start | bytes 393224 | tf_op jit(solution)/shard_map/ppermute | solution.py:315
  164.2 12.4 %collective-permute-start.19 = (bf16[256,256]{1,0:T(8,128)(2,1)S(1)}, bf16[256,256]{1,0:T(8,128)(2,1)S(1)}, u32[]{:S(2)}, u32[]{:S(2)}) collective-permute-start(bf16[256,256]{1,0:T(8,128)(2,1)S(1)} %get-tuple-element.58), channel_id=1, source_target_pairs={{0,64},{2,66},{4,68},{6,70},{8,72},{10,74},{12,76},{14,78},{16,80}... | collective-permute-start | bytes 393224 | tf_op jit(solution)/shard_map/ppermute | solution.py:315
  165.4 0.8 copy-start.18
  166.2 33.9 %copy-start.3 = (f32[1024,256]{1,0:T(8,128)S(1)}, f32[1024,256]{1,0:T(8,128)}, u32[]{:S(2)}) copy-start(f32[1024,256]{1,0:T(8,128)} %copy-done.2) | copy-start | bytes 3145732
  166.2 10.3 %collective-permute-start.18 = (bf16[256,256]{1,0:T(8,128)(2,1)S(1)}, bf16[256,256]{1,0:T(8,128)(2,1)S(1)}, u32[]{:S(2)}, u32[]{:S(2)}) collective-permute-start(bf16[256,256]{1,0:T(8,128)(2,1)S(1)} %get-tuple-element.59), channel_id=1, source_target_pairs={{0,128},{2,130},{4,132},{6,134},{8,136},{10,138},{12,140},{14,142}... | collective-permute-start | bytes 393224 | tf_op jit(solution)/shard_map/ppermute | solution.py:315
  171.5 6.3 %collective-permute-start.23 = (bf16[256,256]{1,0:T(8,128)(2,1)S(1)}, bf16[256,256]{1,0:T(8,128)(2,1)S(1)}, u32[]{:S(2)}, u32[]{:S(2)}) collective-permute-start(bf16[256,256]{1,0:T(8,128)(2,1)S(1)} %get-tuple-element.60), channel_id=1, source_target_pairs={{0,6},{2,0},{4,2},{6,4},{8,14},{10,8},{12,10},{14,12},{16,22},{18,... | collective-permute-start | bytes 393224 | tf_op jit(solution)/shard_map/ppermute | solution.py:318
  174.3 7.6 %collective-permute-start.25 = (bf16[256,256]{1,0:T(8,128)(2,1)S(1)}, bf16[256,256]{1,0:T(8,128)(2,1)S(1)}, u32[]{:S(2)}, u32[]{:S(2)}) collective-permute-start(bf16[256,256]{1,0:T(8,128)(2,1)S(1)} %get-tuple-element.61), channel_id=1, source_target_pairs={{0,2},{2,4},{4,6},{6,0},{8,10},{10,12},{12,14},{14,8},{16,18},{18,... | collective-permute-start | bytes 393224 | tf_op jit(solution)/shard_map/ppermute | solution.py:318
  174.3 7.6 %collective-permute-start.24 = (bf16[256,256]{1,0:T(8,128)(2,1)S(1)}, bf16[256,256]{1,0:T(8,128)(2,1)S(1)}, u32[]{:S(2)}, u32[]{:S(2)}) collective-permute-start(bf16[256,256]{1,0:T(8,128)(2,1)S(1)} %get-tuple-element.62), channel_id=1, source_target_pairs={{0,4},{2,6},{4,0},{6,2},{8,12},{10,14},{12,8},{14,10},{16,20},{18,... | collective-permute-start | bytes 393224 | tf_op jit(solution)/shard_map/ppermute | solution.py:318

commit v4 on v3

--- a/solution.py
+++ b/solution.py
@@ -230,30 +230,28 @@
         return (part / degree[:, None].astype(jnp.float32)).astype(jnp.bfloat16)
 
     shared = scale(both(grad_out[:hub], pre_act[:hub]), degrees[:hub])
+    copies = jnp.broadcast_to(shared, (nz, *shared.shape))
     column = lax.all_to_all(
-        jnp.broadcast_to(shared, (nz, *shared.shape)),
-        "dom",
-        split_axis=0,
-        concat_axis=0,
-        axis_index_groups=columns(),
-        tiled=True,
-    )
-    column, grad_out, pre_act = lax.optimization_barrier((column, grad_out, pre_act))
-
-    low = column[:deep].reshape(deep * hub, width)
-    high = column[deep:].reshape(deep * hub, width)
-    low_set = jnp.stack([low] + [lax.ppermute(low, "dom", ring("x", k)) for k in range(1, nx)])
-    high_set = jnp.stack([high] + [lax.ppermute(high, "dom", ring("y", k)) for k in range(1, ny)])
+        copies, "dom", split_axis=0, concat_axis=0, axis_index_groups=columns(), tiled=True
+    )
 
     block_cols = both(grad_out, pre_act)
-    scaled = scale(block_cols, degrees)
-    self_part = lax.dot_general(block_cols, w_self, contract, preferred_element_type=jnp.float32)
     grad_self = lax.dot_general(features, block_cols, over_rows, preferred_element_type=jnp.float32)
     grad_neigh = lax.dot_general(neigh_mean, block_cols, over_rows, preferred_element_type=jnp.float32)
     pay = jnp.concatenate(
-        [grad_self[:, :width], grad_self[:, width:], grad_neigh[:, :width], grad_neigh[:, width:]], axis=0
+        [grad_self[:, :width], grad_self[:, width:], grad_neigh[:, :width], grad_neigh[:, width:]],
+        axis=0,
     ).astype(jnp.bfloat16)
     tail = pay.shape[0] // parts
+
+    low = column[:deep].reshape(deep * hub, width)
+    high = column[deep:].reshape(deep * hub, width)
+    low_far = [lax.ppermute(low, "dom", ring("x", k)) for k in range(1, nx)]
+    high_far = [lax.ppermute(high, "dom", ring("y", k)) for k in range(1, ny)]
+    scaled = scale(block_cols, degrees)
+    self_part = lax.dot_general(block_cols, w_self, contract, preferred_element_type=jnp.float32)
+    low_set = jnp.stack([low] + low_far)
+    high_set = jnp.stack([high] + high_far)
 
     low_set, high_set, pay = lax.optimization_barrier((low_set, high_set, pay))
     low_got = [low_set] + [lax.ppermute(low_set, "dom", ring("y", k)) for k in range(1, ny)]
@@ -288,11 +286,11 @@
     ).astype(jnp.int32)
 
     lanes = local * halves
-    low_type = jax.ShapeDtypeStruct(low_set.shape, jnp.bfloat16)
-    high_type = jax.ShapeDtypeStruct(high_set.shape, jnp.bfloat16)
+    low_type = pltpu.HBM(low_set.shape, jnp.bfloat16)
+    high_type = pltpu.HBM(high_set.shape, jnp.bfloat16)
     results = pl.pallas_call(
         functools.partial(edge_kernel, GRID, slots),
-        out_shape=[jax.ShapeDtypeStruct((masters, width), jnp.float32)] + [low_type] * ny + [high_type] * nx,
+        out_shape=[pltpu.HBM((masters, width), jnp.float32)] + [low_type] * ny + [high_type] * nx,
         in_specs=[SMEM] * 3 + [VMEM] * (4 + nx + ny),
         out_specs=[VMEM] * (1 + nx + ny),
         scratch_shapes=[pltpu.VMEM((lanes, LANES), jnp.float32)]

time: 203 us -> 188 us (0.926)
  blocking collectives: 37.5 us -> 17 us
  waiting for transfers between devices: 46 us -> 53.9 us
  local copies, waits for them, and re-layouts: 10.2 us -> 2.86 us
  starting transfers between devices: 66.2 us -> 69.8 us
    all_to_all x1 -> x0, blocking collectives: 20.5 us -> none  [on_device(): lax.all_to_all(jnp.broadcast_to(shared, (nz, *shared.shape)), 'dom', spli...]
    all_to_all x0 -> x1, waiting for transfers between devices: none -> 10.4 us  [on_device(): lax.all_to_all(copies, 'dom', split_axis=0, concat_axis=0, axis_index_gro...]
    all_to_all x0 -> x1, starting transfers between devices: none -> 8.47 us  [on_device(): lax.all_to_all(copies, 'dom', split_axis=0, concat_axis=0, axis_index_gro...]
    unnamed x54 -> x36, local copies, waits for them, and re-layouts: 8.89 us -> 0.88 us
    all_to_all x1, starting transfers between devices: 10.5 us -> 6.87 us  [on_device(): lax.all_to_all(pay.reshape(parts, tail, width), 'dom', split_axis=0, conc...]
  transfers between devices with their start and end apart: 28 -> 29, of which waited for: 10 -> 10; matrix products, arithmetic and copies ran while one was open for 5% -> 7% of each run, Pallas kernels for 11% -> 13%
where the time goes in v4:
time: 188 us
  starting transfers between devices  69.8 us (37%)
  waiting for transfers between devices  53.9 us (29%)
  Pallas kernels  26.8 us (14%)
  blocking collectives  17 us (9%)
  other arithmetic  11.4 us (6%)
  matrix products  4.25 us (2%)
  local copies, waits for them, and re-layouts  2.86 us (2%)
    pallas_call x1, Pallas kernels, on_device(): pl.pallas_call(functools.partial(edge_kernel, GRID, slots), out_shape=[pl...  21.5 us
    ppermute x3, waiting for transfers between devices, on_device(): lax.ppermute(low_set, 'dom', ring('y', k))  18 us
    all_to_all x1, blocking collectives, on_device(): lax.all_to_all(column_sum.reshape(nz, hub, width), 'dom', split_axis=0, c...  17 us
    all_to_all x1, starting transfers between devices, on_device(): lax.all_to_all(jnp.broadcast_to(share, (parts, *share.shape)), 'dom', spl...  13.8 us
    ppermute x3, waiting for transfers between devices, on_device(): lax.ppermute(low_back[k], 'dom', ring('y', -k))  12.9 us
    all_to_all x1, waiting for transfers between devices, on_device(): lax.all_to_all(copies, 'dom', split_axis=0, concat_axis=0, axis_index_gro...  10.4 us
    all_to_all x1, starting transfers between devices, on_device(): lax.all_to_all(copies, 'dom', split_axis=0, concat_axis=0, axis_index_gro...  8.47 us
    all_to_all x1, starting transfers between devices, on_device(): lax.all_to_all(pay.reshape(parts, tail, width), 'dom', split_axis=0, conc...  6.87 us
  transfers between devices with their start and end apart: 29, of which 10 were waited for; matrix products, arithmetic and copies ran while one was open for 7% of the time, Pallas kernels for 13%

profile of v4, /device:TPU:2, one launch (start us, length us, event | category | flops | bytes accessed | tf_op | source)
XLA Modules:
  0.0 187.8 jit_solution(12628288128054863362)
XLA Ops:
  0.7 0.8 select_convert_fusion.1
  1.5 0.1 collective-permute-start.1
  1.6 0.7 slice_convert_fusion
  2.3 0.5 collective-permute-done.1
  2.8 1.2 fusion.3
  4.0 0.7 broadcast_in_dim.17
  4.7 8.5 %all-to-all-start = ((bf16[8,64,256]{2,1,0:T(8,128)(2,1)}), bf16[8,64,256]{2,1,0:T(8,128)(2,1)S(1)}, u32[]{:S(2)}, u32[]{:S(2)}) async-start(bf16[8,64,256]{2,1,0:T(8,128)(2,1)} %broadcast_in_dim.17), calls=%async_computation | async-start | bytes 524288 | tf_op jit(solution)/shard_map/all_to_all | solution.py:234
  13.2 1.4 select_convert_fusion
  14.5 0.1 collective-permute-start
  14.7 0.1 add.180
  14.8 0.1 reshape.91
  14.9 0.1 reshape.92
  15.0 10.4 %all-to-all-done = bf16[8,64,256]{2,1,0:T(8,128)(2,1)S(1)} async-done(((bf16[8,64,256]{2,1,0:T(8,128)(2,1)}), bf16[8,64,256]{2,1,0:T(8,128)(2,1)S(1)}, u32[]{:S(2)}, u32[]{:S(2)}) %all-to-all-start) | async-done | bytes 262176 | tf_op jit(solution)/shard_map/all_to_all | solution.py:234
  25.4 0.6 collective-permute-start.4
  26.0 2.4 %collective-permute-start.3 = (bf16[256,256]{1,0:T(8,128)(2,1)S(1)}, bf16[256,256]{1,0:T(8,128)(2,1)S(1)}, u32[]{:S(2)}, u32[]{:S(2)}) collective-permute-start(bf16[256,256]{1,0:T(8,128)(2,1)S(1)} %bitcast.58), channel_id=1, source_target_pairs={{0,128},{2,130},{4,132},{6,134},{8,136},{10,138},{12,140},{14,142}... | collective-permute-start | bytes 393224 | tf_op jit(solution)/shard_map/ppermute | solution.py:249
  28.4 1.8 collective-permute-start.2
  30.2 3.0 %collective-permute-start.7 = (bf16[256,256]{1,0:T(8,128)(2,1)S(1)}, bf16[256,256]{1,0:T(8,128)(2,1)S(1)}, u32[]{:S(2)}, u32[]{:S(2)}) collective-permute-start(bf16[256,256]{1,0:T(8,128)(2,1)S(1)} %bitcast.53), channel_id=1, source_target_pairs={{0,6},{2,0},{4,2},{6,4},{8,14},{10,8},{12,10},{14,12},{16,22},{18,... | collective-permute-start | bytes 393224 | tf_op jit(solution)/shard_map/ppermute | solution.py:250
  33.2 0.6 collective-permute-start.6
  33.9 0.1 broadcast_select_fusion.1
  34.0 0.5 fusion.1
  34.5 0.5 fusion.2
  35.1 1.0 collective-permute-start.5
  36.1 0.8 pad_maximum_fusion.3
  37.0 0.2 collective-permute-done.7
  37.2 2.5 %collective-permute-done.6 = bf16[256,256]{1,0:T(8,128)(2,1)S(1)} collective-permute-done((bf16[256,256]{1,0:T(8,128)(2,1)S(1)}, bf16[256,256]{1,0:T(8,128)(2,1)S(1)}, u32[]{:S(2)}, u32[]{:S(2)}) %collective-permute-start.6) | collective-permute-done | bytes 131104 | tf_op jit(solution)/shard_map/ppermute | solution.py:250
  39.7 1.6 collective-permute-done.5
  41.3 0.9 pad_maximum_fusion.2.rest_4_
  42.2 6.9 %all-to-all-start.1 = ((bf16[128,8,256]{2,1,0:T(8,128)(2,1)}), bf16[128,8,256]{2,1,0:T(8,128)(2,1)}, u32[]{:S(2)}, u32[]{:S(2)}) async-start(bf16[128,8,256]{2,1,0:T(8,128)(2,1)} %bitcast.14), calls=%async_computation.1 | async-start | bytes 1048576 | tf_op jit(solution)/shard_map/all_to_all | solution.py:259
  49.1 2.8 %collective-permute-start.10 = (bf16[4,256,256]{2,1,0:T(8,128)(2,1)S(1)}, bf16[4,256,256]{2,1,0:T(8,128)(2,1)}, u32[]{:S(2)}, u32[]{:S(2)}) collective-permute-start(bf16[4,256,256]{2,1,0:T(8,128)(2,1)S(1)} %pad_maximum_fusion.1.rest_0_), channel_id=1, source_target_pairs={{0,6},{2,0},{4,2},{6,4},{8,14},{10,8},{12,10},{14,12},{16,22},{18,... | collective-permute-start | bytes 1572872 | tf_op jit(solution)/shard_map/ppermute | solution.py:257
  52.5 3.3 %picks.1.pick_ref = bf16[32,128,256]{2,1,0:T(8,128)(2,1)S(1)} custom-call(s32[32,128]{1,0:T(8,128)S(1)} %broadcast_add_fusion.spot_ref), custom_call_target="tpu_custom_call" | custom-call | tf_op jit(solution)/shard_map/picks/pallas_call | solution.py:267
  55.9 0.1 pad_add_fusion.place_ref
  56.1 0.9 collective-permute-start.9
  57.0 0.9 collective-permute-start.8
  57.9 0.5 collective-permute-start.13
  58.3 2.7 %collective-permute-start.12 = (bf16[4,256,256]{2,1,0:T(8,128)(2,1)}, bf16[4,256,256]{2,1,0:T(8,128)(2,1)S(1)}, u32[]{:S(2)}, u32[]{:S(2)}) collective-permute-start(bf16[4,256,256]{2,1,0:T(8,128)(2,1)} %pad_maximum_fusion.2.rest_4_), channel_id=1, source_target_pairs={{0,128},{2,130},{4,132},{6,134},{8,136},{10,138},{12,140},{14,142}... | collective-permute-start | bytes 1572872 | tf_op jit(solution)/shard_map/ppermute | solution.py:258
  61.0 16.0 %collective-permute-done.10.rest_3_ = bf16[4,256,256]{2,1,0:T(8,128)(2,1)} collective-permute-done((bf16[4,256,256]{2,1,0:T(8,128)(2,1)S(1)}, bf16[4,256,256]{2,1,0:T(8,128)(2,1)}, u32[]{:S(2)}, u32[]{:S(2)}) %collective-permute-start.10) | collective-permute-done | bytes 524320 | tf_op jit(solution)/shard_map/ppermute | solution.py:257
  77.0 1.4 collective-permute-start.11
  78.5 1.7 fusion.35.self_ref
  80.2 0.5 fusion.own_ref
  80.6 2.0 %collective-permute-done.8.rest_1_ = bf16[4,256,256]{2,1,0:T(8,128)(2,1)S(1)} collective-permute-done((bf16[4,256,256]{2,1,0:T(8,128)(2,1)S(1)}, bf16[4,256,256]{2,1,0:T(8,128)(2,1)S(1)}, u32[]{:S(2)}, u32[]{:S(2)}) %collective-permute-start.8) | collective-permute-done | bytes 524320 | tf_op jit(solution)/shard_map/ppermute | solution.py:257
  82.7 3.8 %collective-permute-done.11.rest_5_ = bf16[4,256,256]{2,1,0:T(8,128)(2,1)S(1)} collective-permute-done((bf16[4,256,256]{2,1,0:T(8,128)(2,1)}, bf16[4,256,256]{2,1,0:T(8,128)(2,1)S(1)}, u32[]{:S(2)}, u32[]{:S(2)}) %collective-permute-start.11) | collective-permute-done | bytes 524320 | tf_op jit(solution)/shard_map/ppermute | solution.py:258
  86.4 21.5 %edges.1 = (f32[1024,256]{1,0:T(8,128)}, bf16[4,256,256]{2,1,0:T(8,128)(2,1)}, bf16[4,256,256]{2,1,0:T(8,128)(2,1)}, bf16[4,256,256]{2,1,0:T(8,128)(2,1)}, bf16[...) custom-call(s32[8192]{0:T(1024)S(1)} %get-tuple-element.71.from_ref,, ...), custom_call_target="tpu_custom_call" | custom-call | tf_op jit(solution)/shard_map/edges/pallas_call | solution.py:291
  107.9 1.3 reduce_sum.12
  109.2 3.7 %collective-permute-start.14 = (bf16[4,256,256]{2,1,0:T(8,128)(2,1)}, bf16[4,256,256]{2,1,0:T(8,128)(2,1)S(1)}, u32[]{:S(2)}, u32[]{:S(2)}) collective-permute-start(bf16[4,256,256]{2,1,0:T(8,128)(2,1)} %get-tuple-element.39), channel_id=1, source_target_pairs={{0,6},{2,0},{4,2},{6,4},{8,14},{10,8},{12,10},{14,12},{16,22},{18,... | collective-permute-start | bytes 1572872 | tf_op jit(solution)/shard_map/ppermute | solution.py:305
  112.8 1.0 collective-permute-start.16
  113.8 2.2 %collective-permute-start.20 = (bf16[4,256,256]{2,1,0:T(8,128)(2,1)}, bf16[4,256,256]{2,1,0:T(8,128)(2,1)S(1)}, u32[]{:S(2)}, u32[]{:S(2)}) collective-permute-start(bf16[4,256,256]{2,1,0:T(8,128)(2,1)} %get-tuple-element.43), channel_id=1, source_target_pairs={{0,192},{2,194},{4,196},{6,198},{8,200},{10,202},{12,204},{14,206}... | collective-permute-start | bytes 1572872 | tf_op jit(solution)/shard_map/ppermute | solution.py:306
  116.0 2.2 %collective-permute-start.21 = (bf16[4,256,256]{2,1,0:T(8,128)(2,1)}, bf16[4,256,256]{2,1,0:T(8,128)(2,1)}, u32[]{:S(2)}, u32[]{:S(2)}) collective-permute-start(bf16[4,256,256]{2,1,0:T(8,128)(2,1)} %get-tuple-element.44), channel_id=1, source_target_pairs={{0,128},{2,130},{4,132},{6,134},{8,136},{10,138},{12,140},{14,142}... | collective-permute-start | bytes 1572872 | tf_op jit(solution)/shard_map/ppermute | solution.py:306
  118.1 12.9 %collective-permute-done.14 = bf16[4,256,256]{2,1,0:T(8,128)(2,1)S(1)} collective-permute-done((bf16[4,256,256]{2,1,0:T(8,128)(2,1)}, bf16[4,256,256]{2,1,0:T(8,128)(2,1)S(1)}, u32[]{:S(2)}, u32[]{:S(2)}) %collective-permute-start.14) | collective-permute-done | bytes 524320 | tf_op jit(solution)/shard_map/ppermute | solution.py:305
  131.0 2.0 %collective-permute-start.22 = (bf16[4,256,256]{2,1,0:T(8,128)(2,1)}, bf16[4,256,256]{2,1,0:T(8,128)(2,1)}, u32[]{:S(2)}, u32[]{:S(2)}) collective-permute-start(bf16[4,256,256]{2,1,0:T(8,128)(2,1)} %get-tuple-element.45), channel_id=1, source_target_pairs={{0,64},{2,66},{4,68},{6,70},{8,72},{10,74},{12,76},{14,78},{16,80}... | collective-permute-start | bytes 1572872 | tf_op jit(solution)/shard_map/ppermute | solution.py:306
  133.0 0.8 broadcast_in_dim.18
  133.8 13.8 %all-to-all-start.2 = ((bf16[128,8,256]{2,1,0:T(8,128)(2,1)}), bf16[128,8,256]{2,1,0:T(8,128)(2,1)S(1)}, u32[]{:S(2)}, u32[]{:S(2)}) async-start(bf16[128,8,256]{2,1,0:T(8,128)(2,1)} %broadcast_in_dim.18), calls=%async_computation.2 | async-start | bytes 1048576 | tf_op jit(solution)/shard_map/all_to_all | solution.py:307
  147.6 1.4 fusion.10
  149.1 0.9 collective-permute-start.17
  149.9 1.2 collective-permute-start.19
  151.2 0.8 copy-done.9
  152.0 3.7 %collective-permute-start.18 = (bf16[256,256]{1,0:T(8,128)(2,1)S(1)}, bf16[256,256]{1,0:T(8,128)(2,1)S(1)}, u32[]{:S(2)}, u32[]{:S(2)}) collective-permute-start(bf16[256,256]{1,0:T(8,128)(2,1)S(1)} %get-tuple-element.53), channel_id=1, source_target_pairs={{0,128},{2,130},{4,132},{6,134},{8,136},{10,138},{12,140},{14,142}... | collective-permute-start | bytes 393224 | tf_op jit(solution)/shard_map/ppermute | solution.py:313
  155.7 1.5 fusion.13
  157.2 2.8 %collective-permute-start.23 = (bf16[256,256]{1,0:T(8,128)(2,1)S(1)}, bf16[256,256]{1,0:T(8,128)(2,1)S(1)}, u32[]{:S(2)}, u32[]{:S(2)}) collective-permute-start(bf16[256,256]{1,0:T(8,128)(2,1)S(1)} %get-tuple-element.54), channel_id=1, source_target_pairs={{0,6},{2,0},{4,2},{6,4},{8,14},{10,8},{12,10},{14,12},{16,22},{18,... | collective-permute-start | bytes 393224 | tf_op jit(solution)/shard_map/ppermute | solution.py:316
  160.0 2.3 %collective-permute-start.24 = (bf16[256,256]{1,0:T(8,128)(2,1)S(1)}, bf16[256,256]{1,0:T(8,128)(2,1)S(1)}, u32[]{:S(2)}, u32[]{:S(2)}) collective-permute-start(bf16[256,256]{1,0:T(8,128)(2,1)S(1)} %get-tuple-element.56), channel_id=1, source_target_pairs={{0,4},{2,6},{4,0},{6,2},{8,12},{10,14},{12,8},{14,10},{16,20},{18,... | collective-permute-start | bytes 393224 | tf_op jit(solution)/shard_map/ppermute | solution.py:316
  162.3 1.2 fusion.9
  163.5 4.1 %collective-permute-done.25 = bf16[256,256]{1,0:T(8,128)(2,1)S(1)} collective-permute-done((bf16[256,256]{1,0:T(8,128)(2,1)S(1)}, bf16[256,256]{1,0:T(8,128)(2,1)S(1)}, u32[]{:S(2)}, u32[]{:S(2)}) %collective-permute-start.25) | collective-permute-done | bytes 131104 | tf_op jit(solution)/shard_map/ppermute | solution.py:316
  167.6 1.2 fusion.6
  168.8 17.0 %all_to_all.20.home_ref = bf16[8,64,256]{2,1,0:T(8,128)(2,1)S(1)} all-to-all(bf16[8,64,256]{2,1,0:T(8,128)(2,1)S(1)} %bitcast.52), channel_id=1, replica_groups={{0,8,16,24,32,40,48,56},{2,10,18,26,34,42,50,58},{4,12,20,28,36,44,52,6..., dimensions={0} | all-to-all | bytes 524288 | tf_op jit(solution)/shard_map/all_to_all | solution.py:320
  185.8 2.0 %final.1 = (bf16[1024,256]{1,0:T(8,128)(2,1)}, f32[256,512]{1,0:T(8,128)}, f32[256,512]{1,0:T(8,128)}) custom-call(bf16[8,64,256]{2,1,0:T(8,128)(2,1)S(1)} %all_to_all.20.home_ref, f32[1024,256]{1,0:T(8,128)S(1)} %copy-done.2, bf16[128,8,256]{2,1,0:T(8,128)(2,1)S(1)} %all-to-all-done.2.weight_ref), custom_call_target="tpu_custom_call" | custom-call | tf_op jit(solution)/shard_map/final/pallas_call | solution.py:328
  (68 shorter events, 0.5 us)
Async XLA Ops:
  0.6 33.4 %copy-start = (bf16[1024,256]{1,0:T(8,128)(2,1)S(1)}, bf16[1024,256]{1,0:T(8,128)(2,1)}, u32[]{:S(2)}) copy-start(bf16[1024,256]{1,0:T(8,128)(2,1)} %param.11) | copy-start | bytes 1572868
  0.6 14.1 %copy-start.13 = (s32[4096]{0:T(1024)S(1)}, s32[4096]{0:T(1024)}, u32[]{:S(2)}) copy-start(s32[4096]{0:T(1024)} %param.20) | copy-start | bytes 49156
  1.5 1.3 collective-permute-start.1
  4.7 20.7 %all-to-all-start = ((bf16[8,64,256]{2,1,0:T(8,128)(2,1)}), bf16[8,64,256]{2,1,0:T(8,128)(2,1)S(1)}, u32[]{:S(2)}, u32[]{:S(2)}) async-start(bf16[8,64,256]{2,1,0:T(8,128)(2,1)} %broadcast_in_dim.17), calls=%async_computation | async-start | bytes 524288 | tf_op jit(solution)/shard_map/all_to_all | solution.py:234
  14.5 18.7 %collective-permute-start = (bf16[1024,256]{1,0:T(8,128)(2,1)S(1)}, bf16[1024,256]{1,0:T(8,128)(2,1)S(1)}, u32[]{:S(2)}, u32[]{:S(2)}) collective-permute-start(bf16[1024,256]{1,0:T(8,128)(2,1)S(1)} %select_convert_fusion), channel_id=1, source_target_pairs={{0,1},{1,0},{2,3},{3,2},{4,5},{5,4},{6,7},{7,6},{8,9},{9,8},{10,11... | collective-permute-start | bytes 1572872 | tf_op jit(solution)/shard_map/ppermute | solution.py:225
  25.4 9.7 %collective-permute-start.4 = (bf16[256,256]{1,0:T(8,128)(2,1)S(1)}, bf16[256,256]{1,0:T(8,128)(2,1)S(1)}, u32[]{:S(2)}, u32[]{:S(2)}) collective-permute-start(bf16[256,256]{1,0:T(8,128)(2,1)S(1)} %bitcast.57), channel_id=1, source_target_pairs={{0,192},{2,194},{4,196},{6,198},{8,200},{10,202},{12,204},{14,206}... | collective-permute-start | bytes 393224 | tf_op jit(solution)/shard_map/ppermute | solution.py:249
  26.0 10.9 %collective-permute-start.3 = (bf16[256,256]{1,0:T(8,128)(2,1)S(1)}, bf16[256,256]{1,0:T(8,128)(2,1)S(1)}, u32[]{:S(2)}, u32[]{:S(2)}) collective-permute-start(bf16[256,256]{1,0:T(8,128)(2,1)S(1)} %bitcast.58), channel_id=1, source_target_pairs={{0,128},{2,130},{4,132},{6,134},{8,136},{10,138},{12,140},{14,142}... | collective-permute-start | bytes 393224 | tf_op jit(solution)/shard_map/ppermute | solution.py:249
  28.4 8.5 %collective-permute-start.2 = (bf16[256,256]{1,0:T(8,128)(2,1)S(1)}, bf16[256,256]{1,0:T(8,128)(2,1)S(1)}, u32[]{:S(2)}, u32[]{:S(2)}) collective-permute-start(bf16[256,256]{1,0:T(8,128)(2,1)S(1)} %bitcast.59), channel_id=1, source_target_pairs={{0,64},{2,66},{4,68},{6,70},{8,72},{10,74},{12,76},{14,78},{16,80}... | collective-permute-start | bytes 393224 | tf_op jit(solution)/shard_map/ppermute | solution.py:249
  30.2 4.3 %copy-start.15 = (bf16[1024,256]{1,0:T(8,128)(2,1)S(1)}, bf16[1024,256]{1,0:T(8,128)(2,1)}, u32[]{:S(2)}) copy-start(bf16[1024,256]{1,0:T(8,128)(2,1)} %param.14) | copy-start | bytes 1572868
  30.2 7.0 %collective-permute-start.7 = (bf16[256,256]{1,0:T(8,128)(2,1)S(1)}, bf16[256,256]{1,0:T(8,128)(2,1)S(1)}, u32[]{:S(2)}, u32[]{:S(2)}) collective-permute-start(bf16[256,256]{1,0:T(8,128)(2,1)S(1)} %bitcast.53), channel_id=1, source_target_pairs={{0,6},{2,0},{4,2},{6,4},{8,14},{10,8},{12,10},{14,12},{16,22},{18,... | collective-permute-start | bytes 393224 | tf_op jit(solution)/shard_map/ppermute | solution.py:250
  33.2 6.5 %collective-permute-start.6 = (bf16[256,256]{1,0:T(8,128)(2,1)S(1)}, bf16[256,256]{1,0:T(8,128)(2,1)S(1)}, u32[]{:S(2)}, u32[]{:S(2)}) collective-permute-start(bf16[256,256]{1,0:T(8,128)(2,1)S(1)} %bitcast.54), channel_id=1, source_target_pairs={{0,4},{2,6},{4,0},{6,2},{8,12},{10,14},{12,8},{14,10},{16,20},{18,... | collective-permute-start | bytes 393224 | tf_op jit(solution)/shard_map/ppermute | solution.py:250
  34.0 1.0 copy-start.3
  34.0 1.0 copy-start.5
  35.1 6.3 %collective-permute-start.5 = (bf16[256,256]{1,0:T(8,128)(2,1)S(1)}, bf16[256,256]{1,0:T(8,128)(2,1)S(1)}, u32[]{:S(2)}, u32[]{:S(2)}) collective-permute-start(bf16[256,256]{1,0:T(8,128)(2,1)S(1)} %bitcast.55), channel_id=1, source_target_pairs={{0,2},{2,4},{4,6},{6,0},{8,10},{10,12},{12,14},{14,8},{16,18},{18,... | collective-permute-start | bytes 393224 | tf_op jit(solution)/shard_map/ppermute | solution.py:250
  36.1 15.7 %copy-start.14 = (s32[1024]{0:T(1024)S(1)}, s32[1024]{0:T(1024)}, u32[]{:S(2)}) copy-start(s32[1024]{0:T(1024)} %param.21) | copy-start | bytes 12292
  41.3 14.7 %copy-start.11 = (s32[8192]{0:T(1024)S(1)}, s32[8192]{0:T(1024)}, u32[]{:S(2)}) copy-start(s32[8192]{0:T(1024)} %param.17) | copy-start | bytes 98308
  41.3 14.7 %copy-start.12 = (s32[8192]{0:T(1024)S(1)}, s32[8192]{0:T(1024)}, u32[]{:S(2)}) copy-start(s32[8192]{0:T(1024)} %param.18) | copy-start | bytes 98308
  41.3 37.1 %copy-start.16 = (bf16[256,512]{1,0:T(8,128)(2,1)S(1)}, bf16[256,512]{1,0:T(8,128)(2,1)}, u32[]{:S(2)}) copy-start(bf16[256,512]{1,0:T(8,128)(2,1)} %param.15) | copy-start | bytes 786436
  42.2 65.7 %all-to-all-start.1 = ((bf16[128,8,256]{2,1,0:T(8,128)(2,1)}), bf16[128,8,256]{2,1,0:T(8,128)(2,1)}, u32[]{:S(2)}, u32[]{:S(2)}) async-start(bf16[128,8,256]{2,1,0:T(8,128)(2,1)} %bitcast.14), calls=%async_computation.1 | async-start | bytes 1048576 | tf_op jit(solution)/shard_map/all_to_all | solution.py:259
  49.1 28.0 %collective-permute-start.10 = (bf16[4,256,256]{2,1,0:T(8,128)(2,1)S(1)}, bf16[4,256,256]{2,1,0:T(8,128)(2,1)}, u32[]{:S(2)}, u32[]{:S(2)}) collective-permute-start(bf16[4,256,256]{2,1,0:T(8,128)(2,1)S(1)} %pad_maximum_fusion.1.rest_0_), channel_id=1, source_target_pairs={{0,6},{2,0},{4,2},{6,4},{8,14},{10,8},{12,10},{14,12},{16,22},{18,... | collective-permute-start | bytes 1572872 | tf_op jit(solution)/shard_map/ppermute | solution.py:257
  55.9 24.2 %copy-start.4 = (bf16[1024,256]{1,0:T(8,128)(2,1)S(1)}, bf16[1024,256]{1,0:T(8,128)(2,1)}, u32[]{:S(2)}) copy-start(bf16[1024,256]{1,0:T(8,128)(2,1)} %copy-done.3) | copy-start | bytes 1572868
  55.9 24.2 %copy-start.6 = (bf16[1024,256]{1,0:T(8,128)(2,1)S(1)}, bf16[1024,256]{1,0:T(8,128)(2,1)}, u32[]{:S(2)}) copy-start(bf16[1024,256]{1,0:T(8,128)(2,1)} %copy-done.5) | copy-start | bytes 1572868
  55.9 24.2 %copy-start.17 = (bf16[256,512]{1,0:T(8,128)(2,1)S(1)}, bf16[256,512]{1,0:T(8,128)(2,1)}, u32[]{:S(2)}) copy-start(bf16[256,512]{1,0:T(8,128)(2,1)} %param.16) | copy-start | bytes 786436
  56.1 24.6 %collective-permute-start.9 = (bf16[4,256,256]{2,1,0:T(8,128)(2,1)S(1)}, bf16[4,256,256]{2,1,0:T(8,128)(2,1)S(1)}, u32[]{:S(2)}, u32[]{:S(2)}) collective-permute-start(bf16[4,256,256]{2,1,0:T(8,128)(2,1)S(1)} %pad_maximum_fusion.1.rest_0_), channel_id=1, source_target_pairs={{0,4},{2,6},{4,0},{6,2},{8,12},{10,14},{12,8},{14,10},{16,20},{18,... | collective-permute-start | bytes 1572872 | tf_op jit(solution)/shard_map/ppermute | solution.py:257
  57.0 25.6 %collective-permute-start.8 = (bf16[4,256,256]{2,1,0:T(8,128)(2,1)S(1)}, bf16[4,256,256]{2,1,0:T(8,128)(2,1)S(1)}, u32[]{:S(2)}, u32[]{:S(2)}) collective-permute-start(bf16[4,256,256]{2,1,0:T(8,128)(2,1)S(1)} %pad_maximum_fusion.1.rest_0_), channel_id=1, source_target_pairs={{0,2},{2,4},{4,6},{6,0},{8,10},{10,12},{12,14},{14,8},{16,18},{18,... | collective-permute-start | bytes 1572872 | tf_op jit(solution)/shard_map/ppermute | solution.py:257
  57.9 24.8 %collective-permute-start.13 = (bf16[4,256,256]{2,1,0:T(8,128)(2,1)}, bf16[4,256,256]{2,1,0:T(8,128)(2,1)S(1)}, u32[]{:S(2)}, u32[]{:S(2)}) collective-permute-start(bf16[4,256,256]{2,1,0:T(8,128)(2,1)} %pad_maximum_fusion.2.rest_4_), channel_id=1, source_target_pairs={{0,192},{2,194},{4,196},{6,198},{8,200},{10,202},{12,204},{14,206}... | collective-permute-start | bytes 1572872 | tf_op jit(solution)/shard_map/ppermute | solution.py:258
  58.3 24.3 %collective-permute-start.12 = (bf16[4,256,256]{2,1,0:T(8,128)(2,1)}, bf16[4,256,256]{2,1,0:T(8,128)(2,1)S(1)}, u32[]{:S(2)}, u32[]{:S(2)}) collective-permute-start(bf16[4,256,256]{2,1,0:T(8,128)(2,1)} %pad_maximum_fusion.2.rest_4_), channel_id=1, source_target_pairs={{0,128},{2,130},{4,132},{6,134},{8,136},{10,138},{12,140},{14,142}... | collective-permute-start | bytes 1572872 | tf_op jit(solution)/shard_map/ppermute | solution.py:258
  77.0 9.4 %collective-permute-start.11 = (bf16[4,256,256]{2,1,0:T(8,128)(2,1)}, bf16[4,256,256]{2,1,0:T(8,128)(2,1)S(1)}, u32[]{:S(2)}, u32[]{:S(2)}) collective-permute-start(bf16[4,256,256]{2,1,0:T(8,128)(2,1)} %pad_maximum_fusion.2.rest_4_), channel_id=1, source_target_pairs={{0,64},{2,66},{4,68},{6,70},{8,72},{10,74},{12,76},{14,78},{16,80}... | collective-permute-start | bytes 1572872 | tf_op jit(solution)/shard_map/ppermute | solution.py:258
  80.2 6.3 %copy-start.1 = (bf16[4,256,256]{2,1,0:T(8,128)(2,1)S(1)}, bf16[4,256,256]{2,1,0:T(8,128)(2,1)}, u32[]{:S(2)}) copy-start(bf16[4,256,256]{2,1,0:T(8,128)(2,1)} %pad_maximum_fusion.2.rest_4_) | copy-start | bytes 1572868
  107.9 39.8 %copy-start.8 = (bf16[4,256,256]{2,1,0:T(8,128)(2,1)S(1)}, bf16[4,256,256]{2,1,0:T(8,128)(2,1)}, u32[]{:S(2)}) copy-start(bf16[4,256,256]{2,1,0:T(8,128)(2,1)} %get-tuple-element.38) | copy-start | bytes 1572868
  107.9 47.8 %copy-start.7 = (bf16[4,256,256]{2,1,0:T(8,128)(2,1)S(1)}, bf16[4,256,256]{2,1,0:T(8,128)(2,1)}, u32[]{:S(2)}) copy-start(bf16[4,256,256]{2,1,0:T(8,128)(2,1)} %get-tuple-element.42) | copy-start | bytes 1572868
  109.2 21.8 %collective-permute-start.14 = (bf16[4,256,256]{2,1,0:T(8,128)(2,1)}, bf16[4,256,256]{2,1,0:T(8,128)(2,1)S(1)}, u32[]{:S(2)}, u32[]{:S(2)}) collective-permute-start(bf16[4,256,256]{2,1,0:T(8,128)(2,1)} %get-tuple-element.39), channel_id=1, source_target_pairs={{0,6},{2,0},{4,2},{6,4},{8,14},{10,8},{12,10},{14,12},{16,22},{18,... | collective-permute-start | bytes 1572872 | tf_op jit(solution)/shard_map/ppermute | solution.py:305
  112.8 34.8 %collective-permute-start.15 = (bf16[4,256,256]{2,1,0:T(8,128)(2,1)}, bf16[4,256,256]{2,1,0:T(8,128)(2,1)}, u32[]{:S(2)}, u32[]{:S(2)}) collective-permute-start(bf16[4,256,256]{2,1,0:T(8,128)(2,1)} %get-tuple-element.40), channel_id=1, source_target_pairs={{0,4},{2,6},{4,0},{6,2},{8,12},{10,14},{12,8},{14,10},{16,20},{18,... | collective-permute-start | bytes 1572872 | tf_op jit(solution)/shard_map/ppermute | solution.py:305
  112.8 34.8 %collective-permute-start.16 = (bf16[4,256,256]{2,1,0:T(8,128)(2,1)}, bf16[4,256,256]{2,1,0:T(8,128)(2,1)}, u32[]{:S(2)}, u32[]{:S(2)}) collective-permute-start(bf16[4,256,256]{2,1,0:T(8,128)(2,1)} %get-tuple-element.41), channel_id=1, source_target_pairs={{0,2},{2,4},{4,6},{6,0},{8,10},{10,12},{12,14},{14,8},{16,18},{18,... | collective-permute-start | bytes 1572872 | tf_op jit(solution)/shard_map/ppermute | solution.py:305
  113.8 37.4 %collective-permute-start.20 = (bf16[4,256,256]{2,1,0:T(8,128)(2,1)}, bf16[4,256,256]{2,1,0:T(8,128)(2,1)S(1)}, u32[]{:S(2)}, u32[]{:S(2)}) collective-permute-start(bf16[4,256,256]{2,1,0:T(8,128)(2,1)} %get-tuple-element.43), channel_id=1, source_target_pairs={{0,192},{2,194},{4,196},{6,198},{8,200},{10,202},{12,204},{14,206}... | collective-permute-start | bytes 1572872 | tf_op jit(solution)/shard_map/ppermute | solution.py:306
  116.0 39.7 %collective-permute-start.21 = (bf16[4,256,256]{2,1,0:T(8,128)(2,1)}, bf16[4,256,256]{2,1,0:T(8,128)(2,1)}, u32[]{:S(2)}, u32[]{:S(2)}) collective-permute-start(bf16[4,256,256]{2,1,0:T(8,128)(2,1)} %get-tuple-element.44), channel_id=1, source_target_pairs={{0,128},{2,130},{4,132},{6,134},{8,136},{10,138},{12,140},{14,142}... | collective-permute-start | bytes 1572872 | tf_op jit(solution)/shard_map/ppermute | solution.py:306
  131.0 20.2 %copy-start.10 = (bf16[4,256,256]{2,1,0:T(8,128)(2,1)}, bf16[4,256,256]{2,1,0:T(8,128)(2,1)S(1)}, u32[]{:S(2)}) copy-start(bf16[4,256,256]{2,1,0:T(8,128)(2,1)S(1)} %collective-permute-done.14) | copy-start | bytes 1572868
  131.0 24.7 %collective-permute-start.22 = (bf16[4,256,256]{2,1,0:T(8,128)(2,1)}, bf16[4,256,256]{2,1,0:T(8,128)(2,1)}, u32[]{:S(2)}, u32[]{:S(2)}) collective-permute-start(bf16[4,256,256]{2,1,0:T(8,128)(2,1)} %get-tuple-element.45), channel_id=1, source_target_pairs={{0,64},{2,66},{4,68},{6,70},{8,72},{10,74},{12,76},{14,78},{16,80}... | collective-permute-start | bytes 1572872 | tf_op jit(solution)/shard_map/ppermute | solution.py:306
  133.8 35.0 %all-to-all-start.2 = ((bf16[128,8,256]{2,1,0:T(8,128)(2,1)}), bf16[128,8,256]{2,1,0:T(8,128)(2,1)S(1)}, u32[]{:S(2)}, u32[]{:S(2)}) async-start(bf16[128,8,256]{2,1,0:T(8,128)(2,1)} %broadcast_in_dim.18), calls=%async_computation.2 | async-start | bytes 1048576 | tf_op jit(solution)/shard_map/all_to_all | solution.py:307
  149.1 10.9 %collective-permute-start.17 = (bf16[256,256]{1,0:T(8,128)(2,1)S(1)}, bf16[256,256]{1,0:T(8,128)(2,1)S(1)}, u32[]{:S(2)}, u32[]{:S(2)}) collective-permute-start(bf16[256,256]{1,0:T(8,128)(2,1)S(1)} %get-tuple-element.51), channel_id=1, source_target_pairs={{0,192},{2,194},{4,196},{6,198},{8,200},{10,202},{12,204},{14,206}... | collective-permute-start | bytes 393224 | tf_op jit(solution)/shard_map/ppermute | solution.py:313
  149.9 12.4 %collective-permute-start.19 = (bf16[256,256]{1,0:T(8,128)(2,1)S(1)}, bf16[256,256]{1,0:T(8,128)(2,1)S(1)}, u32[]{:S(2)}, u32[]{:S(2)}) collective-permute-start(bf16[256,256]{1,0:T(8,128)(2,1)S(1)} %get-tuple-element.52), channel_id=1, source_target_pairs={{0,64},{2,66},{4,68},{6,70},{8,72},{10,74},{12,76},{14,78},{16,80}... | collective-permute-start | bytes 393224 | tf_op jit(solution)/shard_map/ppermute | solution.py:313
  151.2 0.8 copy-start.9
  152.0 33.9 %copy-start.2 = (f32[1024,256]{1,0:T(8,128)S(1)}, f32[1024,256]{1,0:T(8,128)}, u32[]{:S(2)}) copy-start(f32[1024,256]{1,0:T(8,128)} %get-tuple-element.49.pre_ref) | copy-start | bytes 3145732
  152.0 10.3 %collective-permute-start.18 = (bf16[256,256]{1,0:T(8,128)(2,1)S(1)}, bf16[256,256]{1,0:T(8,128)(2,1)S(1)}, u32[]{:S(2)}, u32[]{:S(2)}) collective-permute-start(bf16[256,256]{1,0:T(8,128)(2,1)S(1)} %get-tuple-element.53), channel_id=1, source_target_pairs={{0,128},{2,130},{4,132},{6,134},{8,136},{10,138},{12,140},{14,142}... | collective-permute-start | bytes 393224 | tf_op jit(solution)/shard_map/ppermute | solution.py:313
  157.2 6.3 %collective-permute-start.23 = (bf16[256,256]{1,0:T(8,128)(2,1)S(1)}, bf16[256,256]{1,0:T(8,128)(2,1)S(1)}, u32[]{:S(2)}, u32[]{:S(2)}) collective-permute-start(bf16[256,256]{1,0:T(8,128)(2,1)S(1)} %get-tuple-element.54), channel_id=1, source_target_pairs={{0,6},{2,0},{4,2},{6,4},{8,14},{10,8},{12,10},{14,12},{16,22},{18,... | collective-permute-start | bytes 393224 | tf_op jit(solution)/shard_map/ppermute | solution.py:316
  160.0 7.6 %collective-permute-start.25 = (bf16[256,256]{1,0:T(8,128)(2,1)S(1)}, bf16[256,256]{1,0:T(8,128)(2,1)S(1)}, u32[]{:S(2)}, u32[]{:S(2)}) collective-permute-start(bf16[256,256]{1,0:T(8,128)(2,1)S(1)} %get-tuple-element.55), channel_id=1, source_target_pairs={{0,2},{2,4},{4,6},{6,0},{8,10},{10,12},{12,14},{14,8},{16,18},{18,... | collective-permute-start | bytes 393224 | tf_op jit(solution)/shard_map/ppermute | solution.py:316
  160.0 7.6 %collective-permute-start.24 = (bf16[256,256]{1,0:T(8,128)(2,1)S(1)}, bf16[256,256]{1,0:T(8,128)(2,1)S(1)}, u32[]{:S(2)}, u32[]{:S(2)}) collective-permute-start(bf16[256,256]{1,0:T(8,128)(2,1)S(1)} %get-tuple-element.56), channel_id=1, source_target_pairs={{0,4},{2,6},{4,0},{6,2},{8,12},{10,14},{12,8},{14,10},{16,20},{18,... | collective-permute-start | bytes 393224 | tf_op jit(solution)/shard_map/ppermute | solution.py:316

commit v5 on v4

--- a/solution.py
+++ b/solution.py
@@ -35,6 +35,15 @@
 def columns():
     nx, nz, ny = GRID
     return [[(x * nz + z) * ny + y for z in range(nz)] for x in range(nx) for y in range(ny)]
+
+
+def planes():
+    nx, nz, ny = GRID
+    return [[(x * nz + z) * ny + y for x in range(nx) for y in range(ny)] for z in range(nz)]
+
+
+def swap(array, groups):
+    return lax.all_to_all(array, "dom", split_axis=0, concat_axis=0, axis_index_groups=groups, tiled=True)
 
 
 def sum_of(arrays):
@@ -256,9 +265,8 @@
     low_set, high_set, pay = lax.optimization_barrier((low_set, high_set, pay))
     low_got = [low_set] + [lax.ppermute(low_set, "dom", ring("y", k)) for k in range(1, ny)]
     high_got = [high_set] + [lax.ppermute(high_set, "dom", ring("x", k)) for k in range(1, nx)]
-    pieces = lax.all_to_all(
-        pay.reshape(parts, tail, width), "dom", split_axis=0, concat_axis=0, tiled=True
-    )
+    pieces = swap(pay.reshape(nz, -1, width), columns())
+    pieces = swap(jnp.sum(pieces.astype(jnp.float32), axis=0).reshape(nx * ny, tail, width), planes())
 
     order = mirror_master.reshape(nx, 2, deep, ny, slots).transpose(0, 3, 1, 2, 4)
     spots = order.reshape(nx * ny * 2, deep * slots) + jnp.repeat(
@@ -288,7 +296,7 @@
     lanes = local * halves
     low_type = pltpu.HBM(low_set.shape, jnp.bfloat16)
     high_type = pltpu.HBM(high_set.shape, jnp.bfloat16)
-    results = pl.pallas_call(
+    edge_call = pl.pallas_call(
         functools.partial(edge_kernel, GRID, slots),
         out_shape=[pltpu.HBM((masters, width), jnp.float32)] + [low_type] * ny + [high_type] * nx,
         in_specs=[SMEM] * 3 + [VMEM] * (4 + nx + ny),
@@ -297,16 +305,16 @@
         + [pltpu.VMEM((lanes + SUB * halves, LANES), jnp.float32) for _ in range(CHAINS)],
         compiler_params=pltpu.CompilerParams(vmem_limit_bytes=34 << 20),
         name="edges",
-    )(from_at, to_at, place, *(near(a) for a in (scaled, self_part, spots, chosen, *low_got, *high_got)))
+    )
+    results = edge_call(from_at, to_at, place, *(near(a) for a in (scaled, self_part, spots, chosen, *low_got, *high_got)))
     pre, low_back, high_back = results[0], results[1 : 1 + ny], results[1 + ny :]
 
-    share = jnp.sum(pieces.astype(jnp.float32), axis=0).astype(jnp.bfloat16)
+    share = jnp.sum(pieces, axis=0).astype(jnp.bfloat16)
     low_back, high_back, share = lax.optimization_barrier((low_back, high_back, share))
     low_part = [low_back[0]] + [lax.ppermute(low_back[k], "dom", ring("y", -k)) for k in range(1, ny)]
     high_part = [high_back[0]] + [lax.ppermute(high_back[k], "dom", ring("x", -k)) for k in range(1, nx)]
-    weights = lax.all_to_all(
-        jnp.broadcast_to(share, (parts, *share.shape)), "dom", split_axis=0, concat_axis=0, tiled=True
-    )
+    weights = swap(jnp.broadcast_to(share, (nx * ny, *share.shape)), planes()).reshape(-1, width)
+    weights = swap(jnp.broadcast_to(weights, (nz, *weights.shape)), columns()).reshape(parts, tail, width)
     low_sum = [sum_of([p[k] for p in low_part]) for k in range(nx)]
     high_sum = [sum_of([p[k] for p in high_part]) for k in range(ny)]
     low_sent = [low_sum[0]] + [

time: 188 us -> 186 us (0.989)
  blocking collectives: 17 us -> 29.9 us
  starting transfers between devices: 69.8 us -> 59.4 us
  waiting for transfers between devices: 53.9 us -> 46.3 us
  matrix products: 4.25 us -> 6.47 us
    all_to_all x0 -> x1, blocking collectives: none -> 12.4 us  [swap(): lax.all_to_all(array, 'dom', split_axis=0, concat_axis=0, axis_index_grou...]
    ppermute x3, waiting for transfers between devices: 18 us -> 6.97 us  [on_device(): lax.ppermute(low_set, 'dom', ring('y', k))]
    all_to_all x2 -> x3, starting transfers between devices: 20.7 us -> 17.1 us  [swap(): lax.all_to_all(array, 'dom', split_axis=0, concat_axis=0, axis_index_grou...]
    ppermute x3, waiting for transfers between devices: 12.9 us -> 16.2 us  [on_device(): lax.ppermute(low_back[k], 'dom', ring('y', -k))]
    ppermute x3, starting transfers between devices: 4.56 us -> 1.47 us  [on_device(): lax.ppermute(high_set, 'dom', ring('x', k))]
    dot_general x2, matrix products: 1.63 us -> 3.69 us  [scale(): lax.dot_general(cols, w_neigh, contract, preferred_element_type=jnp.float32)]
  transfers between devices with their start and end apart: 29 -> 30, of which waited for: 10 -> 12; matrix products, arithmetic and copies ran while one was open for 7% -> 9% of each run, Pallas kernels for 13% -> 13%
where the time goes in v5:
time: 186 us
  starting transfers between devices  59.4 us (32%)
  waiting for transfers between devices  46.3 us (25%)
  blocking collectives  29.9 us (16%)
  Pallas kernels  27 us (15%)
  other arithmetic  12 us (6%)
  matrix products  6.47 us (3%)
  local copies, waits for them, and re-layouts  2.84 us (2%)
    pallas_call x1, Pallas kernels, on_device(): edge_call(from_at, to_at, place, *(near(a) for a in (scaled, self_part, s...  21.7 us
    all_to_all x1, blocking collectives, on_device(): lax.all_to_all(column_sum.reshape(nz, hub, width), 'dom', split_axis=0, c...  17.5 us
    all_to_all x3, starting transfers between devices, swap(): lax.all_to_all(array, 'dom', split_axis=0, concat_axis=0, axis_index_grou...  17.1 us
    ppermute x3, waiting for transfers between devices, on_device(): lax.ppermute(low_back[k], 'dom', ring('y', -k))  16.2 us
    all_to_all x1, blocking collectives, swap(): lax.all_to_all(array, 'dom', split_axis=0, concat_axis=0, axis_index_grou...  12.4 us
    all_to_all x1, waiting for transfers between devices, on_device(): lax.all_to_all(copies, 'dom', split_axis=0, concat_axis=0, axis_index_gro...  10.4 us
    all_to_all x1, starting transfers between devices, on_device(): lax.all_to_all(copies, 'dom', split_axis=0, concat_axis=0, axis_index_gro...  8.47 us
    ppermute x3, starting transfers between devices, on_device(): lax.ppermute(high_back[k], 'dom', ring('x', -k))  7.53 us
  transfers between devices with their start and end apart: 30, of which 12 were waited for; matrix products, arithmetic and copies ran while one was open for 9% of the time, Pallas kernels for 13%

profile of v5, /device:TPU:2, one launch (start us, length us, event | category | flops | bytes accessed | tf_op | source)
XLA Modules:
  0.0 185.6 jit_solution(13081589084807465688)
XLA Ops:
  0.7 0.8 select_convert_fusion.1
  1.6 0.7 slice_convert_fusion
  2.3 0.5 collective-permute-done.1
  2.8 1.2 fusion.3
  4.0 0.7 broadcast_in_dim.20
  4.7 8.5 %all-to-all-start = ((bf16[8,64,256]{2,1,0:T(8,128)(2,1)}), bf16[8,64,256]{2,1,0:T(8,128)(2,1)S(1)}, u32[]{:S(2)}, u32[]{:S(2)}) async-start(bf16[8,64,256]{2,1,0:T(8,128)(2,1)} %broadcast_in_dim.20), calls=%async_computation | async-start | bytes 524288 | tf_op jit(solution)/shard_map/all_to_all | solution.py:243
  13.2 1.4 select_convert_fusion
  14.5 0.1 collective-permute-start
  14.9 0.1 reshape.101
  15.0 10.4 %all-to-all-done = bf16[8,64,256]{2,1,0:T(8,128)(2,1)S(1)} async-done(((bf16[8,64,256]{2,1,0:T(8,128)(2,1)}), bf16[8,64,256]{2,1,0:T(8,128)(2,1)S(1)}, u32[]{:S(2)}, u32[]{:S(2)}) %all-to-all-start) | async-done | bytes 262176 | tf_op jit(solution)/shard_map/all_to_all | solution.py:243
  25.4 0.6 collective-permute-start.4
  26.0 2.4 %collective-permute-start.3 = (bf16[256,256]{1,0:T(8,128)(2,1)S(1)}, bf16[256,256]{1,0:T(8,128)(2,1)S(1)}, u32[]{:S(2)}, u32[]{:S(2)}) collective-permute-start(bf16[256,256]{1,0:T(8,128)(2,1)S(1)} %bitcast.62), channel_id=1, source_target_pairs={{0,128},{2,130},{4,132},{6,134},{8,136},{10,138},{12,140},{14,142}... | collective-permute-start | bytes 393224 | tf_op jit(solution)/shard_map/ppermute | solution.py:258
  28.4 1.8 collective-permute-start.2
  30.2 3.0 %collective-permute-start.7 = (bf16[256,256]{1,0:T(8,128)(2,1)S(1)}, bf16[256,256]{1,0:T(8,128)(2,1)S(1)}, u32[]{:S(2)}, u32[]{:S(2)}) collective-permute-start(bf16[256,256]{1,0:T(8,128)(2,1)S(1)} %bitcast.57), channel_id=1, source_target_pairs={{0,6},{2,0},{4,2},{6,4},{8,14},{10,8},{12,10},{14,12},{16,22},{18,... | collective-permute-start | bytes 393224 | tf_op jit(solution)/shard_map/ppermute | solution.py:259
  33.2 0.6 collective-permute-start.6
  34.0 0.5 fusion.1
  34.5 0.5 fusion.2
  35.1 1.0 collective-permute-start.5
  36.1 0.9 pad_maximum_fusion.3
  37.0 0.2 collective-permute-done.7
  37.2 2.5 %collective-permute-done.6 = bf16[256,256]{1,0:T(8,128)(2,1)S(1)} collective-permute-done((bf16[256,256]{1,0:T(8,128)(2,1)S(1)}, bf16[256,256]{1,0:T(8,128)(2,1)S(1)}, u32[]{:S(2)}, u32[]{:S(2)}) %collective-permute-start.6) | collective-permute-done | bytes 131104 | tf_op jit(solution)/shard_map/ppermute | solution.py:259
  39.7 1.6 collective-permute-done.5
  41.3 0.9 pad_maximum_fusion.2.rest_4_
  42.2 4.1 %all-to-all-start.1 = ((bf16[8,128,256]{2,1,0:T(8,128)(2,1)}), bf16[8,128,256]{2,1,0:T(8,128)(2,1)}, u32[]{:S(2)}, u32[]{:S(2)}) async-start(bf16[8,128,256]{2,1,0:T(8,128)(2,1)} %bitcast.14), calls=%async_computation.1 | async-start | bytes 1048576 | tf_op jit(solution)/shard_map/all_to_all | solution.py:46
  46.3 0.5 collective-permute-start.10
  47.5 3.3 %picks.1.pick_ref = bf16[32,128,256]{2,1,0:T(8,128)(2,1)S(1)} custom-call(s32[32,128]{1,0:T(8,128)S(1)} %broadcast_add_fusion.spot_ref), custom_call_target="tpu_custom_call" | custom-call | tf_op jit(solution)/shard_map/picks/pallas_call | solution.py:275
  51.0 1.5 collective-permute-start.9
  52.5 1.3 collective-permute-start.8
  53.8 0.2 collective-permute-start.13
  54.1 1.2 collective-permute-start.12
  55.3 6.0 %collective-permute-done.10.rest_3_ = bf16[4,256,256]{2,1,0:T(8,128)(2,1)} collective-permute-done((bf16[4,256,256]{2,1,0:T(8,128)(2,1)S(1)}, bf16[4,256,256]{2,1,0:T(8,128)(2,1)}, u32[]{:S(2)}, u32[]{:S(2)}) %collective-permute-start.10) | collective-permute-done | bytes 524320 | tf_op jit(solution)/shard_map/ppermute | solution.py:266
  61.3 2.5 %fusion.own_ref = bf16[1024,256]{1,0:T(8,128)(2,1)} fusion(bf16[256,512]{1,0:T(8,128)(2,1)} %param.16, f32[1024]{0:T(1024)S(1)} %convert_element_type.190, bf16[1024,256]{1,0:T(8,128)(2,1)} %copy-done.5, bf16[1024,256]{1,0:T(8,128)(2,1)} %copy-done.4), kind=kOutput, calls=%fused_computation.1 | convolution fusion | flops 271056896 | bytes 1839104 | tf_op jit(solution)/shard_map/dot_general | solution.py:238
  63.9 1.8 convert_reduce_fusion
  65.6 6.4 %all-to-all-start.2 = ((f32[16,8,256]{2,1,0:T(8,128)}), f32[16,8,256]{2,1,0:T(8,128)S(1)}, u32[]{:S(2)}, u32[]{:S(2)}) async-start(f32[16,8,256]{2,1,0:T(8,128)} %bitcast.15), calls=%async_computation.2 | async-start | bytes 262144 | tf_op jit(solution)/shard_map/all_to_all | solution.py:46
  72.1 1.8 fusion.35.self_ref
  73.9 0.9 collective-permute-done.8.rest_1_
  74.9 2.3 %collective-permute-done.13.rest_7_ = bf16[4,256,256]{2,1,0:T(8,128)(2,1)} collective-permute-done((bf16[4,256,256]{2,1,0:T(8,128)(2,1)}, bf16[4,256,256]{2,1,0:T(8,128)(2,1)}, u32[]{:S(2)}, u32[]{:S(2)}) %collective-permute-start.13) | collective-permute-done | bytes 524320 | tf_op jit(solution)/shard_map/ppermute | solution.py:267
  77.2 1.5 collective-permute-done.11.rest_5_
  78.7 21.7 %edges.1 = (f32[1024,256]{1,0:T(8,128)}, bf16[4,256,256]{2,1,0:T(8,128)(2,1)}, bf16[4,256,256]{2,1,0:T(8,128)(2,1)}, bf16[4,256,256]{2,1,0:T(8,128)(2,1)}, bf16[...) custom-call(s32[8192]{0:T(1024)S(1)} %get-tuple-element.71.from_ref,, ...), custom_call_target="tpu_custom_call" | custom-call | tf_op jit(solution)/shard_map/edges/pallas_call | solution.py:309
  100.4 2.1 %collective-permute-start.14 = (bf16[4,256,256]{2,1,0:T(8,128)(2,1)}, bf16[4,256,256]{2,1,0:T(8,128)(2,1)S(1)}, u32[]{:S(2)}, u32[]{:S(2)}) collective-permute-start(bf16[4,256,256]{2,1,0:T(8,128)(2,1)} %get-tuple-element.39), channel_id=1, source_target_pairs={{0,6},{2,0},{4,2},{6,4},{8,14},{10,8},{12,10},{14,12},{16,22},{18,... | collective-permute-start | bytes 1572872 | tf_op jit(solution)/shard_map/ppermute | solution.py:314
  102.4 0.9 collective-permute-start.15
  103.3 0.6 collective-permute-start.16
  103.9 2.2 %collective-permute-start.20 = (bf16[4,256,256]{2,1,0:T(8,128)(2,1)}, bf16[4,256,256]{2,1,0:T(8,128)(2,1)S(1)}, u32[]{:S(2)}, u32[]{:S(2)}) collective-permute-start(bf16[4,256,256]{2,1,0:T(8,128)(2,1)} %get-tuple-element.43), channel_id=1, source_target_pairs={{0,192},{2,194},{4,196},{6,198},{8,200},{10,202},{12,204},{14,206}... | collective-permute-start | bytes 1572872 | tf_op jit(solution)/shard_map/ppermute | solution.py:315
  106.2 1.4 collective-permute-start.21
  107.6 16.2 %collective-permute-done.14 = bf16[4,256,256]{2,1,0:T(8,128)(2,1)S(1)} collective-permute-done((bf16[4,256,256]{2,1,0:T(8,128)(2,1)}, bf16[4,256,256]{2,1,0:T(8,128)(2,1)S(1)}, u32[]{:S(2)}, u32[]{:S(2)}) %collective-permute-start.14) | collective-permute-done | bytes 524320 | tf_op jit(solution)/shard_map/ppermute | solution.py:314
  123.8 3.9 %collective-permute-start.22 = (bf16[4,256,256]{2,1,0:T(8,128)(2,1)}, bf16[4,256,256]{2,1,0:T(8,128)(2,1)}, u32[]{:S(2)}, u32[]{:S(2)}) collective-permute-start(bf16[4,256,256]{2,1,0:T(8,128)(2,1)} %get-tuple-element.45), channel_id=1, source_target_pairs={{0,64},{2,66},{4,68},{6,70},{8,72},{10,74},{12,76},{14,78},{16,80}... | collective-permute-start | bytes 1572872 | tf_op jit(solution)/shard_map/ppermute | solution.py:315
  127.7 12.4 %all_to_all.30 = bf16[16,8,256]{2,1,0:T(8,128)(2,1)S(1)} all-to-all(bf16[16,8,256]{2,1,0:T(8,128)(2,1)S(1)} %broadcast_in_dim.21), channel_id=1, replica_groups={{0,2,4,6,64,66,68,70,128,130,132,134,192,194,196,198},{8,10,12,14,72,74..., dimensions={0} | all-to-all | bytes 131072 | tf_op jit(solution)/shard_map/all_to_all | solution.py:46
  140.1 0.8 broadcast_in_dim.22
  140.9 6.5 %all-to-all-start.4 = ((bf16[8,128,256]{2,1,0:T(8,128)(2,1)}), bf16[8,128,256]{2,1,0:T(8,128)(2,1)S(1)}, u32[]{:S(2)}, u32[]{:S(2)}) async-start(bf16[8,128,256]{2,1,0:T(8,128)(2,1)} %broadcast_in_dim.22), calls=%async_computation.4 | async-start | bytes 1048576 | tf_op jit(solution)/shard_map/all_to_all | solution.py:46
  147.5 1.4 fusion.10
  148.9 1.6 collective-permute-start.17
  150.5 0.5 collective-permute-start.19
  151.0 0.8 copy-done.8
  151.8 2.7 %collective-permute-start.18 = (bf16[256,256]{1,0:T(8,128)(2,1)S(1)}, bf16[256,256]{1,0:T(8,128)(2,1)S(1)}, u32[]{:S(2)}, u32[]{:S(2)}) collective-permute-start(bf16[256,256]{1,0:T(8,128)(2,1)S(1)} %get-tuple-element.53), channel_id=1, source_target_pairs={{0,128},{2,130},{4,132},{6,134},{8,136},{10,138},{12,140},{14,142}... | collective-permute-start | bytes 393224 | tf_op jit(solution)/shard_map/ppermute | solution.py:321
  154.5 1.5 fusion.13
  156.0 1.3 collective-permute-start.23
  157.3 0.8 collective-permute-start.25
  158.1 1.4 collective-permute-start.24
  159.5 1.2 fusion.9
  160.7 0.4 collective-permute-done.23
  161.1 3.8 %collective-permute-done.25 = bf16[256,256]{1,0:T(8,128)(2,1)S(1)} collective-permute-done((bf16[256,256]{1,0:T(8,128)(2,1)S(1)}, bf16[256,256]{1,0:T(8,128)(2,1)S(1)}, u32[]{:S(2)}, u32[]{:S(2)}) %collective-permute-start.25) | collective-permute-done | bytes 131104 | tf_op jit(solution)/shard_map/ppermute | solution.py:324
  164.9 1.2 fusion.6
  166.1 17.5 %all_to_all.31.home_ref = bf16[8,64,256]{2,1,0:T(8,128)(2,1)S(1)} all-to-all(bf16[8,64,256]{2,1,0:T(8,128)(2,1)S(1)} %bitcast.56), channel_id=1, replica_groups={{0,8,16,24,32,40,48,56},{2,10,18,26,34,42,50,58},{4,12,20,28,36,44,52,6..., dimensions={0} | all-to-all | bytes 524288 | tf_op jit(solution)/shard_map/all_to_all | solution.py:328
  183.6 2.0 %final.1 = (bf16[1024,256]{1,0:T(8,128)(2,1)}, f32[256,512]{1,0:T(8,128)}, f32[256,512]{1,0:T(8,128)}) custom-call(bf16[8,64,256]{2,1,0:T(8,128)(2,1)S(1)} %all_to_all.31.home_ref, f32[1024,256]{1,0:T(8,128)S(1)} %copy-done.2, bf16[128,8,256]{2,1,0:T(8,128)(2,1)S(1)} %bitcast.55), custom_call_target="tpu_custom_call" | custom-call | tf_op jit(solution)/shard_map/final/pallas_call | solution.py:336
  (67 shorter events, 0.9 us)
Async XLA Ops:
  0.6 33.4 %copy-start = (bf16[1024,256]{1,0:T(8,128)(2,1)S(1)}, bf16[1024,256]{1,0:T(8,128)(2,1)}, u32[]{:S(2)}) copy-start(bf16[1024,256]{1,0:T(8,128)(2,1)} %param.11) | copy-start | bytes 1572868
  0.6 14.1 %copy-start.12 = (s32[4096]{0:T(1024)S(1)}, s32[4096]{0:T(1024)}, u32[]{:S(2)}) copy-start(s32[4096]{0:T(1024)} %param.20) | copy-start | bytes 49156
  1.5 1.3 collective-permute-start.1
  4.7 20.7 %all-to-all-start = ((bf16[8,64,256]{2,1,0:T(8,128)(2,1)}), bf16[8,64,256]{2,1,0:T(8,128)(2,1)S(1)}, u32[]{:S(2)}, u32[]{:S(2)}) async-start(bf16[8,64,256]{2,1,0:T(8,128)(2,1)} %broadcast_in_dim.20), calls=%async_computation | async-start | bytes 524288 | tf_op jit(solution)/shard_map/all_to_all | solution.py:243
  14.5 18.7 %collective-permute-start = (bf16[1024,256]{1,0:T(8,128)(2,1)S(1)}, bf16[1024,256]{1,0:T(8,128)(2,1)S(1)}, u32[]{:S(2)}, u32[]{:S(2)}) collective-permute-start(bf16[1024,256]{1,0:T(8,128)(2,1)S(1)} %select_convert_fusion), channel_id=1, source_target_pairs={{0,1},{1,0},{2,3},{3,2},{4,5},{5,4},{6,7},{7,6},{8,9},{9,8},{10,11... | collective-permute-start | bytes 1572872 | tf_op jit(solution)/shard_map/ppermute | solution.py:234
  25.4 9.7 %collective-permute-start.4 = (bf16[256,256]{1,0:T(8,128)(2,1)S(1)}, bf16[256,256]{1,0:T(8,128)(2,1)S(1)}, u32[]{:S(2)}, u32[]{:S(2)}) collective-permute-start(bf16[256,256]{1,0:T(8,128)(2,1)S(1)} %bitcast.61), channel_id=1, source_target_pairs={{0,192},{2,194},{4,196},{6,198},{8,200},{10,202},{12,204},{14,206}... | collective-permute-start | bytes 393224 | tf_op jit(solution)/shard_map/ppermute | solution.py:258
  26.0 11.0 %collective-permute-start.3 = (bf16[256,256]{1,0:T(8,128)(2,1)S(1)}, bf16[256,256]{1,0:T(8,128)(2,1)S(1)}, u32[]{:S(2)}, u32[]{:S(2)}) collective-permute-start(bf16[256,256]{1,0:T(8,128)(2,1)S(1)} %bitcast.62), channel_id=1, source_target_pairs={{0,128},{2,130},{4,132},{6,134},{8,136},{10,138},{12,140},{14,142}... | collective-permute-start | bytes 393224 | tf_op jit(solution)/shard_map/ppermute | solution.py:258
  28.4 8.5 %collective-permute-start.2 = (bf16[256,256]{1,0:T(8,128)(2,1)S(1)}, bf16[256,256]{1,0:T(8,128)(2,1)S(1)}, u32[]{:S(2)}, u32[]{:S(2)}) collective-permute-start(bf16[256,256]{1,0:T(8,128)(2,1)S(1)} %bitcast.63), channel_id=1, source_target_pairs={{0,64},{2,66},{4,68},{6,70},{8,72},{10,74},{12,76},{14,78},{16,80}... | collective-permute-start | bytes 393224 | tf_op jit(solution)/shard_map/ppermute | solution.py:258
  30.2 4.3 %copy-start.14 = (bf16[1024,256]{1,0:T(8,128)(2,1)S(1)}, bf16[1024,256]{1,0:T(8,128)(2,1)}, u32[]{:S(2)}) copy-start(bf16[1024,256]{1,0:T(8,128)(2,1)} %param.14) | copy-start | bytes 1572868
  30.2 7.0 %collective-permute-start.7 = (bf16[256,256]{1,0:T(8,128)(2,1)S(1)}, bf16[256,256]{1,0:T(8,128)(2,1)S(1)}, u32[]{:S(2)}, u32[]{:S(2)}) collective-permute-start(bf16[256,256]{1,0:T(8,128)(2,1)S(1)} %bitcast.57), channel_id=1, source_target_pairs={{0,6},{2,0},{4,2},{6,4},{8,14},{10,8},{12,10},{14,12},{16,22},{18,... | collective-permute-start | bytes 393224 | tf_op jit(solution)/shard_map/ppermute | solution.py:259
  33.2 6.5 %collective-permute-start.6 = (bf16[256,256]{1,0:T(8,128)(2,1)S(1)}, bf16[256,256]{1,0:T(8,128)(2,1)S(1)}, u32[]{:S(2)}, u32[]{:S(2)}) collective-permute-start(bf16[256,256]{1,0:T(8,128)(2,1)S(1)} %bitcast.58), channel_id=1, source_target_pairs={{0,4},{2,6},{4,0},{6,2},{8,12},{10,14},{12,8},{14,10},{16,20},{18,... | collective-permute-start | bytes 393224 | tf_op jit(solution)/shard_map/ppermute | solution.py:259
  34.0 1.0 copy-start.4
  34.0 1.0 copy-start.5
  35.1 6.3 %collective-permute-start.5 = (bf16[256,256]{1,0:T(8,128)(2,1)S(1)}, bf16[256,256]{1,0:T(8,128)(2,1)S(1)}, u32[]{:S(2)}, u32[]{:S(2)}) collective-permute-start(bf16[256,256]{1,0:T(8,128)(2,1)S(1)} %bitcast.59), channel_id=1, source_target_pairs={{0,2},{2,4},{4,6},{6,0},{8,10},{10,12},{12,14},{14,8},{16,18},{18,... | collective-permute-start | bytes 393224 | tf_op jit(solution)/shard_map/ppermute | solution.py:259
  36.1 10.7 %copy-start.13 = (s32[1024]{0:T(1024)S(1)}, s32[1024]{0:T(1024)}, u32[]{:S(2)}) copy-start(s32[1024]{0:T(1024)} %param.21) | copy-start | bytes 12292
  41.3 9.6 %copy-start.10 = (s32[8192]{0:T(1024)S(1)}, s32[8192]{0:T(1024)}, u32[]{:S(2)}) copy-start(s32[8192]{0:T(1024)} %param.17) | copy-start | bytes 98308
  41.3 9.6 %copy-start.11 = (s32[8192]{0:T(1024)S(1)}, s32[8192]{0:T(1024)}, u32[]{:S(2)}) copy-start(s32[8192]{0:T(1024)} %param.18) | copy-start | bytes 98308
  42.2 21.7 %all-to-all-start.1 = ((bf16[8,128,256]{2,1,0:T(8,128)(2,1)}), bf16[8,128,256]{2,1,0:T(8,128)(2,1)}, u32[]{:S(2)}, u32[]{:S(2)}) async-start(bf16[8,128,256]{2,1,0:T(8,128)(2,1)} %bitcast.14), calls=%async_computation.1 | async-start | bytes 1048576 | tf_op jit(solution)/shard_map/all_to_all | solution.py:46
  46.3 15.0 %collective-permute-start.10 = (bf16[4,256,256]{2,1,0:T(8,128)(2,1)S(1)}, bf16[4,256,256]{2,1,0:T(8,128)(2,1)}, u32[]{:S(2)}, u32[]{:S(2)}) collective-permute-start(bf16[4,256,256]{2,1,0:T(8,128)(2,1)S(1)} %pad_maximum_fusion.1.rest_0_), channel_id=1, source_target_pairs={{0,6},{2,0},{4,2},{6,4},{8,14},{10,8},{12,10},{14,12},{16,22},{18,... | collective-permute-start | bytes 1572872 | tf_op jit(solution)/shard_map/ppermute | solution.py:266
  51.0 22.9 %collective-permute-start.9 = (bf16[4,256,256]{2,1,0:T(8,128)(2,1)S(1)}, bf16[4,256,256]{2,1,0:T(8,128)(2,1)}, u32[]{:S(2)}, u32[]{:S(2)}) collective-permute-start(bf16[4,256,256]{2,1,0:T(8,128)(2,1)S(1)} %pad_maximum_fusion.1.rest_0_), channel_id=1, source_target_pairs={{0,4},{2,6},{4,0},{6,2},{8,12},{10,14},{12,8},{14,10},{16,20},{18,... | collective-permute-start | bytes 1572872 | tf_op jit(solution)/shard_map/ppermute | solution.py:266
  52.5 22.3 %collective-permute-start.8 = (bf16[4,256,256]{2,1,0:T(8,128)(2,1)S(1)}, bf16[4,256,256]{2,1,0:T(8,128)(2,1)}, u32[]{:S(2)}, u32[]{:S(2)}) collective-permute-start(bf16[4,256,256]{2,1,0:T(8,128)(2,1)S(1)} %pad_maximum_fusion.1.rest_0_), channel_id=1, source_target_pairs={{0,2},{2,4},{4,6},{6,0},{8,10},{10,12},{12,14},{14,8},{16,18},{18,... | collective-permute-start | bytes 1572872 | tf_op jit(solution)/shard_map/ppermute | solution.py:266
  53.8 23.3 %collective-permute-start.13 = (bf16[4,256,256]{2,1,0:T(8,128)(2,1)}, bf16[4,256,256]{2,1,0:T(8,128)(2,1)}, u32[]{:S(2)}, u32[]{:S(2)}) collective-permute-start(bf16[4,256,256]{2,1,0:T(8,128)(2,1)} %pad_maximum_fusion.2.rest_4_), channel_id=1, source_target_pairs={{0,192},{2,194},{4,196},{6,198},{8,200},{10,202},{12,204},{14,206}... | collective-permute-start | bytes 1572872 | tf_op jit(solution)/shard_map/ppermute | solution.py:267
  54.1 23.1 %collective-permute-start.12 = (bf16[4,256,256]{2,1,0:T(8,128)(2,1)}, bf16[4,256,256]{2,1,0:T(8,128)(2,1)}, u32[]{:S(2)}, u32[]{:S(2)}) collective-permute-start(bf16[4,256,256]{2,1,0:T(8,128)(2,1)} %pad_maximum_fusion.2.rest_4_), channel_id=1, source_target_pairs={{0,128},{2,130},{4,132},{6,134},{8,136},{10,138},{12,140},{14,142}... | collective-permute-start | bytes 1572872 | tf_op jit(solution)/shard_map/ppermute | solution.py:267
  61.3 17.3 %collective-permute-start.11 = (bf16[4,256,256]{2,1,0:T(8,128)(2,1)}, bf16[4,256,256]{2,1,0:T(8,128)(2,1)}, u32[]{:S(2)}, u32[]{:S(2)}) collective-permute-start(bf16[4,256,256]{2,1,0:T(8,128)(2,1)} %pad_maximum_fusion.2.rest_4_), channel_id=1, source_target_pairs={{0,64},{2,66},{4,68},{6,70},{8,72},{10,74},{12,76},{14,78},{16,80}... | collective-permute-start | bytes 1572872 | tf_op jit(solution)/shard_map/ppermute | solution.py:267
  65.6 34.7 %all-to-all-start.2 = ((f32[16,8,256]{2,1,0:T(8,128)}), f32[16,8,256]{2,1,0:T(8,128)S(1)}, u32[]{:S(2)}, u32[]{:S(2)}) async-start(f32[16,8,256]{2,1,0:T(8,128)} %bitcast.15), calls=%async_computation.2 | async-start | bytes 262144 | tf_op jit(solution)/shard_map/all_to_all | solution.py:46
  72.1 6.6 %copy-start.1 = (bf16[4,256,256]{2,1,0:T(8,128)(2,1)S(1)}, bf16[4,256,256]{2,1,0:T(8,128)(2,1)}, u32[]{:S(2)}) copy-start(bf16[4,256,256]{2,1,0:T(8,128)(2,1)} %pad_maximum_fusion.2.rest_4_) | copy-start | bytes 1572868
  72.1 6.6 %copy-start.3 = (bf16[1024,256]{1,0:T(8,128)(2,1)S(1)}, bf16[1024,256]{1,0:T(8,128)(2,1)}, u32[]{:S(2)}) copy-start(bf16[1024,256]{1,0:T(8,128)(2,1)} %fusion.own_ref) | copy-start | bytes 1572868
  100.3 47.2 %copy-start.7 = (bf16[4,256,256]{2,1,0:T(8,128)(2,1)S(1)}, bf16[4,256,256]{2,1,0:T(8,128)(2,1)}, u32[]{:S(2)}) copy-start(bf16[4,256,256]{2,1,0:T(8,128)(2,1)} %get-tuple-element.38) | copy-start | bytes 1572868
  100.3 54.2 %copy-start.6 = (bf16[4,256,256]{2,1,0:T(8,128)(2,1)S(1)}, bf16[4,256,256]{2,1,0:T(8,128)(2,1)}, u32[]{:S(2)}) copy-start(bf16[4,256,256]{2,1,0:T(8,128)(2,1)} %get-tuple-element.42) | copy-start | bytes 1572868
  100.4 23.4 %collective-permute-start.14 = (bf16[4,256,256]{2,1,0:T(8,128)(2,1)}, bf16[4,256,256]{2,1,0:T(8,128)(2,1)S(1)}, u32[]{:S(2)}, u32[]{:S(2)}) collective-permute-start(bf16[4,256,256]{2,1,0:T(8,128)(2,1)} %get-tuple-element.39), channel_id=1, source_target_pairs={{0,6},{2,0},{4,2},{6,4},{8,14},{10,8},{12,10},{14,12},{16,22},{18,... | collective-permute-start | bytes 1572872 | tf_op jit(solution)/shard_map/ppermute | solution.py:314
  102.4 45.1 %collective-permute-start.15 = (bf16[4,256,256]{2,1,0:T(8,128)(2,1)}, bf16[4,256,256]{2,1,0:T(8,128)(2,1)}, u32[]{:S(2)}, u32[]{:S(2)}) collective-permute-start(bf16[4,256,256]{2,1,0:T(8,128)(2,1)} %get-tuple-element.40), channel_id=1, source_target_pairs={{0,4},{2,6},{4,0},{6,2},{8,12},{10,14},{12,8},{14,10},{16,20},{18,... | collective-permute-start | bytes 1572872 | tf_op jit(solution)/shard_map/ppermute | solution.py:314
  103.3 44.2 %collective-permute-start.16 = (bf16[4,256,256]{2,1,0:T(8,128)(2,1)}, bf16[4,256,256]{2,1,0:T(8,128)(2,1)}, u32[]{:S(2)}, u32[]{:S(2)}) collective-permute-start(bf16[4,256,256]{2,1,0:T(8,128)(2,1)} %get-tuple-element.41), channel_id=1, source_target_pairs={{0,2},{2,4},{4,6},{6,0},{8,10},{10,12},{12,14},{14,8},{16,18},{18,... | collective-permute-start | bytes 1572872 | tf_op jit(solution)/shard_map/ppermute | solution.py:314
  103.9 47.1 %collective-permute-start.20 = (bf16[4,256,256]{2,1,0:T(8,128)(2,1)}, bf16[4,256,256]{2,1,0:T(8,128)(2,1)S(1)}, u32[]{:S(2)}, u32[]{:S(2)}) collective-permute-start(bf16[4,256,256]{2,1,0:T(8,128)(2,1)} %get-tuple-element.43), channel_id=1, source_target_pairs={{0,192},{2,194},{4,196},{6,198},{8,200},{10,202},{12,204},{14,206}... | collective-permute-start | bytes 1572872 | tf_op jit(solution)/shard_map/ppermute | solution.py:315
  106.2 48.3 %collective-permute-start.21 = (bf16[4,256,256]{2,1,0:T(8,128)(2,1)}, bf16[4,256,256]{2,1,0:T(8,128)(2,1)}, u32[]{:S(2)}, u32[]{:S(2)}) collective-permute-start(bf16[4,256,256]{2,1,0:T(8,128)(2,1)} %get-tuple-element.44), channel_id=1, source_target_pairs={{0,128},{2,130},{4,132},{6,134},{8,136},{10,138},{12,140},{14,142}... | collective-permute-start | bytes 1572872 | tf_op jit(solution)/shard_map/ppermute | solution.py:315
  123.8 27.2 %copy-start.9 = (bf16[4,256,256]{2,1,0:T(8,128)(2,1)}, bf16[4,256,256]{2,1,0:T(8,128)(2,1)S(1)}, u32[]{:S(2)}) copy-start(bf16[4,256,256]{2,1,0:T(8,128)(2,1)S(1)} %collective-permute-done.14) | copy-start | bytes 1572868
  123.8 30.7 %collective-permute-start.22 = (bf16[4,256,256]{2,1,0:T(8,128)(2,1)}, bf16[4,256,256]{2,1,0:T(8,128)(2,1)}, u32[]{:S(2)}, u32[]{:S(2)}) collective-permute-start(bf16[4,256,256]{2,1,0:T(8,128)(2,1)} %get-tuple-element.45), channel_id=1, source_target_pairs={{0,64},{2,66},{4,68},{6,70},{8,72},{10,74},{12,76},{14,78},{16,80}... | collective-permute-start | bytes 1572872 | tf_op jit(solution)/shard_map/ppermute | solution.py:315
  140.9 25.2 %all-to-all-start.4 = ((bf16[8,128,256]{2,1,0:T(8,128)(2,1)}), bf16[8,128,256]{2,1,0:T(8,128)(2,1)S(1)}, u32[]{:S(2)}, u32[]{:S(2)}) async-start(bf16[8,128,256]{2,1,0:T(8,128)(2,1)} %broadcast_in_dim.22), calls=%async_computation.4 | async-start | bytes 1048576 | tf_op jit(solution)/shard_map/all_to_all | solution.py:46
  148.9 9.2 %collective-permute-start.17 = (bf16[256,256]{1,0:T(8,128)(2,1)S(1)}, bf16[256,256]{1,0:T(8,128)(2,1)S(1)}, u32[]{:S(2)}, u32[]{:S(2)}) collective-permute-start(bf16[256,256]{1,0:T(8,128)(2,1)S(1)} %get-tuple-element.51), channel_id=1, source_target_pairs={{0,192},{2,194},{4,196},{6,198},{8,200},{10,202},{12,204},{14,206}... | collective-permute-start | bytes 393224 | tf_op jit(solution)/shard_map/ppermute | solution.py:321
  150.5 9.0 %collective-permute-start.19 = (bf16[256,256]{1,0:T(8,128)(2,1)S(1)}, bf16[256,256]{1,0:T(8,128)(2,1)S(1)}, u32[]{:S(2)}, u32[]{:S(2)}) collective-permute-start(bf16[256,256]{1,0:T(8,128)(2,1)S(1)} %get-tuple-element.52), channel_id=1, source_target_pairs={{0,64},{2,66},{4,68},{6,70},{8,72},{10,74},{12,76},{14,78},{16,80}... | collective-permute-start | bytes 393224 | tf_op jit(solution)/shard_map/ppermute | solution.py:321
  151.0 0.8 copy-start.8
  151.8 31.8 %copy-start.2 = (f32[1024,256]{1,0:T(8,128)S(1)}, f32[1024,256]{1,0:T(8,128)}, u32[]{:S(2)}) copy-start(f32[1024,256]{1,0:T(8,128)} %get-tuple-element.49.pre_ref) | copy-start | bytes 3145732
  151.8 7.7 %collective-permute-start.18 = (bf16[256,256]{1,0:T(8,128)(2,1)S(1)}, bf16[256,256]{1,0:T(8,128)(2,1)S(1)}, u32[]{:S(2)}, u32[]{:S(2)}) collective-permute-start(bf16[256,256]{1,0:T(8,128)(2,1)S(1)} %get-tuple-element.53), channel_id=1, source_target_pairs={{0,128},{2,130},{4,132},{6,134},{8,136},{10,138},{12,140},{14,142}... | collective-permute-start | bytes 393224 | tf_op jit(solution)/shard_map/ppermute | solution.py:321
  156.0 5.0 %collective-permute-start.23 = (bf16[256,256]{1,0:T(8,128)(2,1)S(1)}, bf16[256,256]{1,0:T(8,128)(2,1)S(1)}, u32[]{:S(2)}, u32[]{:S(2)}) collective-permute-start(bf16[256,256]{1,0:T(8,128)(2,1)S(1)} %get-tuple-element.54), channel_id=1, source_target_pairs={{0,6},{2,0},{4,2},{6,4},{8,14},{10,8},{12,10},{14,12},{16,22},{18,... | collective-permute-start | bytes 393224 | tf_op jit(solution)/shard_map/ppermute | solution.py:324
  157.3 7.6 %collective-permute-start.25 = (bf16[256,256]{1,0:T(8,128)(2,1)S(1)}, bf16[256,256]{1,0:T(8,128)(2,1)S(1)}, u32[]{:S(2)}, u32[]{:S(2)}) collective-permute-start(bf16[256,256]{1,0:T(8,128)(2,1)S(1)} %get-tuple-element.55), channel_id=1, source_target_pairs={{0,2},{2,4},{4,6},{6,0},{8,10},{10,12},{12,14},{14,8},{16,18},{18,... | collective-permute-start | bytes 393224 | tf_op jit(solution)/shard_map/ppermute | solution.py:324
  158.1 6.8 %collective-permute-start.24 = (bf16[256,256]{1,0:T(8,128)(2,1)S(1)}, bf16[256,256]{1,0:T(8,128)(2,1)S(1)}, u32[]{:S(2)}, u32[]{:S(2)}) collective-permute-start(bf16[256,256]{1,0:T(8,128)(2,1)S(1)} %get-tuple-element.56), channel_id=1, source_target_pairs={{0,4},{2,6},{4,0},{6,2},{8,12},{10,14},{12,8},{14,10},{16,20},{18,... | collective-permute-start | bytes 393224 | tf_op jit(solution)/shard_map/ppermute | solution.py:324

commit v6 on v5

--- a/solution.py
+++ b/solution.py
@@ -257,16 +257,16 @@
     high = column[deep:].reshape(deep * hub, width)
     low_far = [lax.ppermute(low, "dom", ring("x", k)) for k in range(1, nx)]
     high_far = [lax.ppermute(high, "dom", ring("y", k)) for k in range(1, ny)]
+    pieces = swap(pay.reshape(nz, -1, width), columns())
+    low_set = jnp.stack([low] + low_far)
+    high_set = jnp.stack([high] + high_far)
+    low_got = [low_set] + [lax.ppermute(low_set, "dom", ring("y", k)) for k in range(1, ny)]
+    high_got = [high_set] + [lax.ppermute(high_set, "dom", ring("x", k)) for k in range(1, nx)]
     scaled = scale(block_cols, degrees)
     self_part = lax.dot_general(block_cols, w_self, contract, preferred_element_type=jnp.float32)
-    low_set = jnp.stack([low] + low_far)
-    high_set = jnp.stack([high] + high_far)
-
-    low_set, high_set, pay = lax.optimization_barrier((low_set, high_set, pay))
-    low_got = [low_set] + [lax.ppermute(low_set, "dom", ring("y", k)) for k in range(1, ny)]
-    high_got = [high_set] + [lax.ppermute(high_set, "dom", ring("x", k)) for k in range(1, nx)]
-    pieces = swap(pay.reshape(nz, -1, width), columns())
-    pieces = swap(jnp.sum(pieces.astype(jnp.float32), axis=0).reshape(nx * ny, tail, width), planes())
+    chunk = jnp.sum(pieces.astype(jnp.float32), axis=0).astype(jnp.bfloat16)
+    chunks = jnp.broadcast_to(chunk, (nx * ny, *chunk.shape))
+    chunks = swap(chunks, planes())
 
     order = mirror_master.reshape(nx, 2, deep, ny, slots).transpose(0, 3, 1, 2, 4)
     spots = order.reshape(nx * ny * 2, deep * slots) + jnp.repeat(
@@ -309,12 +309,11 @@
     results = edge_call(from_at, to_at, place, *(near(a) for a in (scaled, self_part, spots, chosen, *low_got, *high_got)))
     pre, low_back, high_back = results[0], results[1 : 1 + ny], results[1 + ny :]
 
-    share = jnp.sum(pieces, axis=0).astype(jnp.bfloat16)
+    share = jnp.sum(chunks.astype(jnp.float32), axis=0).astype(jnp.bfloat16)
     low_back, high_back, share = lax.optimization_barrier((low_back, high_back, share))
     low_part = [low_back[0]] + [lax.ppermute(low_back[k], "dom", ring("y", -k)) for k in range(1, ny)]
     high_part = [high_back[0]] + [lax.ppermute(high_back[k], "dom", ring("x", -k)) for k in range(1, nx)]
-    weights = swap(jnp.broadcast_to(share, (nx * ny, *share.shape)), planes()).reshape(-1, width)
-    weights = swap(jnp.broadcast_to(weights, (nz, *weights.shape)), columns()).reshape(parts, tail, width)
+    weights = swap(jnp.broadcast_to(share, (nz, *share.shape)), columns()).reshape(parts, tail, width)
     low_sum = [sum_of([p[k] for p in low_part]) for k in range(nx)]
     high_sum = [sum_of([p[k] for p in high_part]) for k in range(ny)]
     low_sent = [low_sum[0]] + [

time: 186 us -> 187 us (level)
  waiting for transfers between devices: 46.3 us -> 62.1 us
  blocking collectives: 29.9 us -> 17.5 us
  matrix products: 6.47 us -> 3.05 us
  starting transfers between devices: 59.4 us -> 62.2 us
  other arithmetic: 12 us -> 9.47 us
    ppermute x3, waiting for transfers between devices: 0.01 us -> 14.3 us  [on_device(): low_far = [lax.ppermute(low, 'dom', ring('x', k)) for k in range(1, nx)]]
    all_to_all x1 -> x0, blocking collectives: 12.4 us -> none  [swap(): lax.all_to_all(array, 'dom', split_axis=0, concat_axis=0, axis_index_grou...]
    ppermute x3, waiting for transfers between devices: 16.2 us -> 10.1 us  [on_device(): lax.ppermute(low_back[k], 'dom', ring('y', -k))]
    ppermute x3, waiting for transfers between devices: 3.8 us -> 7.91 us  [on_device(): lax.ppermute(high_set, 'dom', ring('x', k))]
    all_to_all x3, waiting for transfers between devices: 0.01 us -> 3.56 us  [swap(): lax.all_to_all(array, 'dom', split_axis=0, concat_axis=0, axis_index_grou...]
    all_to_all x3, starting transfers between devices: 17.1 us -> 14.5 us  [swap(): lax.all_to_all(array, 'dom', split_axis=0, concat_axis=0, axis_index_grou...]
    dot_general x2, matrix products: 3.69 us -> 1.63 us  [scale(): lax.dot_general(cols, w_neigh, contract, preferred_element_type=jnp.float32)]
    ppermute x3, starting transfers between devices: 1.47 us -> 3.53 us  [on_device(): lax.ppermute(high_set, 'dom', ring('x', k))]
  transfers between devices with their start and end apart: 30 -> 30, of which waited for: 12 -> 13; matrix products, arithmetic and copies ran while one was open for 9% -> 8% of each run, Pallas kernels for 13% -> 13%
where the time goes in v6:
time: 187 us
  starting transfers between devices  62.2 us (33%)
  waiting for transfers between devices  62.1 us (33%)
  Pallas kernels  26.8 us (14%)
  blocking collectives  17.5 us (9%)
  other arithmetic  9.47 us (5%)
  local copies, waits for them, and re-layouts  3.67 us (2%)
  matrix products  3.05 us (2%)
    pallas_call x1, Pallas kernels, on_device(): edge_call(from_at, to_at, place, *(near(a) for a in (scaled, self_part, s...  21.5 us
    all_to_all x1, blocking collectives, on_device(): lax.all_to_all(column_sum.reshape(nz, hub, width), 'dom', split_axis=0, c...  17.5 us
    all_to_all x3, starting transfers between devices, swap(): lax.all_to_all(array, 'dom', split_axis=0, concat_axis=0, axis_index_grou...  14.5 us
    ppermute x3, waiting for transfers between devices, on_device(): low_far = [lax.ppermute(low, 'dom', ring('x', k)) for k in range(1, nx)]  14.3 us
    ppermute x3, waiting for transfers between devices, on_device(): lax.ppermute(low_back[k], 'dom', ring('y', -k))  10.1 us
    all_to_all x1, waiting for transfers between devices, on_device(): lax.all_to_all(copies, 'dom', split_axis=0, concat_axis=0, axis_index_gro...  9.51 us
    ppermute x3, starting transfers between devices, on_device(): lax.ppermute(high_back[k], 'dom', ring('x', -k))  9.04 us
    all_to_all x1, starting transfers between devices, on_device(): lax.all_to_all(copies, 'dom', split_axis=0, concat_axis=0, axis_index_gro...  8.47 us
  transfers between devices with their start and end apart: 30, of which 13 were waited for; matrix products, arithmetic and copies ran while one was open for 8% of the time, Pallas kernels for 13%

profile of v6, /device:TPU:2, one launch (start us, length us, event | category | flops | bytes accessed | tf_op | source)
XLA Modules:
  0.0 186.5 jit_solution(930784003665180425)
XLA Ops:
  0.6 0.8 select_convert_fusion.1
  1.5 0.1 collective-permute-start.1
  1.6 1.4 select_convert_fusion
  3.0 0.6 collective-permute-start
  3.5 0.7 slice_convert_fusion
  4.2 1.2 fusion.3
  5.4 0.7 broadcast_in_dim.20
  6.1 8.5 %all-to-all-start = ((bf16[8,64,256]{2,1,0:T(8,128)(2,1)}), bf16[8,64,256]{2,1,0:T(8,128)(2,1)S(1)}, u32[]{:S(2)}, u32[]{:S(2)}) async-start(bf16[8,64,256]{2,1,0:T(8,128)(2,1)} %broadcast_in_dim.20), calls=%async_computation | async-start | bytes 524288 | tf_op jit(solution)/shard_map/all_to_all | solution.py:243
  14.7 0.5 fusion.1
  15.2 0.5 copy-done.11
  15.7 0.5 fusion.2
  16.3 0.8 pad_maximum_fusion.3
  17.1 9.5 %all-to-all-done = bf16[8,64,256]{2,1,0:T(8,128)(2,1)S(1)} async-done(((bf16[8,64,256]{2,1,0:T(8,128)(2,1)}), bf16[8,64,256]{2,1,0:T(8,128)(2,1)S(1)}, u32[]{:S(2)}, u32[]{:S(2)}) %all-to-all-start) | async-done | bytes 262176 | tf_op jit(solution)/shard_map/all_to_all | solution.py:243
  26.7 3.5 %all-to-all-start.1 = ((bf16[8,128,256]{2,1,0:T(8,128)(2,1)}), bf16[8,128,256]{2,1,0:T(8,128)(2,1)S(1)}, u32[]{:S(2)}, u32[]{:S(2)}) async-start(bf16[8,128,256]{2,1,0:T(8,128)(2,1)} %bitcast.14), calls=%async_computation.1 | async-start | bytes 1048576 | tf_op jit(solution)/shard_map/all_to_all | solution.py:46
  31.0 0.1 reshape.94
  31.1 0.1 reshape.95
  31.2 3.1 %collective-permute-start.10 = (bf16[256,256]{1,0:T(8,128)(2,1)S(1)}, bf16[256,256]{1,0:T(8,128)(2,1)S(1)}, u32[]{:S(2)}, u32[]{:S(2)}) collective-permute-start(bf16[256,256]{1,0:T(8,128)(2,1)S(1)} %bitcast.59), channel_id=1, source_target_pairs={{0,6},{2,0},{4,2},{6,4},{8,14},{10,8},{12,10},{14,12},{16,22},{18,... | collective-permute-start | bytes 393224 | tf_op jit(solution)/shard_map/ppermute | solution.py:259
  34.3 0.6 collective-permute-start.9
  34.9 1.0 collective-permute-start.8
  36.0 2.6 %collective-permute-done.10 = bf16[256,256]{1,0:T(8,128)(2,1)S(1)} collective-permute-done((bf16[256,256]{1,0:T(8,128)(2,1)S(1)}, bf16[256,256]{1,0:T(8,128)(2,1)S(1)}, u32[]{:S(2)}, u32[]{:S(2)}) %collective-permute-start.10) | collective-permute-done | bytes 131104 | tf_op jit(solution)/shard_map/ppermute | solution.py:259
  38.6 2.2 %collective-permute-done.9 = bf16[256,256]{1,0:T(8,128)(2,1)S(1)} collective-permute-done((bf16[256,256]{1,0:T(8,128)(2,1)S(1)}, bf16[256,256]{1,0:T(8,128)(2,1)S(1)}, u32[]{:S(2)}, u32[]{:S(2)}) %collective-permute-start.9) | collective-permute-done | bytes 131104 | tf_op jit(solution)/shard_map/ppermute | solution.py:259
  40.9 1.3 collective-permute-done.8
  42.3 0.6 collective-permute-start.13
  42.9 3.6 %all-to-all-done.1 = bf16[8,128,256]{2,1,0:T(8,128)(2,1)S(1)} async-done(((bf16[8,128,256]{2,1,0:T(8,128)(2,1)}), bf16[8,128,256]{2,1,0:T(8,128)(2,1)S(1)}, u32[]{:S(2)}, u32[]{:S(2)}) %all-to-all-start.1) | async-done | bytes 524320 | tf_op jit(solution)/shard_map/all_to_all | solution.py:46
  46.5 1.1 broadcast_in_dim.21
  47.6 7.5 %all-to-all-start.2 = ((bf16[16,128,256]{2,1,0:T(8,128)(2,1)}), bf16[16,128,256]{2,1,0:T(8,128)(2,1)S(1)}, u32[]{:S(2)}, u32[]{:S(2)}) async-start(bf16[16,128,256]{2,1,0:T(8,128)(2,1)} %broadcast_in_dim.21), calls=%async_computation.2 | async-start | bytes 2097152 | tf_op jit(solution)/shard_map/all_to_all | solution.py:46
  55.1 0.2 collective-permute-start.4
  55.3 2.8 %collective-permute-start.3 = (bf16[256,256]{1,0:T(8,128)(2,1)S(1)}, bf16[256,256]{1,0:T(8,128)(2,1)S(1)}, u32[]{:S(2)}, u32[]{:S(2)}) collective-permute-start(bf16[256,256]{1,0:T(8,128)(2,1)S(1)} %bitcast.56), channel_id=1, source_target_pairs={{0,128},{2,130},{4,132},{6,134},{8,136},{10,138},{12,140},{14,142}... | collective-permute-start | bytes 393224 | tf_op jit(solution)/shard_map/ppermute | solution.py:258
  58.1 1.8 collective-permute-start.2
  60.0 3.3 %picks.1.pick_ref = bf16[32,128,256]{2,1,0:T(8,128)(2,1)S(1)} custom-call(s32[32,128]{1,0:T(8,128)S(1)} %broadcast_add_fusion.spot_ref), custom_call_target="tpu_custom_call" | custom-call | tf_op jit(solution)/shard_map/picks/pallas_call | solution.py:275
  63.4 1.5 collective-permute-start.12
  64.9 7.3 %collective-permute-done.4 = bf16[256,256]{1,0:T(8,128)(2,1)S(1)} collective-permute-done((bf16[256,256]{1,0:T(8,128)(2,1)S(1)}, bf16[256,256]{1,0:T(8,128)(2,1)S(1)}, u32[]{:S(2)}, u32[]{:S(2)}) %collective-permute-start.4) | collective-permute-done | bytes 131104 | tf_op jit(solution)/shard_map/ppermute | solution.py:258
  72.2 1.4 collective-permute-start.11
  73.6 2.2 %collective-permute-done.3 = bf16[256,256]{1,0:T(8,128)(2,1)S(1)} collective-permute-done((bf16[256,256]{1,0:T(8,128)(2,1)S(1)}, bf16[256,256]{1,0:T(8,128)(2,1)S(1)}, u32[]{:S(2)}, u32[]{:S(2)}) %collective-permute-start.3) | collective-permute-done | bytes 131104 | tf_op jit(solution)/shard_map/ppermute | solution.py:258
  75.8 4.8 %collective-permute-done.2 = bf16[256,256]{1,0:T(8,128)(2,1)S(1)} collective-permute-done((bf16[256,256]{1,0:T(8,128)(2,1)S(1)}, bf16[256,256]{1,0:T(8,128)(2,1)S(1)}, u32[]{:S(2)}, u32[]{:S(2)}) %collective-permute-start.2) | collective-permute-done | bytes 131104 | tf_op jit(solution)/shard_map/ppermute | solution.py:258
  80.7 1.9 %collective-permute-start.7 = (bf16[4,256,256]{2,1,0:T(8,128)(2,1)S(1)}, bf16[4,256,256]{2,1,0:T(8,128)(2,1)S(1)}, u32[]{:S(2)}, u32[]{:S(2)}) collective-permute-start(bf16[4,256,256]{2,1,0:T(8,128)(2,1)S(1)} %pad_maximum_fusion.1.rest_0_), channel_id=1, source_target_pairs={{0,6},{2,0},{4,2},{6,4},{8,14},{10,8},{12,10},{14,12},{16,22},{18,... | collective-permute-start | bytes 1572872 | tf_op jit(solution)/shard_map/ppermute | solution.py:263
  82.6 0.6 collective-permute-start.6
  83.2 1.1 collective-permute-start.5
  84.3 0.5 fusion.35.self_ref
  84.8 0.5 fusion.own_ref
  85.3 7.9 %collective-permute-done.11.rest_5_ = bf16[4,256,256]{2,1,0:T(8,128)(2,1)S(1)} collective-permute-done((bf16[4,256,256]{2,1,0:T(8,128)(2,1)S(1)}, bf16[4,256,256]{2,1,0:T(8,128)(2,1)S(1)}, u32[]{:S(2)}, u32[]{:S(2)}) %collective-permute-start.11) | collective-permute-done | bytes 524320 | tf_op jit(solution)/shard_map/ppermute | solution.py:264
  93.2 1.8 collective-permute-done.7.rest_3_
  94.9 3.9 %collective-permute-done.5.rest_1_ = bf16[4,256,256]{2,1,0:T(8,128)(2,1)S(1)} collective-permute-done((bf16[4,256,256]{2,1,0:T(8,128)(2,1)S(1)}, bf16[4,256,256]{2,1,0:T(8,128)(2,1)S(1)}, u32[]{:S(2)}, u32[]{:S(2)}) %collective-permute-start.5) | collective-permute-done | bytes 524320 | tf_op jit(solution)/shard_map/ppermute | solution.py:263
  98.9 21.5 %edges.1 = (f32[1024,256]{1,0:T(8,128)}, bf16[4,256,256]{2,1,0:T(8,128)(2,1)}, bf16[4,256,256]{2,1,0:T(8,128)(2,1)}, bf16[4,256,256]{2,1,0:T(8,128)(2,1)}, bf16[...) custom-call(s32[8192]{0:T(1024)S(1)} %get-tuple-element.63.from_ref,, ...), custom_call_target="tpu_custom_call" | custom-call | tf_op jit(solution)/shard_map/edges/pallas_call | solution.py:309
  120.4 0.1 reduce_sum.25
  120.5 0.5 collective-permute-start.14
  121.0 1.3 collective-permute-start.15
  122.4 0.6 collective-permute-start.16
  123.0 5.2 %collective-permute-start.20 = (bf16[4,256,256]{2,1,0:T(8,128)(2,1)}, bf16[4,256,256]{2,1,0:T(8,128)(2,1)S(1)}, u32[]{:S(2)}, u32[]{:S(2)}) collective-permute-start(bf16[4,256,256]{2,1,0:T(8,128)(2,1)} %get-tuple-element.37), channel_id=1, source_target_pairs={{0,192},{2,194},{4,196},{6,198},{8,200},{10,202},{12,204},{14,206}... | collective-permute-start | bytes 1572872 | tf_op jit(solution)/shard_map/ppermute | solution.py:315
  128.1 10.1 %collective-permute-done.14 = bf16[4,256,256]{2,1,0:T(8,128)(2,1)S(1)} collective-permute-done((bf16[4,256,256]{2,1,0:T(8,128)(2,1)}, bf16[4,256,256]{2,1,0:T(8,128)(2,1)S(1)}, u32[]{:S(2)}, u32[]{:S(2)}) %collective-permute-start.14) | collective-permute-done | bytes 524320 | tf_op jit(solution)/shard_map/ppermute | solution.py:314
  138.3 3.9 %collective-permute-start.22 = (bf16[4,256,256]{2,1,0:T(8,128)(2,1)}, bf16[4,256,256]{2,1,0:T(8,128)(2,1)}, u32[]{:S(2)}, u32[]{:S(2)}) collective-permute-start(bf16[4,256,256]{2,1,0:T(8,128)(2,1)} %get-tuple-element.39), channel_id=1, source_target_pairs={{0,64},{2,66},{4,68},{6,70},{8,72},{10,74},{12,76},{14,78},{16,80}... | collective-permute-start | bytes 1572872 | tf_op jit(solution)/shard_map/ppermute | solution.py:315
  142.1 0.8 broadcast_in_dim.22
  143.0 3.5 %all-to-all-start.3 = ((bf16[8,128,256]{2,1,0:T(8,128)(2,1)}), bf16[8,128,256]{2,1,0:T(8,128)(2,1)S(1)}, u32[]{:S(2)}, u32[]{:S(2)}) async-start(bf16[8,128,256]{2,1,0:T(8,128)(2,1)} %broadcast_in_dim.22), calls=%async_computation.3 | async-start | bytes 1048576 | tf_op jit(solution)/shard_map/all_to_all | solution.py:46
  146.5 1.4 fusion.10
  148.0 2.0 %collective-permute-start.19 = (bf16[256,256]{1,0:T(8,128)(2,1)S(1)}, bf16[256,256]{1,0:T(8,128)(2,1)S(1)}, u32[]{:S(2)}, u32[]{:S(2)}) collective-permute-start(bf16[256,256]{1,0:T(8,128)(2,1)S(1)} %get-tuple-element.46), channel_id=1, source_target_pairs={{0,64},{2,66},{4,68},{6,70},{8,72},{10,74},{12,76},{14,78},{16,80}... | collective-permute-start | bytes 393224 | tf_op jit(solution)/shard_map/ppermute | solution.py:320
  150.0 3.2 %collective-permute-start.18 = (bf16[256,256]{1,0:T(8,128)(2,1)S(1)}, bf16[256,256]{1,0:T(8,128)(2,1)S(1)}, u32[]{:S(2)}, u32[]{:S(2)}) collective-permute-start(bf16[256,256]{1,0:T(8,128)(2,1)S(1)} %get-tuple-element.47), channel_id=1, source_target_pairs={{0,128},{2,130},{4,132},{6,134},{8,136},{10,138},{12,140},{14,142}... | collective-permute-start | bytes 393224 | tf_op jit(solution)/shard_map/ppermute | solution.py:320
  153.2 1.4 fusion.13
  154.6 3.6 %collective-permute-start.23 = (bf16[256,256]{1,0:T(8,128)(2,1)S(1)}, bf16[256,256]{1,0:T(8,128)(2,1)S(1)}, u32[]{:S(2)}, u32[]{:S(2)}) collective-permute-start(bf16[256,256]{1,0:T(8,128)(2,1)S(1)} %get-tuple-element.48), channel_id=1, source_target_pairs={{0,6},{2,0},{4,2},{6,4},{8,14},{10,8},{12,10},{14,12},{16,22},{18,... | collective-permute-start | bytes 393224 | tf_op jit(solution)/shard_map/ppermute | solution.py:323
  158.3 1.6 collective-permute-start.24
  159.8 1.2 fusion.9
  161.1 4.8 %collective-permute-done.25 = bf16[256,256]{1,0:T(8,128)(2,1)S(1)} collective-permute-done((bf16[256,256]{1,0:T(8,128)(2,1)S(1)}, bf16[256,256]{1,0:T(8,128)(2,1)S(1)}, u32[]{:S(2)}, u32[]{:S(2)}) %collective-permute-start.25) | collective-permute-done | bytes 131104 | tf_op jit(solution)/shard_map/ppermute | solution.py:323
  165.9 1.1 fusion.6
  167.0 17.5 %all_to_all.25.home_ref = bf16[8,64,256]{2,1,0:T(8,128)(2,1)S(1)} all-to-all(bf16[8,64,256]{2,1,0:T(8,128)(2,1)S(1)} %bitcast.54), channel_id=1, replica_groups={{0,8,16,24,32,40,48,56},{2,10,18,26,34,42,50,58},{4,12,20,28,36,44,52,6..., dimensions={0} | all-to-all | bytes 524288 | tf_op jit(solution)/shard_map/all_to_all | solution.py:327
  184.5 2.0 %final.1 = (bf16[1024,256]{1,0:T(8,128)(2,1)}, f32[256,512]{1,0:T(8,128)}, f32[256,512]{1,0:T(8,128)}) custom-call(bf16[8,64,256]{2,1,0:T(8,128)(2,1)S(1)} %all_to_all.25.home_ref, f32[1024,256]{1,0:T(8,128)S(1)} %copy-done.1, bf16[128,8,256]{2,1,0:T(8,128)(2,1)S(1)} %bitcast.53), custom_call_target="tpu_custom_call" | custom-call | tf_op jit(solution)/shard_map/final/pallas_call | solution.py:335
  (64 shorter events, 0.9 us)
Async XLA Ops:
  0.6 14.1 %copy-start = (bf16[1024,256]{1,0:T(8,128)(2,1)S(1)}, bf16[1024,256]{1,0:T(8,128)(2,1)}, u32[]{:S(2)}) copy-start(bf16[1024,256]{1,0:T(8,128)(2,1)} %param.11) | copy-start | bytes 1572868
  1.5 2.7 %collective-permute-start.1 = (bf16[64,256]{1,0:T(8,128)(2,1)S(1)}, bf16[64,256]{1,0:T(8,128)(2,1)S(1)}, u32[]{:S(2)}, u32[]{:S(2)}) collective-permute-start(bf16[64,256]{1,0:T(8,128)(2,1)S(1)} %select_convert_fusion.1), channel_id=1, source_target_pairs={{0,1},{1,0},{2,3},{3,2},{4,5},{5,4},{6,7},{7,6},{8,9},{9,8},{10,11... | collective-permute-start | bytes 98312 | tf_op jit(solution)/shard_map/ppermute | solution.py:234
  3.0 11.6 %collective-permute-start = (bf16[1024,256]{1,0:T(8,128)(2,1)S(1)}, bf16[1024,256]{1,0:T(8,128)(2,1)S(1)}, u32[]{:S(2)}, u32[]{:S(2)}) collective-permute-start(bf16[1024,256]{1,0:T(8,128)(2,1)S(1)} %select_convert_fusion), channel_id=1, source_target_pairs={{0,1},{1,0},{2,3},{3,2},{4,5},{5,4},{6,7},{7,6},{8,9},{9,8},{10,11... | collective-permute-start | bytes 1572872 | tf_op jit(solution)/shard_map/ppermute | solution.py:234
  6.1 20.5 %all-to-all-start = ((bf16[8,64,256]{2,1,0:T(8,128)(2,1)}), bf16[8,64,256]{2,1,0:T(8,128)(2,1)S(1)}, u32[]{:S(2)}, u32[]{:S(2)}) async-start(bf16[8,64,256]{2,1,0:T(8,128)(2,1)} %broadcast_in_dim.20), calls=%async_computation | async-start | bytes 524288 | tf_op jit(solution)/shard_map/all_to_all | solution.py:243
  14.6 1.1 copy-start.11
  14.7 1.5 copy-start.2
  16.2 14.7 %copy-start.9 = (s32[4096]{0:T(1024)S(1)}, s32[4096]{0:T(1024)}, u32[]{:S(2)}) copy-start(s32[4096]{0:T(1024)} %param.20) | copy-start | bytes 49156
  16.2 19.7 %copy-start.7 = (s32[8192]{0:T(1024)S(1)}, s32[8192]{0:T(1024)}, u32[]{:S(2)}) copy-start(s32[8192]{0:T(1024)} %param.17) | copy-start | bytes 98308
  16.3 19.7 %copy-start.8 = (s32[8192]{0:T(1024)S(1)}, s32[8192]{0:T(1024)}, u32[]{:S(2)}) copy-start(s32[8192]{0:T(1024)} %param.18) | copy-start | bytes 98308
  26.7 19.8 %all-to-all-start.1 = ((bf16[8,128,256]{2,1,0:T(8,128)(2,1)}), bf16[8,128,256]{2,1,0:T(8,128)(2,1)S(1)}, u32[]{:S(2)}, u32[]{:S(2)}) async-start(bf16[8,128,256]{2,1,0:T(8,128)(2,1)} %bitcast.14), calls=%async_computation.1 | async-start | bytes 1048576 | tf_op jit(solution)/shard_map/all_to_all | solution.py:46
  31.2 7.4 %collective-permute-start.10 = (bf16[256,256]{1,0:T(8,128)(2,1)S(1)}, bf16[256,256]{1,0:T(8,128)(2,1)S(1)}, u32[]{:S(2)}, u32[]{:S(2)}) collective-permute-start(bf16[256,256]{1,0:T(8,128)(2,1)S(1)} %bitcast.59), channel_id=1, source_target_pairs={{0,6},{2,0},{4,2},{6,4},{8,14},{10,8},{12,10},{14,12},{16,22},{18,... | collective-permute-start | bytes 393224 | tf_op jit(solution)/shard_map/ppermute | solution.py:259
  34.3 6.6 %collective-permute-start.9 = (bf16[256,256]{1,0:T(8,128)(2,1)S(1)}, bf16[256,256]{1,0:T(8,128)(2,1)S(1)}, u32[]{:S(2)}, u32[]{:S(2)}) collective-permute-start(bf16[256,256]{1,0:T(8,128)(2,1)S(1)} %bitcast.60), channel_id=1, source_target_pairs={{0,4},{2,6},{4,0},{6,2},{8,12},{10,14},{12,8},{14,10},{16,20},{18,... | collective-permute-start | bytes 393224 | tf_op jit(solution)/shard_map/ppermute | solution.py:259
  34.9 7.2 %collective-permute-start.8 = (bf16[256,256]{1,0:T(8,128)(2,1)S(1)}, bf16[256,256]{1,0:T(8,128)(2,1)S(1)}, u32[]{:S(2)}, u32[]{:S(2)}) collective-permute-start(bf16[256,256]{1,0:T(8,128)(2,1)S(1)} %bitcast.61), channel_id=1, source_target_pairs={{0,2},{2,4},{4,6},{6,0},{8,10},{10,12},{12,14},{14,8},{16,18},{18,... | collective-permute-start | bytes 393224 | tf_op jit(solution)/shard_map/ppermute | solution.py:259
  42.3 17.7 %copy-start.10 = (s32[1024]{0:T(1024)S(1)}, s32[1024]{0:T(1024)}, u32[]{:S(2)}) copy-start(s32[1024]{0:T(1024)} %param.21) | copy-start | bytes 12292
  42.3 40.9 %collective-permute-start.13 = (bf16[4,256,256]{2,1,0:T(8,128)(2,1)S(1)}, bf16[4,256,256]{2,1,0:T(8,128)(2,1)S(1)}, u32[]{:S(2)}, u32[]{:S(2)}) collective-permute-start(bf16[4,256,256]{2,1,0:T(8,128)(2,1)S(1)} %pad_maximum_fusion.2.rest_4_), channel_id=1, source_target_pairs={{0,192},{2,194},{4,196},{6,198},{8,200},{10,202},{12,204},{14,206}... | collective-permute-start | bytes 1572872 | tf_op jit(solution)/shard_map/ppermute | solution.py:264
  47.6 72.7 %all-to-all-start.2 = ((bf16[16,128,256]{2,1,0:T(8,128)(2,1)}), bf16[16,128,256]{2,1,0:T(8,128)(2,1)S(1)}, u32[]{:S(2)}, u32[]{:S(2)}) async-start(bf16[16,128,256]{2,1,0:T(8,128)(2,1)} %broadcast_in_dim.21), calls=%async_computation.2 | async-start | bytes 2097152 | tf_op jit(solution)/shard_map/all_to_all | solution.py:46
  55.1 29.2 %copy-start.3 = (bf16[1024,256]{1,0:T(8,128)(2,1)S(1)}, bf16[1024,256]{1,0:T(8,128)(2,1)}, u32[]{:S(2)}) copy-start(bf16[1024,256]{1,0:T(8,128)(2,1)} %copy-done.2) | copy-start | bytes 1572868
  55.1 29.2 %copy-start.12 = (bf16[256,512]{1,0:T(8,128)(2,1)S(1)}, bf16[256,512]{1,0:T(8,128)(2,1)}, u32[]{:S(2)}) copy-start(bf16[256,512]{1,0:T(8,128)(2,1)} %param.15) | copy-start | bytes 786436
  55.1 17.0 %collective-permute-start.4 = (bf16[256,256]{1,0:T(8,128)(2,1)S(1)}, bf16[256,256]{1,0:T(8,128)(2,1)S(1)}, u32[]{:S(2)}, u32[]{:S(2)}) collective-permute-start(bf16[256,256]{1,0:T(8,128)(2,1)S(1)} %bitcast.55), channel_id=1, source_target_pairs={{0,192},{2,194},{4,196},{6,198},{8,200},{10,202},{12,204},{14,206}... | collective-permute-start | bytes 393224 | tf_op jit(solution)/shard_map/ppermute | solution.py:258
  55.3 20.5 %collective-permute-start.3 = (bf16[256,256]{1,0:T(8,128)(2,1)S(1)}, bf16[256,256]{1,0:T(8,128)(2,1)S(1)}, u32[]{:S(2)}, u32[]{:S(2)}) collective-permute-start(bf16[256,256]{1,0:T(8,128)(2,1)S(1)} %bitcast.56), channel_id=1, source_target_pairs={{0,128},{2,130},{4,132},{6,134},{8,136},{10,138},{12,140},{14,142}... | collective-permute-start | bytes 393224 | tf_op jit(solution)/shard_map/ppermute | solution.py:258
  58.1 22.5 %collective-permute-start.2 = (bf16[256,256]{1,0:T(8,128)(2,1)S(1)}, bf16[256,256]{1,0:T(8,128)(2,1)S(1)}, u32[]{:S(2)}, u32[]{:S(2)}) collective-permute-start(bf16[256,256]{1,0:T(8,128)(2,1)S(1)} %bitcast.57), channel_id=1, source_target_pairs={{0,64},{2,66},{4,68},{6,70},{8,72},{10,74},{12,76},{14,78},{16,80}... | collective-permute-start | bytes 393224 | tf_op jit(solution)/shard_map/ppermute | solution.py:258
  63.3 21.5 %copy-start.13 = (bf16[256,512]{1,0:T(8,128)(2,1)S(1)}, bf16[256,512]{1,0:T(8,128)(2,1)}, u32[]{:S(2)}) copy-start(bf16[256,512]{1,0:T(8,128)(2,1)} %param.16) | copy-start | bytes 786436
  63.4 21.9 %collective-permute-start.12 = (bf16[4,256,256]{2,1,0:T(8,128)(2,1)S(1)}, bf16[4,256,256]{2,1,0:T(8,128)(2,1)S(1)}, u32[]{:S(2)}, u32[]{:S(2)}) collective-permute-start(bf16[4,256,256]{2,1,0:T(8,128)(2,1)S(1)} %pad_maximum_fusion.2.rest_4_), channel_id=1, source_target_pairs={{0,128},{2,130},{4,132},{6,134},{8,136},{10,138},{12,140},{14,142}... | collective-permute-start | bytes 1572872 | tf_op jit(solution)/shard_map/ppermute | solution.py:264
  72.2 21.0 %collective-permute-start.11 = (bf16[4,256,256]{2,1,0:T(8,128)(2,1)S(1)}, bf16[4,256,256]{2,1,0:T(8,128)(2,1)S(1)}, u32[]{:S(2)}, u32[]{:S(2)}) collective-permute-start(bf16[4,256,256]{2,1,0:T(8,128)(2,1)S(1)} %pad_maximum_fusion.2.rest_4_), channel_id=1, source_target_pairs={{0,64},{2,66},{4,68},{6,70},{8,72},{10,74},{12,76},{14,78},{16,80}... | collective-permute-start | bytes 1572872 | tf_op jit(solution)/shard_map/ppermute | solution.py:264
  80.7 14.2 %collective-permute-start.7 = (bf16[4,256,256]{2,1,0:T(8,128)(2,1)S(1)}, bf16[4,256,256]{2,1,0:T(8,128)(2,1)S(1)}, u32[]{:S(2)}, u32[]{:S(2)}) collective-permute-start(bf16[4,256,256]{2,1,0:T(8,128)(2,1)S(1)} %pad_maximum_fusion.1.rest_0_), channel_id=1, source_target_pairs={{0,6},{2,0},{4,2},{6,4},{8,14},{10,8},{12,10},{14,12},{16,22},{18,... | collective-permute-start | bytes 1572872 | tf_op jit(solution)/shard_map/ppermute | solution.py:263
  82.6 12.4 %collective-permute-start.6 = (bf16[4,256,256]{2,1,0:T(8,128)(2,1)S(1)}, bf16[4,256,256]{2,1,0:T(8,128)(2,1)S(1)}, u32[]{:S(2)}, u32[]{:S(2)}) collective-permute-start(bf16[4,256,256]{2,1,0:T(8,128)(2,1)S(1)} %pad_maximum_fusion.1.rest_0_), channel_id=1, source_target_pairs={{0,4},{2,6},{4,0},{6,2},{8,12},{10,14},{12,8},{14,10},{16,20},{18,... | collective-permute-start | bytes 1572872 | tf_op jit(solution)/shard_map/ppermute | solution.py:263
  83.2 15.7 %collective-permute-start.5 = (bf16[4,256,256]{2,1,0:T(8,128)(2,1)S(1)}, bf16[4,256,256]{2,1,0:T(8,128)(2,1)S(1)}, u32[]{:S(2)}, u32[]{:S(2)}) collective-permute-start(bf16[4,256,256]{2,1,0:T(8,128)(2,1)S(1)} %pad_maximum_fusion.1.rest_0_), channel_id=1, source_target_pairs={{0,2},{2,4},{4,6},{6,0},{8,10},{10,12},{12,14},{14,8},{16,18},{18,... | collective-permute-start | bytes 1572872 | tf_op jit(solution)/shard_map/ppermute | solution.py:263
  120.4 26.2 %copy-start.5 = (bf16[4,256,256]{2,1,0:T(8,128)(2,1)S(1)}, bf16[4,256,256]{2,1,0:T(8,128)(2,1)}, u32[]{:S(2)}) copy-start(bf16[4,256,256]{2,1,0:T(8,128)(2,1)} %get-tuple-element.32) | copy-start | bytes 1572868
  120.4 32.9 %copy-start.4 = (bf16[4,256,256]{2,1,0:T(8,128)(2,1)S(1)}, bf16[4,256,256]{2,1,0:T(8,128)(2,1)}, u32[]{:S(2)}) copy-start(bf16[4,256,256]{2,1,0:T(8,128)(2,1)} %get-tuple-element.36) | copy-start | bytes 1572868
  120.5 17.8 %collective-permute-start.14 = (bf16[4,256,256]{2,1,0:T(8,128)(2,1)}, bf16[4,256,256]{2,1,0:T(8,128)(2,1)S(1)}, u32[]{:S(2)}, u32[]{:S(2)}) collective-permute-start(bf16[4,256,256]{2,1,0:T(8,128)(2,1)} %get-tuple-element.33), channel_id=1, source_target_pairs={{0,6},{2,0},{4,2},{6,4},{8,14},{10,8},{12,10},{14,12},{16,22},{18,... | collective-permute-start | bytes 1572872 | tf_op jit(solution)/shard_map/ppermute | solution.py:314
  121.0 25.5 %collective-permute-start.15 = (bf16[4,256,256]{2,1,0:T(8,128)(2,1)}, bf16[4,256,256]{2,1,0:T(8,128)(2,1)}, u32[]{:S(2)}, u32[]{:S(2)}) collective-permute-start(bf16[4,256,256]{2,1,0:T(8,128)(2,1)} %get-tuple-element.34), channel_id=1, source_target_pairs={{0,4},{2,6},{4,0},{6,2},{8,12},{10,14},{12,8},{14,10},{16,20},{18,... | collective-permute-start | bytes 1572872 | tf_op jit(solution)/shard_map/ppermute | solution.py:314
  122.4 24.1 %collective-permute-start.16 = (bf16[4,256,256]{2,1,0:T(8,128)(2,1)}, bf16[4,256,256]{2,1,0:T(8,128)(2,1)}, u32[]{:S(2)}, u32[]{:S(2)}) collective-permute-start(bf16[4,256,256]{2,1,0:T(8,128)(2,1)} %get-tuple-element.35), channel_id=1, source_target_pairs={{0,2},{2,4},{4,6},{6,0},{8,10},{10,12},{12,14},{14,8},{16,18},{18,... | collective-permute-start | bytes 1572872 | tf_op jit(solution)/shard_map/ppermute | solution.py:314
  123.0 27.1 %collective-permute-start.20 = (bf16[4,256,256]{2,1,0:T(8,128)(2,1)}, bf16[4,256,256]{2,1,0:T(8,128)(2,1)S(1)}, u32[]{:S(2)}, u32[]{:S(2)}) collective-permute-start(bf16[4,256,256]{2,1,0:T(8,128)(2,1)} %get-tuple-element.37), channel_id=1, source_target_pairs={{0,192},{2,194},{4,196},{6,198},{8,200},{10,202},{12,204},{14,206}... | collective-permute-start | bytes 1572872 | tf_op jit(solution)/shard_map/ppermute | solution.py:315
  128.1 25.1 %collective-permute-start.21 = (bf16[4,256,256]{2,1,0:T(8,128)(2,1)}, bf16[4,256,256]{2,1,0:T(8,128)(2,1)}, u32[]{:S(2)}, u32[]{:S(2)}) collective-permute-start(bf16[4,256,256]{2,1,0:T(8,128)(2,1)} %get-tuple-element.38), channel_id=1, source_target_pairs={{0,128},{2,130},{4,132},{6,134},{8,136},{10,138},{12,140},{14,142}... | collective-permute-start | bytes 1572872 | tf_op jit(solution)/shard_map/ppermute | solution.py:315
  138.3 11.8 %copy-start.6 = (bf16[4,256,256]{2,1,0:T(8,128)(2,1)}, bf16[4,256,256]{2,1,0:T(8,128)(2,1)S(1)}, u32[]{:S(2)}) copy-start(bf16[4,256,256]{2,1,0:T(8,128)(2,1)S(1)} %collective-permute-done.14) | copy-start | bytes 1572868
  138.3 15.0 %collective-permute-start.22 = (bf16[4,256,256]{2,1,0:T(8,128)(2,1)}, bf16[4,256,256]{2,1,0:T(8,128)(2,1)}, u32[]{:S(2)}, u32[]{:S(2)}) collective-permute-start(bf16[4,256,256]{2,1,0:T(8,128)(2,1)} %get-tuple-element.39), channel_id=1, source_target_pairs={{0,64},{2,66},{4,68},{6,70},{8,72},{10,74},{12,76},{14,78},{16,80}... | collective-permute-start | bytes 1572872 | tf_op jit(solution)/shard_map/ppermute | solution.py:315
  143.0 24.0 %all-to-all-start.3 = ((bf16[8,128,256]{2,1,0:T(8,128)(2,1)}), bf16[8,128,256]{2,1,0:T(8,128)(2,1)S(1)}, u32[]{:S(2)}, u32[]{:S(2)}) async-start(bf16[8,128,256]{2,1,0:T(8,128)(2,1)} %broadcast_in_dim.22), calls=%async_computation.3 | async-start | bytes 1048576 | tf_op jit(solution)/shard_map/all_to_all | solution.py:46
  147.9 10.4 %collective-permute-start.17 = (bf16[256,256]{1,0:T(8,128)(2,1)S(1)}, bf16[256,256]{1,0:T(8,128)(2,1)S(1)}, u32[]{:S(2)}, u32[]{:S(2)}) collective-permute-start(bf16[256,256]{1,0:T(8,128)(2,1)S(1)} %get-tuple-element.45), channel_id=1, source_target_pairs={{0,192},{2,194},{4,196},{6,198},{8,200},{10,202},{12,204},{14,206}... | collective-permute-start | bytes 393224 | tf_op jit(solution)/shard_map/ppermute | solution.py:320
  148.0 11.8 %collective-permute-start.19 = (bf16[256,256]{1,0:T(8,128)(2,1)S(1)}, bf16[256,256]{1,0:T(8,128)(2,1)S(1)}, u32[]{:S(2)}, u32[]{:S(2)}) collective-permute-start(bf16[256,256]{1,0:T(8,128)(2,1)S(1)} %get-tuple-element.46), channel_id=1, source_target_pairs={{0,64},{2,66},{4,68},{6,70},{8,72},{10,74},{12,76},{14,78},{16,80}... | collective-permute-start | bytes 393224 | tf_op jit(solution)/shard_map/ppermute | solution.py:320
  150.0 34.5 %copy-start.1 = (f32[1024,256]{1,0:T(8,128)S(1)}, f32[1024,256]{1,0:T(8,128)}, u32[]{:S(2)}) copy-start(f32[1024,256]{1,0:T(8,128)} %get-tuple-element.43.pre_ref) | copy-start | bytes 3145732
  150.0 9.8 %collective-permute-start.18 = (bf16[256,256]{1,0:T(8,128)(2,1)S(1)}, bf16[256,256]{1,0:T(8,128)(2,1)S(1)}, u32[]{:S(2)}, u32[]{:S(2)}) collective-permute-start(bf16[256,256]{1,0:T(8,128)(2,1)S(1)} %get-tuple-element.47), channel_id=1, source_target_pairs={{0,128},{2,130},{4,132},{6,134},{8,136},{10,138},{12,140},{14,142}... | collective-permute-start | bytes 393224 | tf_op jit(solution)/shard_map/ppermute | solution.py:320
  154.6 6.4 %collective-permute-start.23 = (bf16[256,256]{1,0:T(8,128)(2,1)S(1)}, bf16[256,256]{1,0:T(8,128)(2,1)S(1)}, u32[]{:S(2)}, u32[]{:S(2)}) collective-permute-start(bf16[256,256]{1,0:T(8,128)(2,1)S(1)} %get-tuple-element.48), channel_id=1, source_target_pairs={{0,6},{2,0},{4,2},{6,4},{8,14},{10,8},{12,10},{14,12},{16,22},{18,... | collective-permute-start | bytes 393224 | tf_op jit(solution)/shard_map/ppermute | solution.py:323
  158.3 7.6 %collective-permute-start.25 = (bf16[256,256]{1,0:T(8,128)(2,1)S(1)}, bf16[256,256]{1,0:T(8,128)(2,1)S(1)}, u32[]{:S(2)}, u32[]{:S(2)}) collective-permute-start(bf16[256,256]{1,0:T(8,128)(2,1)S(1)} %get-tuple-element.49), channel_id=1, source_target_pairs={{0,2},{2,4},{4,6},{6,0},{8,10},{10,12},{12,14},{14,8},{16,18},{18,... | collective-permute-start | bytes 393224 | tf_op jit(solution)/shard_map/ppermute | solution.py:323
  158.3 7.6 %collective-permute-start.24 = (bf16[256,256]{1,0:T(8,128)(2,1)S(1)}, bf16[256,256]{1,0:T(8,128)(2,1)S(1)}, u32[]{:S(2)}, u32[]{:S(2)}) collective-permute-start(bf16[256,256]{1,0:T(8,128)(2,1)S(1)} %get-tuple-element.50), channel_id=1, source_target_pairs={{0,4},{2,6},{4,0},{6,2},{8,12},{10,14},{12,8},{14,10},{16,20},{18,... | collective-permute-start | bytes 393224 | tf_op jit(solution)/shard_map/ppermute | solution.py:323

commit v7 on v6

--- a/solution.py
+++ b/solution.py
@@ -18,6 +18,10 @@
 
 def near(array):
     return pltpu.with_memory_space_constraint(array, pltpu.VMEM)
+
+
+def far(array):
+    return pltpu.with_memory_space_constraint(array, pltpu.HBM)
 
 
 def ring(axis, shift):
@@ -303,14 +307,13 @@
         out_specs=[VMEM] * (1 + nx + ny),
         scratch_shapes=[pltpu.VMEM((lanes, LANES), jnp.float32)]
         + [pltpu.VMEM((lanes + SUB * halves, LANES), jnp.float32) for _ in range(CHAINS)],
-        compiler_params=pltpu.CompilerParams(vmem_limit_bytes=34 << 20),
+        compiler_params=pltpu.CompilerParams(vmem_limit_bytes=42 << 20),
         name="edges",
     )
-    results = edge_call(from_at, to_at, place, *(near(a) for a in (scaled, self_part, spots, chosen, *low_got, *high_got)))
+    results = edge_call(from_at, to_at, place, far(scaled), far(self_part), near(spots), near(chosen), *low_got, *high_got)
     pre, low_back, high_back = results[0], results[1 : 1 + ny], results[1 + ny :]
 
     share = jnp.sum(chunks.astype(jnp.float32), axis=0).astype(jnp.bfloat16)
-    low_back, high_back, share = lax.optimization_barrier((low_back, high_back, share))
     low_part = [low_back[0]] + [lax.ppermute(low_back[k], "dom", ring("y", -k)) for k in range(1, ny)]
     high_part = [high_back[0]] + [lax.ppermute(high_back[k], "dom", ring("x", -k)) for k in range(1, nx)]
     weights = swap(jnp.broadcast_to(share, (nz, *share.shape)), columns()).reshape(parts, tail, width)

time: 187 us -> 180 us (0.963)
  waiting for transfers between devices: 62.1 us -> 28.7 us
  starting transfers between devices: 62.2 us -> 79.8 us
  other arithmetic: 9.47 us -> 12.9 us
  matrix products: 3.05 us -> 6.17 us
    all_to_all x3, starting transfers between devices: 14.5 us -> 29.8 us  [swap(): lax.all_to_all(array, 'dom', split_axis=0, concat_axis=0, axis_index_grou...]
    ppermute x3, waiting for transfers between devices: 7.91 us -> 0.01 us  [on_device(): lax.ppermute(high_set, 'dom', ring('x', k))]
    ppermute x3, waiting for transfers between devices: 14.3 us -> 8.59 us  [on_device(): low_far = [lax.ppermute(low, 'dom', ring('x', k)) for k in range(1, nx)]]
    ppermute x3, waiting for transfers between devices: 6.2 us -> 0.5 us  [on_device(): high_far = [lax.ppermute(high, 'dom', ring('y', k)) for k in range(1, ny)]]
    ppermute x3, waiting for transfers between devices: 10.1 us -> 4.5 us  [on_device(): lax.ppermute(low_back[k], 'dom', ring('y', -k))]
    ppermute x3, waiting for transfers between devices: 5.71 us -> 0.13 us  [on_device(): lax.ppermute(low_set, 'dom', ring('y', k))]
    all_to_all x3, waiting for transfers between devices: 3.56 us -> 0.01 us  [swap(): lax.all_to_all(array, 'dom', split_axis=0, concat_axis=0, axis_index_grou...]
    dot_general x1, matrix products: 0.46 us -> 2.77 us  [on_device(): lax.dot_general(block_cols, w_self, contract, preferred_element_type=jnp....]
  transfers between devices with their start and end apart: 30 -> 30, of which waited for: 13 -> 8; matrix products, arithmetic and copies ran while one was open for 8% -> 11% of each run, Pallas kernels for 13% -> 14%
where the time goes in v7:
time: 180 us; the launch traced here: 179 us
  starting transfers between devices  79.8 us (44%)
  waiting for transfers between devices  28.7 us (16%)
  Pallas kernels  27.5 us (15%)
  blocking collectives  17.5 us (10%)
  other arithmetic  12.9 us (7%)
  matrix products  6.17 us (3%)
  local copies, waits for them, and re-layouts  4.74 us (3%)
    all_to_all x3, starting transfers between devices, swap(): lax.all_to_all(array, 'dom', split_axis=0, concat_axis=0, axis_index_grou...  29.8 us
    pallas_call x1, Pallas kernels, on_device(): edge_call(from_at, to_at, place, far(scaled), far(self_part), near(spots)...  22.2 us
    all_to_all x1, blocking collectives, on_device(): lax.all_to_all(column_sum.reshape(nz, hub, width), 'dom', split_axis=0, c...  17.5 us
    ppermute x3, starting transfers between devices, on_device(): lax.ppermute(high_back[k], 'dom', ring('x', -k))  9.87 us
    all_to_all x1, waiting for transfers between devices, on_device(): lax.all_to_all(copies, 'dom', split_axis=0, concat_axis=0, axis_index_gro...  9.57 us
    ppermute x3, waiting for transfers between devices, on_device(): low_far = [lax.ppermute(low, 'dom', ring('x', k)) for k in range(1, nx)]  8.59 us
    all_to_all x1, starting transfers between devices, on_device(): lax.all_to_all(copies, 'dom', split_axis=0, concat_axis=0, axis_index_gro...  8.47 us
    ppermute x3, starting transfers between devices, on_device(): lax.ppermute(high_sum[k].astype(jnp.bfloat16), 'dom', ring('y', -k))  5.18 us
  transfers between devices with their start and end apart: 30, of which 8 were waited for; matrix products, arithmetic and copies ran while one was open for 11% of the time, Pallas kernels for 14%

profile of v7, /device:TPU:2, one launch (start us, length us, event | category | flops | bytes accessed | tf_op | source)
XLA Modules:
  0.0 179.0 jit_solution(5212937017764851948)
XLA Ops:
  0.7 0.8 select_convert_fusion.1
  1.5 0.1 collective-permute-start.1
  1.6 0.7 slice_convert_fusion
  2.3 0.5 collective-permute-done.1
  2.8 1.2 fusion.3
  4.0 0.7 broadcast_in_dim.20
  4.7 8.5 %all-to-all-start = ((bf16[8,64,256]{2,1,0:T(8,128)(2,1)}), bf16[8,64,256]{2,1,0:T(8,128)(2,1)S(1)}, u32[]{:S(2)}, u32[]{:S(2)}) async-start(bf16[8,64,256]{2,1,0:T(8,128)(2,1)} %broadcast_in_dim.20), calls=%async_computation | async-start | bytes 524288 | tf_op jit(solution)/shard_map/all_to_all | solution.py:247
  13.2 1.4 select_convert_fusion
  14.5 0.1 collective-permute-start
  15.4 0.1 add.180
  15.5 0.1 reshape.94
  15.6 0.1 reshape.95
  15.8 9.6 %all-to-all-done = bf16[8,64,256]{2,1,0:T(8,128)(2,1)S(1)} async-done(((bf16[8,64,256]{2,1,0:T(8,128)(2,1)}), bf16[8,64,256]{2,1,0:T(8,128)(2,1)S(1)}, u32[]{:S(2)}, u32[]{:S(2)}) %all-to-all-start) | async-done | bytes 262176 | tf_op jit(solution)/shard_map/all_to_all | solution.py:247
  25.4 3.1 %collective-permute-start.10 = (bf16[256,256]{1,0:T(8,128)(2,1)S(1)}, bf16[256,256]{1,0:T(8,128)(2,1)S(1)}, u32[]{:S(2)}, u32[]{:S(2)}) collective-permute-start(bf16[256,256]{1,0:T(8,128)(2,1)S(1)} %bitcast.59), channel_id=1, source_target_pairs={{0,6},{2,0},{4,2},{6,4},{8,14},{10,8},{12,10},{14,12},{16,22},{18,... | collective-permute-start | bytes 393224 | tf_op jit(solution)/shard_map/ppermute | solution.py:263
  28.5 0.6 collective-permute-start.9
  29.1 1.0 collective-permute-start.8
  30.2 0.5 fusion.1
  30.7 0.5 fusion.2
  31.3 0.9 pad_maximum_fusion.3
  32.2 4.1 %all-to-all-start.1 = ((bf16[8,128,256]{2,1,0:T(8,128)(2,1)}), bf16[8,128,256]{2,1,0:T(8,128)(2,1)}, u32[]{:S(2)}, u32[]{:S(2)}) async-start(bf16[8,128,256]{2,1,0:T(8,128)(2,1)} %bitcast.22), calls=%async_computation.1 | async-start | bytes 1048576 | tf_op jit(solution)/shard_map/all_to_all | solution.py:50
  36.3 0.5 collective-permute-done.8
  36.9 0.6 collective-permute-start.13
  37.5 2.8 %collective-permute-start.4 = (bf16[256,256]{1,0:T(8,128)(2,1)S(1)}, bf16[256,256]{1,0:T(8,128)(2,1)S(1)}, u32[]{:S(2)}, u32[]{:S(2)}) collective-permute-start(bf16[256,256]{1,0:T(8,128)(2,1)S(1)} %bitcast.55), channel_id=1, source_target_pairs={{0,192},{2,194},{4,196},{6,198},{8,200},{10,202},{12,204},{14,206}... | collective-permute-start | bytes 393224 | tf_op jit(solution)/shard_map/ppermute | solution.py:262
  40.3 0.2 collective-permute-start.3
  40.5 2.1 %collective-permute-start.2 = (bf16[256,256]{1,0:T(8,128)(2,1)S(1)}, bf16[256,256]{1,0:T(8,128)(2,1)S(1)}, u32[]{:S(2)}, u32[]{:S(2)}) collective-permute-start(bf16[256,256]{1,0:T(8,128)(2,1)S(1)} %bitcast.57), channel_id=1, source_target_pairs={{0,64},{2,66},{4,68},{6,70},{8,72},{10,74},{12,76},{14,78},{16,80}... | collective-permute-start | bytes 393224 | tf_op jit(solution)/shard_map/ppermute | solution.py:262
  42.6 3.3 %picks.1.pick_ref = bf16[32,128,256]{2,1,0:T(8,128)(2,1)S(1)} custom-call(s32[32,128]{1,0:T(8,128)S(1)} %broadcast_add_fusion.spot_ref), custom_call_target="tpu_custom_call" | custom-call | tf_op jit(solution)/shard_map/picks/pallas_call | solution.py:279
  46.1 1.3 collective-permute-start.12
  47.3 6.3 %collective-permute-done.4 = bf16[256,256]{1,0:T(8,128)(2,1)S(1)} collective-permute-done((bf16[256,256]{1,0:T(8,128)(2,1)S(1)}, bf16[256,256]{1,0:T(8,128)(2,1)S(1)}, u32[]{:S(2)}, u32[]{:S(2)}) %collective-permute-start.4) | collective-permute-done | bytes 131104 | tf_op jit(solution)/shard_map/ppermute | solution.py:262
  53.7 2.4 %collective-permute-start.11 = (bf16[4,256,256]{2,1,0:T(8,128)(2,1)S(1)}, bf16[4,256,256]{2,1,0:T(8,128)(2,1)}, u32[]{:S(2)}, u32[]{:S(2)}) collective-permute-start(bf16[4,256,256]{2,1,0:T(8,128)(2,1)S(1)} %pad_maximum_fusion.2.rest_4_), channel_id=1, source_target_pairs={{0,64},{2,66},{4,68},{6,70},{8,72},{10,74},{12,76},{14,78},{16,80}... | collective-permute-start | bytes 1572872 | tf_op jit(solution)/shard_map/ppermute | solution.py:268
  56.1 2.2 %collective-permute-done.3 = bf16[256,256]{1,0:T(8,128)(2,1)S(1)} collective-permute-done((bf16[256,256]{1,0:T(8,128)(2,1)S(1)}, bf16[256,256]{1,0:T(8,128)(2,1)S(1)}, u32[]{:S(2)}, u32[]{:S(2)}) %collective-permute-start.3) | collective-permute-done | bytes 131104 | tf_op jit(solution)/shard_map/ppermute | solution.py:262
  58.3 0.9 pad_maximum_fusion.1.rest_0_
  59.2 1.8 %collective-permute-start.7 = (bf16[4,256,256]{2,1,0:T(8,128)(2,1)}, bf16[4,256,256]{2,1,0:T(8,128)(2,1)}, u32[]{:S(2)}, u32[]{:S(2)}) collective-permute-start(bf16[4,256,256]{2,1,0:T(8,128)(2,1)} %pad_maximum_fusion.1.rest_0_), channel_id=1, source_target_pairs={{0,6},{2,0},{4,2},{6,4},{8,14},{10,8},{12,10},{14,12},{16,22},{18,... | collective-permute-start | bytes 1572872 | tf_op jit(solution)/shard_map/ppermute | solution.py:267
  61.0 1.7 collective-permute-start.6
  62.7 0.8 copy-done.2
  63.6 1.3 fusion.own_ref
  64.8 1.1 reduce_sum.24
  66.0 1.1 broadcast_in_dim.21
  67.0 17.7 %all-to-all-start.2 = ((bf16[16,128,256]{2,1,0:T(8,128)(2,1)}), bf16[16,128,256]{2,1,0:T(8,128)(2,1)}, u32[]{:S(2)}, u32[]{:S(2)}) async-start(bf16[16,128,256]{2,1,0:T(8,128)(2,1)} %broadcast_in_dim.21), calls=%async_computation.2 | async-start | bytes 2097152 | tf_op jit(solution)/shard_map/all_to_all | solution.py:50
  84.7 2.8 %fusion.35.self_ref = f32[1024,256]{1,0:T(8,128)} fusion(bf16[256,512]{1,0:T(8,128)(2,1)} %param.15, bf16[1024,256]{1,0:T(8,128)(2,1)} %copy-done.6, bf16[1024,256]{1,0:T(8,128)(2,1)} %copy-done.4), kind=kOutput, calls=%fused_computation.81 | convolution fusion | flops 270532608 | bytes 2359296 | tf_op jit(solution)/shard_map/dot_general | solution.py:270
  87.5 0.1 collective-permute-done.5.rest_1_
  87.7 22.2 %edges.1 = (f32[1024,256]{1,0:T(8,128)}, bf16[4,256,256]{2,1,0:T(8,128)(2,1)}, bf16[4,256,256]{2,1,0:T(8,128)(2,1)}, bf16[4,256,256]{2,1,0:T(8,128)(2,1)}, bf16[...) custom-call(s32[8192]{0:T(1024)S(1)} %get-tuple-element.45.from_ref,, ...), custom_call_target="tpu_custom_call" | custom-call | tf_op jit(solution)/shard_map/edges/pallas_call | solution.py:313
  109.8 2.5 %collective-permute-start.14 = (bf16[4,256,256]{2,1,0:T(8,128)(2,1)}, bf16[4,256,256]{2,1,0:T(8,128)(2,1)S(1)}, u32[]{:S(2)}, u32[]{:S(2)}) collective-permute-start(bf16[4,256,256]{2,1,0:T(8,128)(2,1)} %get-tuple-element.16), channel_id=1, source_target_pairs={{0,6},{2,0},{4,2},{6,4},{8,14},{10,8},{12,10},{14,12},{16,22},{18,... | collective-permute-start | bytes 1572872 | tf_op jit(solution)/shard_map/ppermute | solution.py:317
  112.3 1.6 collective-permute-start.15
  113.9 0.7 collective-permute-start.16
  114.5 1.5 collective-permute-start.20
  116.1 4.3 %collective-permute-start.21 = (bf16[4,256,256]{2,1,0:T(8,128)(2,1)}, bf16[4,256,256]{2,1,0:T(8,128)(2,1)S(1)}, u32[]{:S(2)}, u32[]{:S(2)}) collective-permute-start(bf16[4,256,256]{2,1,0:T(8,128)(2,1)} %get-tuple-element.21), channel_id=1, source_target_pairs={{0,128},{2,130},{4,132},{6,134},{8,136},{10,138},{12,140},{14,142}... | collective-permute-start | bytes 1572872 | tf_op jit(solution)/shard_map/ppermute | solution.py:318
  120.4 4.5 %collective-permute-done.14 = bf16[4,256,256]{2,1,0:T(8,128)(2,1)S(1)} collective-permute-done((bf16[4,256,256]{2,1,0:T(8,128)(2,1)}, bf16[4,256,256]{2,1,0:T(8,128)(2,1)S(1)}, u32[]{:S(2)}, u32[]{:S(2)}) %collective-permute-start.14) | collective-permute-done | bytes 524320 | tf_op jit(solution)/shard_map/ppermute | solution.py:317
  124.9 4.0 %collective-permute-start.22 = (bf16[4,256,256]{2,1,0:T(8,128)(2,1)}, bf16[4,256,256]{2,1,0:T(8,128)(2,1)}, u32[]{:S(2)}, u32[]{:S(2)}) collective-permute-start(bf16[4,256,256]{2,1,0:T(8,128)(2,1)} %get-tuple-element.22), channel_id=1, source_target_pairs={{0,64},{2,66},{4,68},{6,70},{8,72},{10,74},{12,76},{14,78},{16,80}... | collective-permute-start | bytes 1572872 | tf_op jit(solution)/shard_map/ppermute | solution.py:318
  128.9 1.4 reduce_sum.25
  130.3 0.8 broadcast_in_dim.22
  131.1 8.0 %all-to-all-start.3 = ((bf16[8,128,256]{2,1,0:T(8,128)(2,1)}), bf16[8,128,256]{2,1,0:T(8,128)(2,1)S(1)}, u32[]{:S(2)}, u32[]{:S(2)}) async-start(bf16[8,128,256]{2,1,0:T(8,128)(2,1)} %broadcast_in_dim.22), calls=%async_computation.3 | async-start | bytes 1048576 | tf_op jit(solution)/shard_map/all_to_all | solution.py:50
  139.1 1.5 fusion.10
  140.6 1.9 %collective-permute-start.17 = (bf16[256,256]{1,0:T(8,128)(2,1)S(1)}, bf16[256,256]{1,0:T(8,128)(2,1)S(1)}, u32[]{:S(2)}, u32[]{:S(2)}) collective-permute-start(bf16[256,256]{1,0:T(8,128)(2,1)S(1)} %get-tuple-element.27), channel_id=1, source_target_pairs={{0,192},{2,194},{4,196},{6,198},{8,200},{10,202},{12,204},{14,206}... | collective-permute-start | bytes 393224 | tf_op jit(solution)/shard_map/ppermute | solution.py:323
  142.5 0.2 collective-permute-start.19
  142.7 1.9 %collective-permute-start.18 = (bf16[256,256]{1,0:T(8,128)(2,1)S(1)}, bf16[256,256]{1,0:T(8,128)(2,1)S(1)}, u32[]{:S(2)}, u32[]{:S(2)}) collective-permute-start(bf16[256,256]{1,0:T(8,128)(2,1)S(1)} %get-tuple-element.29), channel_id=1, source_target_pairs={{0,128},{2,130},{4,132},{6,134},{8,136},{10,138},{12,140},{14,142}... | collective-permute-start | bytes 393224 | tf_op jit(solution)/shard_map/ppermute | solution.py:323
  144.7 0.8 copy-done.11
  145.5 1.6 fusion.13
  147.1 3.6 %collective-permute-start.23 = (bf16[256,256]{1,0:T(8,128)(2,1)S(1)}, bf16[256,256]{1,0:T(8,128)(2,1)S(1)}, u32[]{:S(2)}, u32[]{:S(2)}) collective-permute-start(bf16[256,256]{1,0:T(8,128)(2,1)S(1)} %get-tuple-element.30), channel_id=1, source_target_pairs={{0,6},{2,0},{4,2},{6,4},{8,14},{10,8},{12,10},{14,12},{16,22},{18,... | collective-permute-start | bytes 393224 | tf_op jit(solution)/shard_map/ppermute | solution.py:326
  150.7 1.6 collective-permute-start.24
  152.3 1.2 fusion.9
  153.4 4.9 %collective-permute-done.25 = bf16[256,256]{1,0:T(8,128)(2,1)S(1)} collective-permute-done((bf16[256,256]{1,0:T(8,128)(2,1)S(1)}, bf16[256,256]{1,0:T(8,128)(2,1)S(1)}, u32[]{:S(2)}, u32[]{:S(2)}) %collective-permute-start.25) | collective-permute-done | bytes 131104 | tf_op jit(solution)/shard_map/ppermute | solution.py:326
  158.3 1.2 fusion.6
  159.5 17.5 %all_to_all.25.home_ref = bf16[8,64,256]{2,1,0:T(8,128)(2,1)S(1)} all-to-all(bf16[8,64,256]{2,1,0:T(8,128)(2,1)S(1)} %bitcast.54), channel_id=1, replica_groups={{0,8,16,24,32,40,48,56},{2,10,18,26,34,42,50,58},{4,12,20,28,36,44,52,6..., dimensions={0} | all-to-all | bytes 524288 | tf_op jit(solution)/shard_map/all_to_all | solution.py:330
  177.0 2.0 %final.1 = (bf16[1024,256]{1,0:T(8,128)(2,1)}, f32[256,512]{1,0:T(8,128)}, f32[256,512]{1,0:T(8,128)}) custom-call(bf16[8,64,256]{2,1,0:T(8,128)(2,1)S(1)} %all_to_all.25.home_ref, f32[1024,256]{1,0:T(8,128)S(1)} %copy-done.1, bf16[128,8,256]{2,1,0:T(8,128)(2,1)S(1)} %bitcast.53), custom_call_target="tpu_custom_call" | custom-call | tf_op jit(solution)/shard_map/final/pallas_call | solution.py:338
  (74 shorter events, 0.6 us)
Async XLA Ops:
  0.6 29.6 %copy-start = (bf16[1024,256]{1,0:T(8,128)(2,1)S(1)}, bf16[1024,256]{1,0:T(8,128)(2,1)}, u32[]{:S(2)}) copy-start(bf16[1024,256]{1,0:T(8,128)(2,1)} %param.11) | copy-start | bytes 1572868
  0.6 14.8 %copy-start.15 = (s32[4096]{0:T(1024)S(1)}, s32[4096]{0:T(1024)}, u32[]{:S(2)}) copy-start(s32[4096]{0:T(1024)} %param.20) | copy-start | bytes 49156
  0.7 15.1 %copy-start.14 = (s32[8192]{0:T(1024)S(1)}, s32[8192]{0:T(1024)}, u32[]{:S(2)}) copy-start(s32[8192]{0:T(1024)} %param.18) | copy-start | bytes 98308
  0.7 15.1 %copy-start.13 = (s32[8192]{0:T(1024)S(1)}, s32[8192]{0:T(1024)}, u32[]{:S(2)}) copy-start(s32[8192]{0:T(1024)} %param.17) | copy-start | bytes 98308
  1.5 1.3 collective-permute-start.1
  4.7 20.7 %all-to-all-start = ((bf16[8,64,256]{2,1,0:T(8,128)(2,1)}), bf16[8,64,256]{2,1,0:T(8,128)(2,1)S(1)}, u32[]{:S(2)}, u32[]{:S(2)}) async-start(bf16[8,64,256]{2,1,0:T(8,128)(2,1)} %broadcast_in_dim.20), calls=%async_computation | async-start | bytes 524288 | tf_op jit(solution)/shard_map/all_to_all | solution.py:247
  14.5 15.6 %collective-permute-start = (bf16[1024,256]{1,0:T(8,128)(2,1)S(1)}, bf16[1024,256]{1,0:T(8,128)(2,1)S(1)}, u32[]{:S(2)}, u32[]{:S(2)}) collective-permute-start(bf16[1024,256]{1,0:T(8,128)(2,1)S(1)} %select_convert_fusion), channel_id=1, source_target_pairs={{0,1},{1,0},{2,3},{3,2},{4,5},{5,4},{6,7},{7,6},{8,9},{9,8},{10,11... | collective-permute-start | bytes 1572872 | tf_op jit(solution)/shard_map/ppermute | solution.py:238
  25.4 5.3 %copy-start.17 = (bf16[1024,256]{1,0:T(8,128)(2,1)S(1)}, bf16[1024,256]{1,0:T(8,128)(2,1)}, u32[]{:S(2)}) copy-start(bf16[1024,256]{1,0:T(8,128)(2,1)} %param.14) | copy-start | bytes 1572868
  25.4 10.9 %collective-permute-start.10 = (bf16[256,256]{1,0:T(8,128)(2,1)S(1)}, bf16[256,256]{1,0:T(8,128)(2,1)S(1)}, u32[]{:S(2)}, u32[]{:S(2)}) collective-permute-start(bf16[256,256]{1,0:T(8,128)(2,1)S(1)} %bitcast.59), channel_id=1, source_target_pairs={{0,6},{2,0},{4,2},{6,4},{8,14},{10,8},{12,10},{14,12},{16,22},{18,... | collective-permute-start | bytes 393224 | tf_op jit(solution)/shard_map/ppermute | solution.py:263
  28.5 7.8 %collective-permute-start.9 = (bf16[256,256]{1,0:T(8,128)(2,1)S(1)}, bf16[256,256]{1,0:T(8,128)(2,1)S(1)}, u32[]{:S(2)}, u32[]{:S(2)}) collective-permute-start(bf16[256,256]{1,0:T(8,128)(2,1)S(1)} %bitcast.60), channel_id=1, source_target_pairs={{0,4},{2,6},{4,0},{6,2},{8,12},{10,14},{12,8},{14,10},{16,20},{18,... | collective-permute-start | bytes 393224 | tf_op jit(solution)/shard_map/ppermute | solution.py:263
  29.1 7.7 %collective-permute-start.8 = (bf16[256,256]{1,0:T(8,128)(2,1)S(1)}, bf16[256,256]{1,0:T(8,128)(2,1)S(1)}, u32[]{:S(2)}, u32[]{:S(2)}) collective-permute-start(bf16[256,256]{1,0:T(8,128)(2,1)S(1)} %bitcast.61), channel_id=1, source_target_pairs={{0,2},{2,4},{4,6},{6,0},{8,10},{10,12},{12,14},{14,8},{16,18},{18,... | collective-permute-start | bytes 393224 | tf_op jit(solution)/shard_map/ppermute | solution.py:263
  30.2 1.0 copy-start.4
  30.2 1.0 copy-start.6
  31.2 11.4 %copy-start.16 = (s32[1024]{0:T(1024)S(1)}, s32[1024]{0:T(1024)}, u32[]{:S(2)}) copy-start(s32[1024]{0:T(1024)} %param.21) | copy-start | bytes 12292
  32.2 32.7 %all-to-all-start.1 = ((bf16[8,128,256]{2,1,0:T(8,128)(2,1)}), bf16[8,128,256]{2,1,0:T(8,128)(2,1)}, u32[]{:S(2)}, u32[]{:S(2)}) async-start(bf16[8,128,256]{2,1,0:T(8,128)(2,1)} %bitcast.22), calls=%async_computation.1 | async-start | bytes 1048576 | tf_op jit(solution)/shard_map/all_to_all | solution.py:50
  36.8 26.7 %copy-start.5 = (bf16[1024,256]{1,0:T(8,128)(2,1)S(1)}, bf16[1024,256]{1,0:T(8,128)(2,1)}, u32[]{:S(2)}) copy-start(bf16[1024,256]{1,0:T(8,128)(2,1)} %copy-done.4) | copy-start | bytes 1572868
  36.8 26.7 %copy-start.7 = (bf16[1024,256]{1,0:T(8,128)(2,1)S(1)}, bf16[1024,256]{1,0:T(8,128)(2,1)}, u32[]{:S(2)}) copy-start(bf16[1024,256]{1,0:T(8,128)(2,1)} %copy-done.6) | copy-start | bytes 1572868
  36.8 26.7 %copy-start.18 = (bf16[256,512]{1,0:T(8,128)(2,1)S(1)}, bf16[256,512]{1,0:T(8,128)(2,1)}, u32[]{:S(2)}) copy-start(bf16[256,512]{1,0:T(8,128)(2,1)} %param.16) | copy-start | bytes 786436
  36.9 25.8 %collective-permute-start.13 = (bf16[4,256,256]{2,1,0:T(8,128)(2,1)S(1)}, bf16[4,256,256]{2,1,0:T(8,128)(2,1)S(1)}, u32[]{:S(2)}, u32[]{:S(2)}) collective-permute-start(bf16[4,256,256]{2,1,0:T(8,128)(2,1)S(1)} %pad_maximum_fusion.2.rest_4_), channel_id=1, source_target_pairs={{0,192},{2,194},{4,196},{6,198},{8,200},{10,202},{12,204},{14,206}... | collective-permute-start | bytes 1572872 | tf_op jit(solution)/shard_map/ppermute | solution.py:268
  37.5 16.1 %collective-permute-start.4 = (bf16[256,256]{1,0:T(8,128)(2,1)S(1)}, bf16[256,256]{1,0:T(8,128)(2,1)S(1)}, u32[]{:S(2)}, u32[]{:S(2)}) collective-permute-start(bf16[256,256]{1,0:T(8,128)(2,1)S(1)} %bitcast.55), channel_id=1, source_target_pairs={{0,192},{2,194},{4,196},{6,198},{8,200},{10,202},{12,204},{14,206}... | collective-permute-start | bytes 393224 | tf_op jit(solution)/shard_map/ppermute | solution.py:262
  40.3 18.0 %collective-permute-start.3 = (bf16[256,256]{1,0:T(8,128)(2,1)S(1)}, bf16[256,256]{1,0:T(8,128)(2,1)S(1)}, u32[]{:S(2)}, u32[]{:S(2)}) collective-permute-start(bf16[256,256]{1,0:T(8,128)(2,1)S(1)} %bitcast.56), channel_id=1, source_target_pairs={{0,128},{2,130},{4,132},{6,134},{8,136},{10,138},{12,140},{14,142}... | collective-permute-start | bytes 393224 | tf_op jit(solution)/shard_map/ppermute | solution.py:262
  40.5 17.8 %collective-permute-start.2 = (bf16[256,256]{1,0:T(8,128)(2,1)S(1)}, bf16[256,256]{1,0:T(8,128)(2,1)S(1)}, u32[]{:S(2)}, u32[]{:S(2)}) collective-permute-start(bf16[256,256]{1,0:T(8,128)(2,1)S(1)} %bitcast.57), channel_id=1, source_target_pairs={{0,64},{2,66},{4,68},{6,70},{8,72},{10,74},{12,76},{14,78},{16,80}... | collective-permute-start | bytes 393224 | tf_op jit(solution)/shard_map/ppermute | solution.py:262
  46.1 41.4 %collective-permute-start.12 = (bf16[4,256,256]{2,1,0:T(8,128)(2,1)S(1)}, bf16[4,256,256]{2,1,0:T(8,128)(2,1)}, u32[]{:S(2)}, u32[]{:S(2)}) collective-permute-start(bf16[4,256,256]{2,1,0:T(8,128)(2,1)S(1)} %pad_maximum_fusion.2.rest_4_), channel_id=1, source_target_pairs={{0,128},{2,130},{4,132},{6,134},{8,136},{10,138},{12,140},{14,142}... | collective-permute-start | bytes 1572872 | tf_op jit(solution)/shard_map/ppermute | solution.py:268
  53.7 33.8 %collective-permute-start.11 = (bf16[4,256,256]{2,1,0:T(8,128)(2,1)S(1)}, bf16[4,256,256]{2,1,0:T(8,128)(2,1)}, u32[]{:S(2)}, u32[]{:S(2)}) collective-permute-start(bf16[4,256,256]{2,1,0:T(8,128)(2,1)S(1)} %pad_maximum_fusion.2.rest_4_), channel_id=1, source_target_pairs={{0,64},{2,66},{4,68},{6,70},{8,72},{10,74},{12,76},{14,78},{16,80}... | collective-permute-start | bytes 1572872 | tf_op jit(solution)/shard_map/ppermute | solution.py:268
  59.2 28.3 %collective-permute-start.7 = (bf16[4,256,256]{2,1,0:T(8,128)(2,1)}, bf16[4,256,256]{2,1,0:T(8,128)(2,1)}, u32[]{:S(2)}, u32[]{:S(2)}) collective-permute-start(bf16[4,256,256]{2,1,0:T(8,128)(2,1)} %pad_maximum_fusion.1.rest_0_), channel_id=1, source_target_pairs={{0,6},{2,0},{4,2},{6,4},{8,14},{10,8},{12,10},{14,12},{16,22},{18,... | collective-permute-start | bytes 1572872 | tf_op jit(solution)/shard_map/ppermute | solution.py:267
  61.0 26.5 %collective-permute-start.6 = (bf16[4,256,256]{2,1,0:T(8,128)(2,1)}, bf16[4,256,256]{2,1,0:T(8,128)(2,1)}, u32[]{:S(2)}, u32[]{:S(2)}) collective-permute-start(bf16[4,256,256]{2,1,0:T(8,128)(2,1)} %pad_maximum_fusion.1.rest_0_), channel_id=1, source_target_pairs={{0,4},{2,6},{4,0},{6,2},{8,12},{10,14},{12,8},{14,10},{16,20},{18,... | collective-permute-start | bytes 1572872 | tf_op jit(solution)/shard_map/ppermute | solution.py:267
  62.7 0.8 copy-start.2
  63.5 24.1 %collective-permute-start.5 = (bf16[4,256,256]{2,1,0:T(8,128)(2,1)}, bf16[4,256,256]{2,1,0:T(8,128)(2,1)}, u32[]{:S(2)}, u32[]{:S(2)}) collective-permute-start(bf16[4,256,256]{2,1,0:T(8,128)(2,1)} %pad_maximum_fusion.1.rest_0_), channel_id=1, source_target_pairs={{0,2},{2,4},{4,6},{6,0},{8,10},{10,12},{12,14},{14,8},{16,18},{18,... | collective-permute-start | bytes 1572872 | tf_op jit(solution)/shard_map/ppermute | solution.py:267
  67.0 61.9 %all-to-all-start.2 = ((bf16[16,128,256]{2,1,0:T(8,128)(2,1)}), bf16[16,128,256]{2,1,0:T(8,128)(2,1)}, u32[]{:S(2)}, u32[]{:S(2)}) async-start(bf16[16,128,256]{2,1,0:T(8,128)(2,1)} %broadcast_in_dim.21), calls=%async_computation.2 | async-start | bytes 2097152 | tf_op jit(solution)/shard_map/all_to_all | solution.py:50
  84.7 2.9 %copy-start.3 = (bf16[4,256,256]{2,1,0:T(8,128)(2,1)S(1)}, bf16[4,256,256]{2,1,0:T(8,128)(2,1)}, u32[]{:S(2)}) copy-start(bf16[4,256,256]{2,1,0:T(8,128)(2,1)} %copy-done.2) | copy-start | bytes 1572868
  109.8 29.3 %copy-start.9 = (bf16[4,256,256]{2,1,0:T(8,128)(2,1)S(1)}, bf16[4,256,256]{2,1,0:T(8,128)(2,1)}, u32[]{:S(2)}) copy-start(bf16[4,256,256]{2,1,0:T(8,128)(2,1)} %get-tuple-element.15) | copy-start | bytes 1572868
  109.8 15.1 %collective-permute-start.14 = (bf16[4,256,256]{2,1,0:T(8,128)(2,1)}, bf16[4,256,256]{2,1,0:T(8,128)(2,1)S(1)}, u32[]{:S(2)}, u32[]{:S(2)}) collective-permute-start(bf16[4,256,256]{2,1,0:T(8,128)(2,1)} %get-tuple-element.16), channel_id=1, source_target_pairs={{0,6},{2,0},{4,2},{6,4},{8,14},{10,8},{12,10},{14,12},{16,22},{18,... | collective-permute-start | bytes 1572872 | tf_op jit(solution)/shard_map/ppermute | solution.py:317
  112.3 26.8 %collective-permute-start.15 = (bf16[4,256,256]{2,1,0:T(8,128)(2,1)}, bf16[4,256,256]{2,1,0:T(8,128)(2,1)}, u32[]{:S(2)}, u32[]{:S(2)}) collective-permute-start(bf16[4,256,256]{2,1,0:T(8,128)(2,1)} %get-tuple-element.17), channel_id=1, source_target_pairs={{0,4},{2,6},{4,0},{6,2},{8,12},{10,14},{12,8},{14,10},{16,20},{18,... | collective-permute-start | bytes 1572872 | tf_op jit(solution)/shard_map/ppermute | solution.py:317
  113.9 25.2 %collective-permute-start.16 = (bf16[4,256,256]{2,1,0:T(8,128)(2,1)}, bf16[4,256,256]{2,1,0:T(8,128)(2,1)}, u32[]{:S(2)}, u32[]{:S(2)}) collective-permute-start(bf16[4,256,256]{2,1,0:T(8,128)(2,1)} %get-tuple-element.18), channel_id=1, source_target_pairs={{0,2},{2,4},{4,6},{6,0},{8,10},{10,12},{12,14},{14,8},{16,18},{18,... | collective-permute-start | bytes 1572872 | tf_op jit(solution)/shard_map/ppermute | solution.py:317
  114.5 28.2 %collective-permute-start.20 = (bf16[4,256,256]{2,1,0:T(8,128)(2,1)}, bf16[4,256,256]{2,1,0:T(8,128)(2,1)S(1)}, u32[]{:S(2)}, u32[]{:S(2)}) collective-permute-start(bf16[4,256,256]{2,1,0:T(8,128)(2,1)} %get-tuple-element.20), channel_id=1, source_target_pairs={{0,192},{2,194},{4,196},{6,198},{8,200},{10,202},{12,204},{14,206}... | collective-permute-start | bytes 1572872 | tf_op jit(solution)/shard_map/ppermute | solution.py:318
  116.1 28.6 %collective-permute-start.21 = (bf16[4,256,256]{2,1,0:T(8,128)(2,1)}, bf16[4,256,256]{2,1,0:T(8,128)(2,1)S(1)}, u32[]{:S(2)}, u32[]{:S(2)}) collective-permute-start(bf16[4,256,256]{2,1,0:T(8,128)(2,1)} %get-tuple-element.21), channel_id=1, source_target_pairs={{0,128},{2,130},{4,132},{6,134},{8,136},{10,138},{12,140},{14,142}... | collective-permute-start | bytes 1572872 | tf_op jit(solution)/shard_map/ppermute | solution.py:318
  124.9 6.2 %copy-start.12 = (bf16[4,256,256]{2,1,0:T(8,128)(2,1)}, bf16[4,256,256]{2,1,0:T(8,128)(2,1)S(1)}, u32[]{:S(2)}) copy-start(bf16[4,256,256]{2,1,0:T(8,128)(2,1)S(1)} %collective-permute-done.14) | copy-start | bytes 1572868
  124.9 20.6 %copy-start.8 = (bf16[4,256,256]{2,1,0:T(8,128)(2,1)S(1)}, bf16[4,256,256]{2,1,0:T(8,128)(2,1)}, u32[]{:S(2)}) copy-start(bf16[4,256,256]{2,1,0:T(8,128)(2,1)} %get-tuple-element.19) | copy-start | bytes 1572868
  124.9 19.8 %collective-permute-start.22 = (bf16[4,256,256]{2,1,0:T(8,128)(2,1)}, bf16[4,256,256]{2,1,0:T(8,128)(2,1)}, u32[]{:S(2)}, u32[]{:S(2)}) collective-permute-start(bf16[4,256,256]{2,1,0:T(8,128)(2,1)} %get-tuple-element.22), channel_id=1, source_target_pairs={{0,64},{2,66},{4,68},{6,70},{8,72},{10,74},{12,76},{14,78},{16,80}... | collective-permute-start | bytes 1572872 | tf_op jit(solution)/shard_map/ppermute | solution.py:318
  131.1 28.4 %all-to-all-start.3 = ((bf16[8,128,256]{2,1,0:T(8,128)(2,1)}), bf16[8,128,256]{2,1,0:T(8,128)(2,1)S(1)}, u32[]{:S(2)}, u32[]{:S(2)}) async-start(bf16[8,128,256]{2,1,0:T(8,128)(2,1)} %broadcast_in_dim.22), calls=%async_computation.3 | async-start | bytes 1048576 | tf_op jit(solution)/shard_map/all_to_all | solution.py:50
  140.6 10.1 %collective-permute-start.17 = (bf16[256,256]{1,0:T(8,128)(2,1)S(1)}, bf16[256,256]{1,0:T(8,128)(2,1)S(1)}, u32[]{:S(2)}, u32[]{:S(2)}) collective-permute-start(bf16[256,256]{1,0:T(8,128)(2,1)S(1)} %get-tuple-element.27), channel_id=1, source_target_pairs={{0,192},{2,194},{4,196},{6,198},{8,200},{10,202},{12,204},{14,206}... | collective-permute-start | bytes 393224 | tf_op jit(solution)/shard_map/ppermute | solution.py:323
  142.5 9.8 %collective-permute-start.19 = (bf16[256,256]{1,0:T(8,128)(2,1)S(1)}, bf16[256,256]{1,0:T(8,128)(2,1)S(1)}, u32[]{:S(2)}, u32[]{:S(2)}) collective-permute-start(bf16[256,256]{1,0:T(8,128)(2,1)S(1)} %get-tuple-element.28), channel_id=1, source_target_pairs={{0,64},{2,66},{4,68},{6,70},{8,72},{10,74},{12,76},{14,78},{16,80}... | collective-permute-start | bytes 393224 | tf_op jit(solution)/shard_map/ppermute | solution.py:323
  142.7 2.0 %copy-start.10 = (bf16[4,256,256]{2,1,0:T(8,128)(2,1)}, bf16[4,256,256]{2,1,0:T(8,128)(2,1)S(1)}, u32[]{:S(2)}) copy-start(bf16[4,256,256]{2,1,0:T(8,128)(2,1)S(1)} %collective-permute-done.20) | copy-start | bytes 1572868
  142.7 9.5 %collective-permute-start.18 = (bf16[256,256]{1,0:T(8,128)(2,1)S(1)}, bf16[256,256]{1,0:T(8,128)(2,1)S(1)}, u32[]{:S(2)}, u32[]{:S(2)}) collective-permute-start(bf16[256,256]{1,0:T(8,128)(2,1)S(1)} %get-tuple-element.29), channel_id=1, source_target_pairs={{0,128},{2,130},{4,132},{6,134},{8,136},{10,138},{12,140},{14,142}... | collective-permute-start | bytes 393224 | tf_op jit(solution)/shard_map/ppermute | solution.py:323
  144.7 0.8 copy-start.11
  145.5 31.5 %copy-start.1 = (f32[1024,256]{1,0:T(8,128)S(1)}, f32[1024,256]{1,0:T(8,128)}, u32[]{:S(2)}) copy-start(f32[1024,256]{1,0:T(8,128)} %get-tuple-element.25.pre_ref) | copy-start | bytes 3145732
  147.1 6.4 %collective-permute-start.23 = (bf16[256,256]{1,0:T(8,128)(2,1)S(1)}, bf16[256,256]{1,0:T(8,128)(2,1)S(1)}, u32[]{:S(2)}, u32[]{:S(2)}) collective-permute-start(bf16[256,256]{1,0:T(8,128)(2,1)S(1)} %get-tuple-element.30), channel_id=1, source_target_pairs={{0,6},{2,0},{4,2},{6,4},{8,14},{10,8},{12,10},{14,12},{16,22},{18,... | collective-permute-start | bytes 393224 | tf_op jit(solution)/shard_map/ppermute | solution.py:326
  150.7 7.6 %collective-permute-start.25 = (bf16[256,256]{1,0:T(8,128)(2,1)S(1)}, bf16[256,256]{1,0:T(8,128)(2,1)S(1)}, u32[]{:S(2)}, u32[]{:S(2)}) collective-permute-start(bf16[256,256]{1,0:T(8,128)(2,1)S(1)} %get-tuple-element.31), channel_id=1, source_target_pairs={{0,2},{2,4},{4,6},{6,0},{8,10},{10,12},{12,14},{14,8},{16,18},{18,... | collective-permute-start | bytes 393224 | tf_op jit(solution)/shard_map/ppermute | solution.py:326
  150.7 7.6 %collective-permute-start.24 = (bf16[256,256]{1,0:T(8,128)(2,1)S(1)}, bf16[256,256]{1,0:T(8,128)(2,1)S(1)}, u32[]{:S(2)}, u32[]{:S(2)}) collective-permute-start(bf16[256,256]{1,0:T(8,128)(2,1)S(1)} %get-tuple-element.32), channel_id=1, source_target_pairs={{0,4},{2,6},{4,0},{6,2},{8,12},{10,14},{12,8},{14,10},{16,20},{18,... | collective-permute-start | bytes 393224 | tf_op jit(solution)/shard_map/ppermute | solution.py:326

commit v8 on v7

--- a/solution.py
+++ b/solution.py
@@ -124,13 +124,14 @@
                 fetch(second, 0)
 
     clear = 16 * SUB
+    cleared = (masters + nx * nz * ny * slots) * halves
 
     def zero(i, carry):
         for s in sums:
             s[pl.ds(pl.multiple_of(i * clear, clear), clear), :] = jnp.zeros((clear, LANES), jnp.float32)
         return carry
 
-    lax.fori_loop(0, table.shape[0] // clear, zero, 0)
+    lax.fori_loop(0, cleared // clear, zero, 0)
 
     step = CHAINS * UNROLL
 
@@ -298,6 +299,7 @@
     ).astype(jnp.int32)
 
     lanes = local * halves
+    spare = SUB * SUB
     low_type = pltpu.HBM(low_set.shape, jnp.bfloat16)
     high_type = pltpu.HBM(high_set.shape, jnp.bfloat16)
     edge_call = pl.pallas_call(
@@ -305,8 +307,8 @@
         out_shape=[pltpu.HBM((masters, width), jnp.float32)] + [low_type] * ny + [high_type] * nx,
         in_specs=[SMEM] * 3 + [VMEM] * (4 + nx + ny),
         out_specs=[VMEM] * (1 + nx + ny),
-        scratch_shapes=[pltpu.VMEM((lanes, LANES), jnp.float32)]
-        + [pltpu.VMEM((lanes + SUB * halves, LANES), jnp.float32) for _ in range(CHAINS)],
+        scratch_shapes=[pltpu.VMEM((lanes + spare, LANES), jnp.float32)]
+        + [pltpu.VMEM((lanes + SUB * halves + spare, LANES), jnp.float32) for _ in range(CHAINS)],
         compiler_params=pltpu.CompilerParams(vmem_limit_bytes=42 << 20),
         name="edges",
     )

time: 180 us -> 180 us (level)
  no operation moved by 1% of the time
where the time goes in v8:
time: 180 us; the launch traced here: 179 us
  starting transfers between devices  79.8 us (44%)
  waiting for transfers between devices  28.7 us (16%)
  Pallas kernels  27.5 us (15%)
  blocking collectives  17.5 us (10%)
  other arithmetic  12.9 us (7%)
  matrix products  6.17 us (3%)
  local copies, waits for them, and re-layouts  4.74 us (3%)
    all_to_all x3, starting transfers between devices, swap(): lax.all_to_all(array, 'dom', split_axis=0, concat_axis=0, axis_index_grou...  29.8 us
    pallas_call x1, Pallas kernels, on_device(): edge_call(from_at, to_at, place, far(scaled), far(self_part), near(spots)...  22.2 us
    all_to_all x1, blocking collectives, on_device(): lax.all_to_all(column_sum.reshape(nz, hub, width), 'dom', split_axis=0, c...  17.5 us
    ppermute x3, starting transfers between devices, on_device(): lax.ppermute(high_back[k], 'dom', ring('x', -k))  9.87 us
    all_to_all x1, waiting for transfers between devices, on_device(): lax.all_to_all(copies, 'dom', split_axis=0, concat_axis=0, axis_index_gro...  9.57 us
    ppermute x3, waiting for transfers between devices, on_device(): low_far = [lax.ppermute(low, 'dom', ring('x', k)) for k in range(1, nx)]  8.59 us
    all_to_all x1, starting transfers between devices, on_device(): lax.all_to_all(copies, 'dom', split_axis=0, concat_axis=0, axis_index_gro...  8.47 us
    ppermute x3, starting transfers between devices, on_device(): lax.ppermute(high_sum[k].astype(jnp.bfloat16), 'dom', ring('y', -k))  5.18 us
  transfers between devices with their start and end apart: 30, of which 8 were waited for; matrix products, arithmetic and copies ran while one was open for 11% of the time, Pallas kernels for 14%

profile of v8, /device:TPU:2, one launch (start us, length us, event | category | flops | bytes accessed | tf_op | source)
XLA Modules:
  0.0 179.0 jit_solution(11260613063708939801)
XLA Ops:
  0.7 0.8 select_convert_fusion.1
  1.5 0.1 collective-permute-start.1
  1.6 0.7 slice_convert_fusion
  2.3 0.5 collective-permute-done.1
  2.8 1.2 fusion.3
  4.0 0.7 broadcast_in_dim.20
  4.7 8.5 %all-to-all-start = ((bf16[8,64,256]{2,1,0:T(8,128)(2,1)}), bf16[8,64,256]{2,1,0:T(8,128)(2,1)S(1)}, u32[]{:S(2)}, u32[]{:S(2)}) async-start(bf16[8,64,256]{2,1,0:T(8,128)(2,1)} %broadcast_in_dim.20), calls=%async_computation | async-start | bytes 524288 | tf_op jit(solution)/shard_map/all_to_all | solution.py:248
  13.2 1.4 select_convert_fusion
  14.5 0.1 collective-permute-start
  15.4 0.1 add.180
  15.5 0.1 reshape.94
  15.6 0.1 reshape.95
  15.8 9.6 %all-to-all-done = bf16[8,64,256]{2,1,0:T(8,128)(2,1)S(1)} async-done(((bf16[8,64,256]{2,1,0:T(8,128)(2,1)}), bf16[8,64,256]{2,1,0:T(8,128)(2,1)S(1)}, u32[]{:S(2)}, u32[]{:S(2)}) %all-to-all-start) | async-done | bytes 262176 | tf_op jit(solution)/shard_map/all_to_all | solution.py:248
  25.4 3.1 %collective-permute-start.10 = (bf16[256,256]{1,0:T(8,128)(2,1)S(1)}, bf16[256,256]{1,0:T(8,128)(2,1)S(1)}, u32[]{:S(2)}, u32[]{:S(2)}) collective-permute-start(bf16[256,256]{1,0:T(8,128)(2,1)S(1)} %bitcast.59), channel_id=1, source_target_pairs={{0,6},{2,0},{4,2},{6,4},{8,14},{10,8},{12,10},{14,12},{16,22},{18,... | collective-permute-start | bytes 393224 | tf_op jit(solution)/shard_map/ppermute | solution.py:264
  28.5 0.6 collective-permute-start.9
  29.1 1.0 collective-permute-start.8
  30.2 0.5 fusion.1
  30.7 0.5 fusion.2
  31.3 0.9 pad_maximum_fusion.3
  32.2 4.1 %all-to-all-start.1 = ((bf16[8,128,256]{2,1,0:T(8,128)(2,1)}), bf16[8,128,256]{2,1,0:T(8,128)(2,1)}, u32[]{:S(2)}, u32[]{:S(2)}) async-start(bf16[8,128,256]{2,1,0:T(8,128)(2,1)} %bitcast.22), calls=%async_computation.1 | async-start | bytes 1048576 | tf_op jit(solution)/shard_map/all_to_all | solution.py:50
  36.3 0.5 collective-permute-done.8
  36.9 0.6 collective-permute-start.13
  37.5 2.8 %collective-permute-start.4 = (bf16[256,256]{1,0:T(8,128)(2,1)S(1)}, bf16[256,256]{1,0:T(8,128)(2,1)S(1)}, u32[]{:S(2)}, u32[]{:S(2)}) collective-permute-start(bf16[256,256]{1,0:T(8,128)(2,1)S(1)} %bitcast.55), channel_id=1, source_target_pairs={{0,192},{2,194},{4,196},{6,198},{8,200},{10,202},{12,204},{14,206}... | collective-permute-start | bytes 393224 | tf_op jit(solution)/shard_map/ppermute | solution.py:263
  40.3 0.2 collective-permute-start.3
  40.5 2.1 %collective-permute-start.2 = (bf16[256,256]{1,0:T(8,128)(2,1)S(1)}, bf16[256,256]{1,0:T(8,128)(2,1)S(1)}, u32[]{:S(2)}, u32[]{:S(2)}) collective-permute-start(bf16[256,256]{1,0:T(8,128)(2,1)S(1)} %bitcast.57), channel_id=1, source_target_pairs={{0,64},{2,66},{4,68},{6,70},{8,72},{10,74},{12,76},{14,78},{16,80}... | collective-permute-start | bytes 393224 | tf_op jit(solution)/shard_map/ppermute | solution.py:263
  42.6 3.3 %picks.1.pick_ref = bf16[32,128,256]{2,1,0:T(8,128)(2,1)S(1)} custom-call(s32[32,128]{1,0:T(8,128)S(1)} %broadcast_add_fusion.spot_ref), custom_call_target="tpu_custom_call" | custom-call | tf_op jit(solution)/shard_map/picks/pallas_call | solution.py:280
  46.1 1.3 collective-permute-start.12
  47.3 6.3 %collective-permute-done.4 = bf16[256,256]{1,0:T(8,128)(2,1)S(1)} collective-permute-done((bf16[256,256]{1,0:T(8,128)(2,1)S(1)}, bf16[256,256]{1,0:T(8,128)(2,1)S(1)}, u32[]{:S(2)}, u32[]{:S(2)}) %collective-permute-start.4) | collective-permute-done | bytes 131104 | tf_op jit(solution)/shard_map/ppermute | solution.py:263
  53.7 2.4 %collective-permute-start.11 = (bf16[4,256,256]{2,1,0:T(8,128)(2,1)S(1)}, bf16[4,256,256]{2,1,0:T(8,128)(2,1)}, u32[]{:S(2)}, u32[]{:S(2)}) collective-permute-start(bf16[4,256,256]{2,1,0:T(8,128)(2,1)S(1)} %pad_maximum_fusion.2.rest_4_), channel_id=1, source_target_pairs={{0,64},{2,66},{4,68},{6,70},{8,72},{10,74},{12,76},{14,78},{16,80}... | collective-permute-start | bytes 1572872 | tf_op jit(solution)/shard_map/ppermute | solution.py:269
  56.1 2.2 %collective-permute-done.3 = bf16[256,256]{1,0:T(8,128)(2,1)S(1)} collective-permute-done((bf16[256,256]{1,0:T(8,128)(2,1)S(1)}, bf16[256,256]{1,0:T(8,128)(2,1)S(1)}, u32[]{:S(2)}, u32[]{:S(2)}) %collective-permute-start.3) | collective-permute-done | bytes 131104 | tf_op jit(solution)/shard_map/ppermute | solution.py:263
  58.3 0.9 pad_maximum_fusion.1.rest_0_
  59.2 1.8 %collective-permute-start.7 = (bf16[4,256,256]{2,1,0:T(8,128)(2,1)}, bf16[4,256,256]{2,1,0:T(8,128)(2,1)}, u32[]{:S(2)}, u32[]{:S(2)}) collective-permute-start(bf16[4,256,256]{2,1,0:T(8,128)(2,1)} %pad_maximum_fusion.1.rest_0_), channel_id=1, source_target_pairs={{0,6},{2,0},{4,2},{6,4},{8,14},{10,8},{12,10},{14,12},{16,22},{18,... | collective-permute-start | bytes 1572872 | tf_op jit(solution)/shard_map/ppermute | solution.py:268
  61.0 1.7 collective-permute-start.6
  62.7 0.8 copy-done.2
  63.6 1.3 fusion.own_ref
  64.8 1.1 reduce_sum.24
  66.0 1.1 broadcast_in_dim.21
  67.0 17.7 %all-to-all-start.2 = ((bf16[16,128,256]{2,1,0:T(8,128)(2,1)}), bf16[16,128,256]{2,1,0:T(8,128)(2,1)}, u32[]{:S(2)}, u32[]{:S(2)}) async-start(bf16[16,128,256]{2,1,0:T(8,128)(2,1)} %broadcast_in_dim.21), calls=%async_computation.2 | async-start | bytes 2097152 | tf_op jit(solution)/shard_map/all_to_all | solution.py:50
  84.7 2.8 %fusion.35.self_ref = f32[1024,256]{1,0:T(8,128)} fusion(bf16[256,512]{1,0:T(8,128)(2,1)} %param.15, bf16[1024,256]{1,0:T(8,128)(2,1)} %copy-done.6, bf16[1024,256]{1,0:T(8,128)(2,1)} %copy-done.4), kind=kOutput, calls=%fused_computation.81 | convolution fusion | flops 270532608 | bytes 2359296 | tf_op jit(solution)/shard_map/dot_general | solution.py:271
  87.5 0.1 collective-permute-done.5.rest_1_
  87.7 22.2 %edges.1 = (f32[1024,256]{1,0:T(8,128)}, bf16[4,256,256]{2,1,0:T(8,128)(2,1)}, bf16[4,256,256]{2,1,0:T(8,128)(2,1)}, bf16[4,256,256]{2,1,0:T(8,128)(2,1)}, bf16[...) custom-call(s32[8192]{0:T(1024)S(1)} %get-tuple-element.45.from_ref,, ...), custom_call_target="tpu_custom_call" | custom-call | tf_op jit(solution)/shard_map/edges/pallas_call | solution.py:315
  109.8 2.5 %collective-permute-start.14 = (bf16[4,256,256]{2,1,0:T(8,128)(2,1)}, bf16[4,256,256]{2,1,0:T(8,128)(2,1)S(1)}, u32[]{:S(2)}, u32[]{:S(2)}) collective-permute-start(bf16[4,256,256]{2,1,0:T(8,128)(2,1)} %get-tuple-element.16), channel_id=1, source_target_pairs={{0,6},{2,0},{4,2},{6,4},{8,14},{10,8},{12,10},{14,12},{16,22},{18,... | collective-permute-start | bytes 1572872 | tf_op jit(solution)/shard_map/ppermute | solution.py:319
  112.3 1.6 collective-permute-start.15
  113.9 0.7 collective-permute-start.16
  114.5 1.5 collective-permute-start.20
  116.1 4.3 %collective-permute-start.21 = (bf16[4,256,256]{2,1,0:T(8,128)(2,1)}, bf16[4,256,256]{2,1,0:T(8,128)(2,1)S(1)}, u32[]{:S(2)}, u32[]{:S(2)}) collective-permute-start(bf16[4,256,256]{2,1,0:T(8,128)(2,1)} %get-tuple-element.21), channel_id=1, source_target_pairs={{0,128},{2,130},{4,132},{6,134},{8,136},{10,138},{12,140},{14,142}... | collective-permute-start | bytes 1572872 | tf_op jit(solution)/shard_map/ppermute | solution.py:320
  120.4 4.5 %collective-permute-done.14 = bf16[4,256,256]{2,1,0:T(8,128)(2,1)S(1)} collective-permute-done((bf16[4,256,256]{2,1,0:T(8,128)(2,1)}, bf16[4,256,256]{2,1,0:T(8,128)(2,1)S(1)}, u32[]{:S(2)}, u32[]{:S(2)}) %collective-permute-start.14) | collective-permute-done | bytes 524320 | tf_op jit(solution)/shard_map/ppermute | solution.py:319
  124.9 4.0 %collective-permute-start.22 = (bf16[4,256,256]{2,1,0:T(8,128)(2,1)}, bf16[4,256,256]{2,1,0:T(8,128)(2,1)}, u32[]{:S(2)}, u32[]{:S(2)}) collective-permute-start(bf16[4,256,256]{2,1,0:T(8,128)(2,1)} %get-tuple-element.22), channel_id=1, source_target_pairs={{0,64},{2,66},{4,68},{6,70},{8,72},{10,74},{12,76},{14,78},{16,80}... | collective-permute-start | bytes 1572872 | tf_op jit(solution)/shard_map/ppermute | solution.py:320
  128.9 1.4 reduce_sum.25
  130.3 0.8 broadcast_in_dim.22
  131.1 8.0 %all-to-all-start.3 = ((bf16[8,128,256]{2,1,0:T(8,128)(2,1)}), bf16[8,128,256]{2,1,0:T(8,128)(2,1)S(1)}, u32[]{:S(2)}, u32[]{:S(2)}) async-start(bf16[8,128,256]{2,1,0:T(8,128)(2,1)} %broadcast_in_dim.22), calls=%async_computation.3 | async-start | bytes 1048576 | tf_op jit(solution)/shard_map/all_to_all | solution.py:50
  139.1 1.5 fusion.10
  140.6 1.9 %collective-permute-start.17 = (bf16[256,256]{1,0:T(8,128)(2,1)S(1)}, bf16[256,256]{1,0:T(8,128)(2,1)S(1)}, u32[]{:S(2)}, u32[]{:S(2)}) collective-permute-start(bf16[256,256]{1,0:T(8,128)(2,1)S(1)} %get-tuple-element.27), channel_id=1, source_target_pairs={{0,192},{2,194},{4,196},{6,198},{8,200},{10,202},{12,204},{14,206}... | collective-permute-start | bytes 393224 | tf_op jit(solution)/shard_map/ppermute | solution.py:325
  142.5 0.2 collective-permute-start.19
  142.7 1.9 %collective-permute-start.18 = (bf16[256,256]{1,0:T(8,128)(2,1)S(1)}, bf16[256,256]{1,0:T(8,128)(2,1)S(1)}, u32[]{:S(2)}, u32[]{:S(2)}) collective-permute-start(bf16[256,256]{1,0:T(8,128)(2,1)S(1)} %get-tuple-element.29), channel_id=1, source_target_pairs={{0,128},{2,130},{4,132},{6,134},{8,136},{10,138},{12,140},{14,142}... | collective-permute-start | bytes 393224 | tf_op jit(solution)/shard_map/ppermute | solution.py:325
  144.7 0.8 copy-done.11
  145.5 1.6 fusion.13
  147.1 3.6 %collective-permute-start.23 = (bf16[256,256]{1,0:T(8,128)(2,1)S(1)}, bf16[256,256]{1,0:T(8,128)(2,1)S(1)}, u32[]{:S(2)}, u32[]{:S(2)}) collective-permute-start(bf16[256,256]{1,0:T(8,128)(2,1)S(1)} %get-tuple-element.30), channel_id=1, source_target_pairs={{0,6},{2,0},{4,2},{6,4},{8,14},{10,8},{12,10},{14,12},{16,22},{18,... | collective-permute-start | bytes 393224 | tf_op jit(solution)/shard_map/ppermute | solution.py:328
  150.7 1.6 collective-permute-start.24
  152.3 1.2 fusion.9
  153.4 4.9 %collective-permute-done.25 = bf16[256,256]{1,0:T(8,128)(2,1)S(1)} collective-permute-done((bf16[256,256]{1,0:T(8,128)(2,1)S(1)}, bf16[256,256]{1,0:T(8,128)(2,1)S(1)}, u32[]{:S(2)}, u32[]{:S(2)}) %collective-permute-start.25) | collective-permute-done | bytes 131104 | tf_op jit(solution)/shard_map/ppermute | solution.py:328
  158.3 1.2 fusion.6
  159.5 17.5 %all_to_all.25.home_ref = bf16[8,64,256]{2,1,0:T(8,128)(2,1)S(1)} all-to-all(bf16[8,64,256]{2,1,0:T(8,128)(2,1)S(1)} %bitcast.54), channel_id=1, replica_groups={{0,8,16,24,32,40,48,56},{2,10,18,26,34,42,50,58},{4,12,20,28,36,44,52,6..., dimensions={0} | all-to-all | bytes 524288 | tf_op jit(solution)/shard_map/all_to_all | solution.py:332
  177.0 2.0 %final.1 = (bf16[1024,256]{1,0:T(8,128)(2,1)}, f32[256,512]{1,0:T(8,128)}, f32[256,512]{1,0:T(8,128)}) custom-call(bf16[8,64,256]{2,1,0:T(8,128)(2,1)S(1)} %all_to_all.25.home_ref, f32[1024,256]{1,0:T(8,128)S(1)} %copy-done.1, bf16[128,8,256]{2,1,0:T(8,128)(2,1)S(1)} %bitcast.53), custom_call_target="tpu_custom_call" | custom-call | tf_op jit(solution)/shard_map/final/pallas_call | solution.py:340
  (74 shorter events, 0.6 us)
Async XLA Ops:
  0.6 29.6 %copy-start = (bf16[1024,256]{1,0:T(8,128)(2,1)S(1)}, bf16[1024,256]{1,0:T(8,128)(2,1)}, u32[]{:S(2)}) copy-start(bf16[1024,256]{1,0:T(8,128)(2,1)} %param.11) | copy-start | bytes 1572868
  0.6 14.8 %copy-start.15 = (s32[4096]{0:T(1024)S(1)}, s32[4096]{0:T(1024)}, u32[]{:S(2)}) copy-start(s32[4096]{0:T(1024)} %param.20) | copy-start | bytes 49156
  0.7 15.1 %copy-start.14 = (s32[8192]{0:T(1024)S(1)}, s32[8192]{0:T(1024)}, u32[]{:S(2)}) copy-start(s32[8192]{0:T(1024)} %param.18) | copy-start | bytes 98308
  0.7 15.1 %copy-start.13 = (s32[8192]{0:T(1024)S(1)}, s32[8192]{0:T(1024)}, u32[]{:S(2)}) copy-start(s32[8192]{0:T(1024)} %param.17) | copy-start | bytes 98308
  1.5 1.3 collective-permute-start.1
  4.7 20.7 %all-to-all-start = ((bf16[8,64,256]{2,1,0:T(8,128)(2,1)}), bf16[8,64,256]{2,1,0:T(8,128)(2,1)S(1)}, u32[]{:S(2)}, u32[]{:S(2)}) async-start(bf16[8,64,256]{2,1,0:T(8,128)(2,1)} %broadcast_in_dim.20), calls=%async_computation | async-start | bytes 524288 | tf_op jit(solution)/shard_map/all_to_all | solution.py:248
  14.5 15.6 %collective-permute-start = (bf16[1024,256]{1,0:T(8,128)(2,1)S(1)}, bf16[1024,256]{1,0:T(8,128)(2,1)S(1)}, u32[]{:S(2)}, u32[]{:S(2)}) collective-permute-start(bf16[1024,256]{1,0:T(8,128)(2,1)S(1)} %select_convert_fusion), channel_id=1, source_target_pairs={{0,1},{1,0},{2,3},{3,2},{4,5},{5,4},{6,7},{7,6},{8,9},{9,8},{10,11... | collective-permute-start | bytes 1572872 | tf_op jit(solution)/shard_map/ppermute | solution.py:239
  25.4 5.3 %copy-start.17 = (bf16[1024,256]{1,0:T(8,128)(2,1)S(1)}, bf16[1024,256]{1,0:T(8,128)(2,1)}, u32[]{:S(2)}) copy-start(bf16[1024,256]{1,0:T(8,128)(2,1)} %param.14) | copy-start | bytes 1572868
  25.4 10.9 %collective-permute-start.10 = (bf16[256,256]{1,0:T(8,128)(2,1)S(1)}, bf16[256,256]{1,0:T(8,128)(2,1)S(1)}, u32[]{:S(2)}, u32[]{:S(2)}) collective-permute-start(bf16[256,256]{1,0:T(8,128)(2,1)S(1)} %bitcast.59), channel_id=1, source_target_pairs={{0,6},{2,0},{4,2},{6,4},{8,14},{10,8},{12,10},{14,12},{16,22},{18,... | collective-permute-start | bytes 393224 | tf_op jit(solution)/shard_map/ppermute | solution.py:264
  28.5 7.8 %collective-permute-start.9 = (bf16[256,256]{1,0:T(8,128)(2,1)S(1)}, bf16[256,256]{1,0:T(8,128)(2,1)S(1)}, u32[]{:S(2)}, u32[]{:S(2)}) collective-permute-start(bf16[256,256]{1,0:T(8,128)(2,1)S(1)} %bitcast.60), channel_id=1, source_target_pairs={{0,4},{2,6},{4,0},{6,2},{8,12},{10,14},{12,8},{14,10},{16,20},{18,... | collective-permute-start | bytes 393224 | tf_op jit(solution)/shard_map/ppermute | solution.py:264
  29.1 7.7 %collective-permute-start.8 = (bf16[256,256]{1,0:T(8,128)(2,1)S(1)}, bf16[256,256]{1,0:T(8,128)(2,1)S(1)}, u32[]{:S(2)}, u32[]{:S(2)}) collective-permute-start(bf16[256,256]{1,0:T(8,128)(2,1)S(1)} %bitcast.61), channel_id=1, source_target_pairs={{0,2},{2,4},{4,6},{6,0},{8,10},{10,12},{12,14},{14,8},{16,18},{18,... | collective-permute-start | bytes 393224 | tf_op jit(solution)/shard_map/ppermute | solution.py:264
  30.2 1.0 copy-start.4
  30.2 1.0 copy-start.6
  31.2 11.4 %copy-start.16 = (s32[1024]{0:T(1024)S(1)}, s32[1024]{0:T(1024)}, u32[]{:S(2)}) copy-start(s32[1024]{0:T(1024)} %param.21) | copy-start | bytes 12292
  32.2 32.7 %all-to-all-start.1 = ((bf16[8,128,256]{2,1,0:T(8,128)(2,1)}), bf16[8,128,256]{2,1,0:T(8,128)(2,1)}, u32[]{:S(2)}, u32[]{:S(2)}) async-start(bf16[8,128,256]{2,1,0:T(8,128)(2,1)} %bitcast.22), calls=%async_computation.1 | async-start | bytes 1048576 | tf_op jit(solution)/shard_map/all_to_all | solution.py:50
  36.8 26.7 %copy-start.5 = (bf16[1024,256]{1,0:T(8,128)(2,1)S(1)}, bf16[1024,256]{1,0:T(8,128)(2,1)}, u32[]{:S(2)}) copy-start(bf16[1024,256]{1,0:T(8,128)(2,1)} %copy-done.4) | copy-start | bytes 1572868
  36.8 26.7 %copy-start.7 = (bf16[1024,256]{1,0:T(8,128)(2,1)S(1)}, bf16[1024,256]{1,0:T(8,128)(2,1)}, u32[]{:S(2)}) copy-start(bf16[1024,256]{1,0:T(8,128)(2,1)} %copy-done.6) | copy-start | bytes 1572868
  36.8 26.7 %copy-start.18 = (bf16[256,512]{1,0:T(8,128)(2,1)S(1)}, bf16[256,512]{1,0:T(8,128)(2,1)}, u32[]{:S(2)}) copy-start(bf16[256,512]{1,0:T(8,128)(2,1)} %param.16) | copy-start | bytes 786436
  36.9 25.8 %collective-permute-start.13 = (bf16[4,256,256]{2,1,0:T(8,128)(2,1)S(1)}, bf16[4,256,256]{2,1,0:T(8,128)(2,1)S(1)}, u32[]{:S(2)}, u32[]{:S(2)}) collective-permute-start(bf16[4,256,256]{2,1,0:T(8,128)(2,1)S(1)} %pad_maximum_fusion.2.rest_4_), channel_id=1, source_target_pairs={{0,192},{2,194},{4,196},{6,198},{8,200},{10,202},{12,204},{14,206}... | collective-permute-start | bytes 1572872 | tf_op jit(solution)/shard_map/ppermute | solution.py:269
  37.5 16.1 %collective-permute-start.4 = (bf16[256,256]{1,0:T(8,128)(2,1)S(1)}, bf16[256,256]{1,0:T(8,128)(2,1)S(1)}, u32[]{:S(2)}, u32[]{:S(2)}) collective-permute-start(bf16[256,256]{1,0:T(8,128)(2,1)S(1)} %bitcast.55), channel_id=1, source_target_pairs={{0,192},{2,194},{4,196},{6,198},{8,200},{10,202},{12,204},{14,206}... | collective-permute-start | bytes 393224 | tf_op jit(solution)/shard_map/ppermute | solution.py:263
  40.3 18.0 %collective-permute-start.3 = (bf16[256,256]{1,0:T(8,128)(2,1)S(1)}, bf16[256,256]{1,0:T(8,128)(2,1)S(1)}, u32[]{:S(2)}, u32[]{:S(2)}) collective-permute-start(bf16[256,256]{1,0:T(8,128)(2,1)S(1)} %bitcast.56), channel_id=1, source_target_pairs={{0,128},{2,130},{4,132},{6,134},{8,136},{10,138},{12,140},{14,142}... | collective-permute-start | bytes 393224 | tf_op jit(solution)/shard_map/ppermute | solution.py:263
  40.5 17.8 %collective-permute-start.2 = (bf16[256,256]{1,0:T(8,128)(2,1)S(1)}, bf16[256,256]{1,0:T(8,128)(2,1)S(1)}, u32[]{:S(2)}, u32[]{:S(2)}) collective-permute-start(bf16[256,256]{1,0:T(8,128)(2,1)S(1)} %bitcast.57), channel_id=1, source_target_pairs={{0,64},{2,66},{4,68},{6,70},{8,72},{10,74},{12,76},{14,78},{16,80}... | collective-permute-start | bytes 393224 | tf_op jit(solution)/shard_map/ppermute | solution.py:263
  46.1 41.4 %collective-permute-start.12 = (bf16[4,256,256]{2,1,0:T(8,128)(2,1)S(1)}, bf16[4,256,256]{2,1,0:T(8,128)(2,1)}, u32[]{:S(2)}, u32[]{:S(2)}) collective-permute-start(bf16[4,256,256]{2,1,0:T(8,128)(2,1)S(1)} %pad_maximum_fusion.2.rest_4_), channel_id=1, source_target_pairs={{0,128},{2,130},{4,132},{6,134},{8,136},{10,138},{12,140},{14,142}... | collective-permute-start | bytes 1572872 | tf_op jit(solution)/shard_map/ppermute | solution.py:269
  53.7 33.8 %collective-permute-start.11 = (bf16[4,256,256]{2,1,0:T(8,128)(2,1)S(1)}, bf16[4,256,256]{2,1,0:T(8,128)(2,1)}, u32[]{:S(2)}, u32[]{:S(2)}) collective-permute-start(bf16[4,256,256]{2,1,0:T(8,128)(2,1)S(1)} %pad_maximum_fusion.2.rest_4_), channel_id=1, source_target_pairs={{0,64},{2,66},{4,68},{6,70},{8,72},{10,74},{12,76},{14,78},{16,80}... | collective-permute-start | bytes 1572872 | tf_op jit(solution)/shard_map/ppermute | solution.py:269
  59.2 28.3 %collective-permute-start.7 = (bf16[4,256,256]{2,1,0:T(8,128)(2,1)}, bf16[4,256,256]{2,1,0:T(8,128)(2,1)}, u32[]{:S(2)}, u32[]{:S(2)}) collective-permute-start(bf16[4,256,256]{2,1,0:T(8,128)(2,1)} %pad_maximum_fusion.1.rest_0_), channel_id=1, source_target_pairs={{0,6},{2,0},{4,2},{6,4},{8,14},{10,8},{12,10},{14,12},{16,22},{18,... | collective-permute-start | bytes 1572872 | tf_op jit(solution)/shard_map/ppermute | solution.py:268
  61.0 26.5 %collective-permute-start.6 = (bf16[4,256,256]{2,1,0:T(8,128)(2,1)}, bf16[4,256,256]{2,1,0:T(8,128)(2,1)}, u32[]{:S(2)}, u32[]{:S(2)}) collective-permute-start(bf16[4,256,256]{2,1,0:T(8,128)(2,1)} %pad_maximum_fusion.1.rest_0_), channel_id=1, source_target_pairs={{0,4},{2,6},{4,0},{6,2},{8,12},{10,14},{12,8},{14,10},{16,20},{18,... | collective-permute-start | bytes 1572872 | tf_op jit(solution)/shard_map/ppermute | solution.py:268
  62.7 0.8 copy-start.2
  63.5 24.1 %collective-permute-start.5 = (bf16[4,256,256]{2,1,0:T(8,128)(2,1)}, bf16[4,256,256]{2,1,0:T(8,128)(2,1)}, u32[]{:S(2)}, u32[]{:S(2)}) collective-permute-start(bf16[4,256,256]{2,1,0:T(8,128)(2,1)} %pad_maximum_fusion.1.rest_0_), channel_id=1, source_target_pairs={{0,2},{2,4},{4,6},{6,0},{8,10},{10,12},{12,14},{14,8},{16,18},{18,... | collective-permute-start | bytes 1572872 | tf_op jit(solution)/shard_map/ppermute | solution.py:268
  67.0 61.9 %all-to-all-start.2 = ((bf16[16,128,256]{2,1,0:T(8,128)(2,1)}), bf16[16,128,256]{2,1,0:T(8,128)(2,1)}, u32[]{:S(2)}, u32[]{:S(2)}) async-start(bf16[16,128,256]{2,1,0:T(8,128)(2,1)} %broadcast_in_dim.21), calls=%async_computation.2 | async-start | bytes 2097152 | tf_op jit(solution)/shard_map/all_to_all | solution.py:50
  84.7 2.9 %copy-start.3 = (bf16[4,256,256]{2,1,0:T(8,128)(2,1)S(1)}, bf16[4,256,256]{2,1,0:T(8,128)(2,1)}, u32[]{:S(2)}) copy-start(bf16[4,256,256]{2,1,0:T(8,128)(2,1)} %copy-done.2) | copy-start | bytes 1572868
  109.8 29.3 %copy-start.9 = (bf16[4,256,256]{2,1,0:T(8,128)(2,1)S(1)}, bf16[4,256,256]{2,1,0:T(8,128)(2,1)}, u32[]{:S(2)}) copy-start(bf16[4,256,256]{2,1,0:T(8,128)(2,1)} %get-tuple-element.15) | copy-start | bytes 1572868
  109.8 15.1 %collective-permute-start.14 = (bf16[4,256,256]{2,1,0:T(8,128)(2,1)}, bf16[4,256,256]{2,1,0:T(8,128)(2,1)S(1)}, u32[]{:S(2)}, u32[]{:S(2)}) collective-permute-start(bf16[4,256,256]{2,1,0:T(8,128)(2,1)} %get-tuple-element.16), channel_id=1, source_target_pairs={{0,6},{2,0},{4,2},{6,4},{8,14},{10,8},{12,10},{14,12},{16,22},{18,... | collective-permute-start | bytes 1572872 | tf_op jit(solution)/shard_map/ppermute | solution.py:319
  112.3 26.8 %collective-permute-start.15 = (bf16[4,256,256]{2,1,0:T(8,128)(2,1)}, bf16[4,256,256]{2,1,0:T(8,128)(2,1)}, u32[]{:S(2)}, u32[]{:S(2)}) collective-permute-start(bf16[4,256,256]{2,1,0:T(8,128)(2,1)} %get-tuple-element.17), channel_id=1, source_target_pairs={{0,4},{2,6},{4,0},{6,2},{8,12},{10,14},{12,8},{14,10},{16,20},{18,... | collective-permute-start | bytes 1572872 | tf_op jit(solution)/shard_map/ppermute | solution.py:319
  113.9 25.2 %collective-permute-start.16 = (bf16[4,256,256]{2,1,0:T(8,128)(2,1)}, bf16[4,256,256]{2,1,0:T(8,128)(2,1)}, u32[]{:S(2)}, u32[]{:S(2)}) collective-permute-start(bf16[4,256,256]{2,1,0:T(8,128)(2,1)} %get-tuple-element.18), channel_id=1, source_target_pairs={{0,2},{2,4},{4,6},{6,0},{8,10},{10,12},{12,14},{14,8},{16,18},{18,... | collective-permute-start | bytes 1572872 | tf_op jit(solution)/shard_map/ppermute | solution.py:319
  114.5 28.2 %collective-permute-start.20 = (bf16[4,256,256]{2,1,0:T(8,128)(2,1)}, bf16[4,256,256]{2,1,0:T(8,128)(2,1)S(1)}, u32[]{:S(2)}, u32[]{:S(2)}) collective-permute-start(bf16[4,256,256]{2,1,0:T(8,128)(2,1)} %get-tuple-element.20), channel_id=1, source_target_pairs={{0,192},{2,194},{4,196},{6,198},{8,200},{10,202},{12,204},{14,206}... | collective-permute-start | bytes 1572872 | tf_op jit(solution)/shard_map/ppermute | solution.py:320
  116.1 28.6 %collective-permute-start.21 = (bf16[4,256,256]{2,1,0:T(8,128)(2,1)}, bf16[4,256,256]{2,1,0:T(8,128)(2,1)S(1)}, u32[]{:S(2)}, u32[]{:S(2)}) collective-permute-start(bf16[4,256,256]{2,1,0:T(8,128)(2,1)} %get-tuple-element.21), channel_id=1, source_target_pairs={{0,128},{2,130},{4,132},{6,134},{8,136},{10,138},{12,140},{14,142}... | collective-permute-start | bytes 1572872 | tf_op jit(solution)/shard_map/ppermute | solution.py:320
  124.9 6.2 %copy-start.12 = (bf16[4,256,256]{2,1,0:T(8,128)(2,1)}, bf16[4,256,256]{2,1,0:T(8,128)(2,1)S(1)}, u32[]{:S(2)}) copy-start(bf16[4,256,256]{2,1,0:T(8,128)(2,1)S(1)} %collective-permute-done.14) | copy-start | bytes 1572868
  124.9 20.6 %copy-start.8 = (bf16[4,256,256]{2,1,0:T(8,128)(2,1)S(1)}, bf16[4,256,256]{2,1,0:T(8,128)(2,1)}, u32[]{:S(2)}) copy-start(bf16[4,256,256]{2,1,0:T(8,128)(2,1)} %get-tuple-element.19) | copy-start | bytes 1572868
  124.9 19.8 %collective-permute-start.22 = (bf16[4,256,256]{2,1,0:T(8,128)(2,1)}, bf16[4,256,256]{2,1,0:T(8,128)(2,1)}, u32[]{:S(2)}, u32[]{:S(2)}) collective-permute-start(bf16[4,256,256]{2,1,0:T(8,128)(2,1)} %get-tuple-element.22), channel_id=1, source_target_pairs={{0,64},{2,66},{4,68},{6,70},{8,72},{10,74},{12,76},{14,78},{16,80}... | collective-permute-start | bytes 1572872 | tf_op jit(solution)/shard_map/ppermute | solution.py:320
  131.1 28.4 %all-to-all-start.3 = ((bf16[8,128,256]{2,1,0:T(8,128)(2,1)}), bf16[8,128,256]{2,1,0:T(8,128)(2,1)S(1)}, u32[]{:S(2)}, u32[]{:S(2)}) async-start(bf16[8,128,256]{2,1,0:T(8,128)(2,1)} %broadcast_in_dim.22), calls=%async_computation.3 | async-start | bytes 1048576 | tf_op jit(solution)/shard_map/all_to_all | solution.py:50
  140.6 10.1 %collective-permute-start.17 = (bf16[256,256]{1,0:T(8,128)(2,1)S(1)}, bf16[256,256]{1,0:T(8,128)(2,1)S(1)}, u32[]{:S(2)}, u32[]{:S(2)}) collective-permute-start(bf16[256,256]{1,0:T(8,128)(2,1)S(1)} %get-tuple-element.27), channel_id=1, source_target_pairs={{0,192},{2,194},{4,196},{6,198},{8,200},{10,202},{12,204},{14,206}... | collective-permute-start | bytes 393224 | tf_op jit(solution)/shard_map/ppermute | solution.py:325
  142.5 9.8 %collective-permute-start.19 = (bf16[256,256]{1,0:T(8,128)(2,1)S(1)}, bf16[256,256]{1,0:T(8,128)(2,1)S(1)}, u32[]{:S(2)}, u32[]{:S(2)}) collective-permute-start(bf16[256,256]{1,0:T(8,128)(2,1)S(1)} %get-tuple-element.28), channel_id=1, source_target_pairs={{0,64},{2,66},{4,68},{6,70},{8,72},{10,74},{12,76},{14,78},{16,80}... | collective-permute-start | bytes 393224 | tf_op jit(solution)/shard_map/ppermute | solution.py:325
  142.7 2.0 %copy-start.10 = (bf16[4,256,256]{2,1,0:T(8,128)(2,1)}, bf16[4,256,256]{2,1,0:T(8,128)(2,1)S(1)}, u32[]{:S(2)}) copy-start(bf16[4,256,256]{2,1,0:T(8,128)(2,1)S(1)} %collective-permute-done.20) | copy-start | bytes 1572868
  142.7 9.5 %collective-permute-start.18 = (bf16[256,256]{1,0:T(8,128)(2,1)S(1)}, bf16[256,256]{1,0:T(8,128)(2,1)S(1)}, u32[]{:S(2)}, u32[]{:S(2)}) collective-permute-start(bf16[256,256]{1,0:T(8,128)(2,1)S(1)} %get-tuple-element.29), channel_id=1, source_target_pairs={{0,128},{2,130},{4,132},{6,134},{8,136},{10,138},{12,140},{14,142}... | collective-permute-start | bytes 393224 | tf_op jit(solution)/shard_map/ppermute | solution.py:325
  144.7 0.8 copy-start.11
  145.5 31.5 %copy-start.1 = (f32[1024,256]{1,0:T(8,128)S(1)}, f32[1024,256]{1,0:T(8,128)}, u32[]{:S(2)}) copy-start(f32[1024,256]{1,0:T(8,128)} %get-tuple-element.25.pre_ref) | copy-start | bytes 3145732
  147.1 6.4 %collective-permute-start.23 = (bf16[256,256]{1,0:T(8,128)(2,1)S(1)}, bf16[256,256]{1,0:T(8,128)(2,1)S(1)}, u32[]{:S(2)}, u32[]{:S(2)}) collective-permute-start(bf16[256,256]{1,0:T(8,128)(2,1)S(1)} %get-tuple-element.30), channel_id=1, source_target_pairs={{0,6},{2,0},{4,2},{6,4},{8,14},{10,8},{12,10},{14,12},{16,22},{18,... | collective-permute-start | bytes 393224 | tf_op jit(solution)/shard_map/ppermute | solution.py:328
  150.7 7.6 %collective-permute-start.25 = (bf16[256,256]{1,0:T(8,128)(2,1)S(1)}, bf16[256,256]{1,0:T(8,128)(2,1)S(1)}, u32[]{:S(2)}, u32[]{:S(2)}) collective-permute-start(bf16[256,256]{1,0:T(8,128)(2,1)S(1)} %get-tuple-element.31), channel_id=1, source_target_pairs={{0,2},{2,4},{4,6},{6,0},{8,10},{10,12},{12,14},{14,8},{16,18},{18,... | collective-permute-start | bytes 393224 | tf_op jit(solution)/shard_map/ppermute | solution.py:328
  150.7 7.6 %collective-permute-start.24 = (bf16[256,256]{1,0:T(8,128)(2,1)S(1)}, bf16[256,256]{1,0:T(8,128)(2,1)S(1)}, u32[]{:S(2)}, u32[]{:S(2)}) collective-permute-start(bf16[256,256]{1,0:T(8,128)(2,1)S(1)} %get-tuple-element.32), channel_id=1, source_target_pairs={{0,4},{2,6},{4,0},{6,2},{8,12},{10,14},{12,8},{14,10},{16,20},{18,... | collective-permute-start | bytes 393224 | tf_op jit(solution)/shard_map/ppermute | solution.py:328
